TPU v7x, 32 devices: a whole 2x2x4 slice. The times are simulated.
32 devices in a mesh: groups: 2 (over x), img: 8 (over z, y), space: 2 (over core).
Axes of the slice: x: 2, y: 2, z: 4, core: 2. Of those that a mesh axis runs over, the one named last changes fastest.
Arguments:
- path: float32 [64, 64, 4096], P(('groups', 'img'), 'space'), parts along dimension 0, may hold values from -3 to 3
- bracket: int32 [64], P(('groups', 'img')), parts along dimension 0, may hold values from 0 to 30, as said below
Outputs:
- new_path: float32 [64, 64, 4096], P(('groups', 'img'), 'space'), parts along dimension 0
There are 2 independent parts, one for each index of `groups`. A program takes and returns all parts, laid end to end along the dimension named above; each array names one. Nothing has to cross between parts.
Inputs may be any that keep to these rules, and one draw needn't show every extreme that they name: bracket[j] differs from j by at most 2; it is given, not derived from the arc lengths, so the target arc length of image j need not lie between arc_b and arc_(b+1).
All inputs are finite; a program needn't handle non-finite values.
Results may differ from a plain program's by a relative error of at most 0.0003.
Values sent between devices are 32-bit elements; how exact they have to be, the bound alone decides.
No kernel may reach another device: no remote copies, remote signals or barrier semaphores. Data moves between devices by JAX's collectives and lax.ppermute only.
A program may use at most 64 MiB of HBM per device.

v0:
```python
import jax
import jax.numpy as jnp
from jax import lax
from jax.sharding import PartitionSpec as P

REACH = 2
ITERS = 2


TIME_STEP = 0.002
EPSILON = 1e-06


def with_halo(block, sides, width, periodic):
    for axis, dim in sides:
        count = lax.axis_size(axis)
        forward = [(i, i + 1) for i in range(count - 1)]
        if periodic:
            forward.append((count - 1, 0))
        backward = [(target, source) for source, target in forward]
        low = lax.ppermute(
            lax.slice_in_dim(block, block.shape[dim] - width, None, axis=dim), axis, forward
        )
        high = lax.ppermute(lax.slice_in_dim(block, 0, width, axis=dim), axis, backward)
        block = jnp.concatenate([low, block, high], axis=dim)
    return block


def laplace(field):
    padded = with_halo(field, (("space", 1),), 1, True)
    return (
        padded[:, 2:]
        + padded[:, :-2]
        + jnp.roll(field, 1, -1)
        + jnp.roll(field, -1, -1)
        - 4.0 * field
    )


def tangent_of(window, global_ids, count):
    center = window[1:-1]
    is_first = (global_ids == 0)[:, None, None]
    is_last = (global_ids == count - 1)[:, None, None]
    earlier = jnp.where(is_first, center, window[:-2])
    following = jnp.where(is_last, center, window[2:])
    stretch = jnp.where(is_first | is_last, jnp.float32(count - 1), jnp.float32((count - 1) / 2.0))
    return (following - earlier) * stretch


def theta_of(window, global_ids, count):
    center = window[1:-1]
    tangent = tangent_of(window, global_ids, count)
    drift_v = laplace(center) + center - center**3
    norm_sums = lax.psum(
        (jnp.sum(drift_v * drift_v, axis=(1, 2)), jnp.sum(tangent * tangent, axis=(1, 2))), "space"
    )
    speed = jnp.sqrt(norm_sums[0] + EPSILON) / jnp.sqrt(norm_sums[1] + EPSILON)
    return (speed[:, None, None] * tangent - drift_v, speed)


def per_device(path, bracket):
    local_count = path.shape[0]
    count = local_count * lax.axis_size("img")
    start = lax.axis_index("img") * local_count
    own_ids = start + jnp.arange(local_count)
    images = path
    for iteration in range(ITERS):
        window = with_halo(images, (("img", 0),), 1, False)
        theta, speed = theta_of(window, own_ids, count)
        theta_window = with_halo(theta, (("img", 0),), 1, False)
        descent = (
            speed[:, None, None] * tangent_of(theta_window, own_ids, count)
            + laplace(theta)
            + (1.0 - 3.0 * images * images) * theta
        )
        inside = ((own_ids > 0) & (own_ids < count - 1))[:, None, None]
        images = images + TIME_STEP * jnp.where(inside, descent, 0.0)
    margin = REACH + 1
    window = with_halo(images, (("img", 0),), margin, False)
    window_ids = start - margin + jnp.arange(local_count + 2 * margin)
    diffs = window[1:] - window[:-1]
    squares = lax.psum(jnp.sum(diffs * diffs, axis=(1, 2)), "space")
    counted = (window_ids[1:] >= 1) & (window_ids[1:] <= count - 1)
    segments = jnp.where(counted, jnp.sqrt(squares + EPSILON), 0.0)
    seg_full = jnp.concatenate([jnp.zeros((1,), segments.dtype), segments])
    running = jnp.cumsum(seg_full)
    own_length = running[margin + local_count - 1] - running[margin - 1]
    shares = lax.all_gather(own_length[None], "img", axis=0, tiled=True)
    device_ids = jnp.arange(shares.shape[0])
    offset = jnp.sum(jnp.where(device_ids < lax.axis_index("img"), shares, 0.0))
    length = jnp.sum(shares)
    arc_window = offset + running - running[margin - 1]
    target = length * own_ids.astype(segments.dtype) / (count - 1)
    local_pick = bracket - (start - margin)
    weight = (target - jnp.take(arc_window, local_pick)) / jnp.take(seg_full, local_pick + 1)
    base = jnp.take(window, local_pick, axis=0)
    upper = jnp.take(window, local_pick + 1, axis=0)
    return base + weight[:, None, None] * (upper - base)


def solution(mesh):
    return jax.shard_map(
        per_device,
        mesh=mesh,
        in_specs=(P(("groups", "img"), "space", None), P(("groups", "img"))),
        out_specs=P(("groups", "img"), "space", None),
        check_vma=False,
    )
```

profile of v0, /device:TPU:0, one launch (start us, length us, event | category | flops | bytes accessed | tf_op | source)
XLA Modules:
  0.0 261.5 jit_solution(10743141789068860042)
XLA Ops:
  0.0 2.4 fusion.78
  3.7 5.6 %collective-permute-start.3 = (f32[1,32,4096]{2,1,0:T(8,128)}, f32[1,32,4096]{2,1,0:T(8,128)S(1)}, u32[]{:S(2)}, u32[]{:S(2)}) collective-permute-start(f32[1,32,4096]{2,1,0:T(8,128)} %get-tuple-element.56), channel_id=1, source_target_pairs={{0,2},{2,4},{4,6},{6,8},{8,10},{10,12},{12,14},{1,3},{3,5},{5,7},{... | collective-permute-start | bytes 1572872 | tf_op jit(solution)/shard_map/ppermute | solution.py:21
  9.9 2.8 %fusion.81 = (f32[4,32,4095]{2,1,0:T(8,128)}, f32[4,32,4095]{2,1,0:T(8,128)}) fusion(f32[4,32,4096]{2,1,0:T(8,128)S(1)} %copy-done.1), kind=kLoop, calls=%fused_computation.128 | loop fusion | bytes 8386560 | tf_op jit(solution)/shard_map/jit(_roll_static)/slice | solution.py:34
  12.8 6.6 %collective-permute-done.2 = f32[1,32,4096]{2,1,0:T(8,128)S(1)} collective-permute-done((f32[1,32,4096]{2,1,0:T(8,128)}, f32[1,32,4096]{2,1,0:T(8,128)S(1)}, u32[]{:S(2)}, u32[]{:S(2)}) %collective-permute-start.2) | collective-permute-done | bytes 524320 | tf_op jit(solution)/shard_map/ppermute | solution.py:24
  19.4 11.5 %collective-permute-done.3 = f32[1,32,4096]{2,1,0:T(8,128)S(1)} collective-permute-done((f32[1,32,4096]{2,1,0:T(8,128)}, f32[1,32,4096]{2,1,0:T(8,128)S(1)}, u32[]{:S(2)}, u32[]{:S(2)}) %collective-permute-start.3) | collective-permute-done | bytes 524320 | tf_op jit(solution)/shard_map/ppermute | solution.py:21
  30.9 5.5 %multiply_reduce_fusion.2 = (f32[4]{0:T(128)S(1)}, f32[4,32,4096]{2,1,0:T(8,128)}, f32[4]{0:T(128)S(1)}, f32[4,32,4096]{2,1,0:T(8,128)}) fusion(f32[4]{0:T(128)S(1)} %or_select_fusion, f32[4,32,4096]{2,1,0:T(8,128)S(1)} %copy-done.1, f32[1,32,4096]{2,1,0:T(8,128)S(1)} %collective-permute-done.3, pred[4]{0:T(512)(128)(4,1)S(1)} %get-tuple-element.69, ...), kind=kLoop, calls=%fused_computation.87 | loop fusion | flops 12058616 | bytes 11665464 | tf_op jit(solution)/shard_map/reduce_sum | solution.py:55
  36.4 2.4 all-reduce.2
  38.9 2.5 multiply_subtract_fusion.1
  43.7 4.9 %collective-permute-start.5 = (f32[1,32,4096]{2,1,0:T(8,128)S(1)}, f32[1,32,4096]{2,1,0:T(8,128)S(1)}, u32[]{:S(2)}, u32[]{:S(2)}) collective-permute-start(f32[1,32,4096]{2,1,0:T(8,128)S(1)} %get-tuple-element.50), channel_id=1, source_target_pairs={{0,2},{2,4},{4,6},{6,8},{8,10},{10,12},{12,14},{1,3},{3,5},{5,7},{... | collective-permute-start | bytes 1572872 | tf_op jit(solution)/shard_map/ppermute | solution.py:21
  50.2 8.7 %collective-permute-done.4 = f32[1,32,4096]{2,1,0:T(8,128)S(1)} collective-permute-done((f32[1,32,4096]{2,1,0:T(8,128)S(1)}, f32[1,32,4096]{2,1,0:T(8,128)S(1)}, u32[]{:S(2)}, u32[]{:S(2)}) %collective-permute-start.4) | collective-permute-done | bytes 524320 | tf_op jit(solution)/shard_map/ppermute | solution.py:24
  58.9 11.4 %collective-permute-done.5 = f32[1,32,4096]{2,1,0:T(8,128)S(1)} collective-permute-done((f32[1,32,4096]{2,1,0:T(8,128)S(1)}, f32[1,32,4096]{2,1,0:T(8,128)S(1)}, u32[]{:S(2)}, u32[]{:S(2)}) %collective-permute-start.5) | collective-permute-done | bytes 524320 | tf_op jit(solution)/shard_map/ppermute | solution.py:21
  70.3 2.5 fusion.8
  74.9 5.0 %collective-permute-start.11 = (f32[1,32,4096]{2,1,0:T(8,128)S(1)}, f32[1,32,4096]{2,1,0:T(8,128)S(1)}, u32[]{:S(2)}, u32[]{:S(2)}) collective-permute-start(f32[1,32,4096]{2,1,0:T(8,128)S(1)} %get-tuple-element.38), channel_id=1, source_target_pairs={{0,2},{2,4},{4,6},{6,8},{8,10},{10,12},{12,14},{1,3},{3,5},{5,7},{... | collective-permute-start | bytes 1572872 | tf_op jit(solution)/shard_map/ppermute | solution.py:21
  81.5 8.6 %collective-permute-done.10 = f32[1,32,4096]{2,1,0:T(8,128)S(1)} collective-permute-done((f32[1,32,4096]{2,1,0:T(8,128)S(1)}, f32[1,32,4096]{2,1,0:T(8,128)S(1)}, u32[]{:S(2)}, u32[]{:S(2)}) %collective-permute-start.10) | collective-permute-done | bytes 524320 | tf_op jit(solution)/shard_map/ppermute | solution.py:24
  90.1 11.4 %collective-permute-done.11 = f32[1,32,4096]{2,1,0:T(8,128)S(1)} collective-permute-done((f32[1,32,4096]{2,1,0:T(8,128)S(1)}, f32[1,32,4096]{2,1,0:T(8,128)S(1)}, u32[]{:S(2)}, u32[]{:S(2)}) %collective-permute-start.11) | collective-permute-done | bytes 524320 | tf_op jit(solution)/shard_map/ppermute | solution.py:21
  101.5 4.1 %multiply_reduce_fusion = (f32[4]{0:T(128)S(1)}, f32[4,32,4096]{2,1,0:T(8,128)}, f32[4]{0:T(128)S(1)}, f32[4,32,4096]{2,1,0:T(8,128)}) fusion(f32[4]{0:T(128)S(1)} %or_select_fusion, f32[4,32,4096]{2,1,0:T(8,128)S(1)} %fusion.8, f32[1,32,4096]{2,1,0:T(8,128)S(1)} %collective-permute-done.11, pred[4]{0:T(512)(128)(4,1)S(1)} %get-tuple-element.69, ...), kind=kLoop, calls=%fused_computation.84 | loop fusion | flops 12058616 | bytes 11665464 | tf_op jit(solution)/shard_map/reduce_sum | solution.py:55
  105.5 2.4 all-reduce.1
  108.0 2.5 multiply_subtract_fusion
  112.6 5.0 %collective-permute-start.13 = (f32[1,32,4096]{2,1,0:T(8,128)S(1)}, f32[1,32,4096]{2,1,0:T(8,128)S(1)}, u32[]{:S(2)}, u32[]{:S(2)}) collective-permute-start(f32[1,32,4096]{2,1,0:T(8,128)S(1)} %get-tuple-element.32), channel_id=1, source_target_pairs={{0,2},{2,4},{4,6},{6,8},{8,10},{10,12},{12,14},{1,3},{3,5},{5,7},{... | collective-permute-start | bytes 1572872 | tf_op jit(solution)/shard_map/ppermute | solution.py:21
  119.3 8.7 %collective-permute-done.12 = f32[1,32,4096]{2,1,0:T(8,128)S(1)} collective-permute-done((f32[1,32,4096]{2,1,0:T(8,128)S(1)}, f32[1,32,4096]{2,1,0:T(8,128)S(1)}, u32[]{:S(2)}, u32[]{:S(2)}) %collective-permute-start.12) | collective-permute-done | bytes 524320 | tf_op jit(solution)/shard_map/ppermute | solution.py:24
  128.0 11.4 %collective-permute-done.13 = f32[1,32,4096]{2,1,0:T(8,128)S(1)} collective-permute-done((f32[1,32,4096]{2,1,0:T(8,128)S(1)}, f32[1,32,4096]{2,1,0:T(8,128)S(1)}, u32[]{:S(2)}, u32[]{:S(2)}) %collective-permute-start.13) | collective-permute-done | bytes 524320 | tf_op jit(solution)/shard_map/ppermute | solution.py:21
  139.4 2.5 fusion.15
  141.9 2.3 fusion.65
  144.3 4.5 %collective-permute-start.16 = (f32[3,32,4096]{2,1,0:T(8,128)}, f32[3,32,4096]{2,1,0:T(8,128)S(1)}, u32[]{:S(2)}, u32[]{:S(2)}) collective-permute-start(f32[3,32,4096]{2,1,0:T(8,128)} %get-tuple-element.25), channel_id=1, source_target_pairs={{0,2},{2,4},{4,6},{6,8},{8,10},{10,12},{12,14},{1,3},{3,5},{5,7},{... | collective-permute-start | bytes 4718600 | tf_op jit(solution)/shard_map/ppermute | solution.py:21
  150.1 66.4 %collective-permute-done.16 = f32[3,32,4096]{2,1,0:T(8,128)S(1)} collective-permute-done((f32[3,32,4096]{2,1,0:T(8,128)}, f32[3,32,4096]{2,1,0:T(8,128)S(1)}, u32[]{:S(2)}, u32[]{:S(2)}) %collective-permute-start.16) | collective-permute-done | bytes 1572896 | tf_op jit(solution)/shard_map/ppermute | solution.py:21
  216.5 2.1 pad_maximum_fusion
  219.2 1.6 copy-done
  221.5 2.4 psum.39
  226.9 19.7 %all-reduce = f32[8]{0:T(128)S(1)} all-reduce(f32[8]{0:T(128)S(1)} %dynamic-update-slice), channel_id=1, replica_groups=mesh['groups'=2,'img'=8,'space'=2] {'img'}, use_global_device_ids=true, to_apply=%add | all-reduce | flops 8 | bytes 64
  248.5 3.2 %gather_fusion = f32[4,32,4096]{2,1,0:T(8,128)S(1)} fusion(f32[10,32,4096]{2,1,0:T(8,128)} %copy-done, s32[1024]{0:T(1024)S(1)} %get-tuple-element.72), kind=kCustom, calls=%fused_computation.clone | custom fusion | bytes 4194320 | tf_op jit(solution)/shard_map/jit(_take)/gather | solution.py:96
  252.3 4.5 %gather_fusion.3 = f32[4,32,4096]{2,1,0:T(8,128)} fusion(f32[10,32,4096]{2,1,0:T(8,128)} %copy-done, s32[1024]{0:T(1024)S(1)} %get-tuple-element.71), kind=kCustom, calls=%fused_computation.2.clone | custom fusion | bytes 4194320 | tf_op jit(solution)/shard_map/jit(_take)/gather | solution.py:97
  258.1 3.3 %fusion.55 = f32[4,32,4096]{2,1,0:T(8,128)} fusion(f32[4,32,4096]{2,1,0:T(8,128)} %gather_fusion.3, f32[4,32,4096]{2,1,0:T(8,128)S(1)} %gather_fusion, f32[4]{0:T(128)S(1)} %select_divide_fusion, pred[4]{0:T(512)(128)(4,1)S(1)} %get-tuple-element.67, pred[4]{0:T(512)(128)(4,1)S(1)} %get-tuple-element.13), kind=kLoop, calls=%fused_computation.82 | loop fusion | flops 2621440 | bytes 6291480 | tf_op jit(solution)/shard_map/add | solution.py:98
  (68 shorter events, 21.3 us)
Async XLA Ops:
  0.0 9.3 %copy-start.1 = (f32[4,32,4096]{2,1,0:T(8,128)S(1)}, f32[4,32,4096]{2,1,0:T(8,128)}, u32[]{:S(2)}) copy-start(f32[4,32,4096]{2,1,0:T(8,128)} %param.6) | copy-start | bytes 6291460
  2.4 17.0 %collective-permute-start.2 = (f32[1,32,4096]{2,1,0:T(8,128)}, f32[1,32,4096]{2,1,0:T(8,128)S(1)}, u32[]{:S(2)}, u32[]{:S(2)}) collective-permute-start(f32[1,32,4096]{2,1,0:T(8,128)} %get-tuple-element.55), channel_id=1, source_target_pairs={{2,0},{4,2},{6,4},{8,6},{10,8},{12,10},{14,12},{3,1},{5,3},{7,5},{... | collective-permute-start | bytes 1572872 | tf_op jit(solution)/shard_map/ppermute | solution.py:24
  3.7 27.2 %collective-permute-start.3 = (f32[1,32,4096]{2,1,0:T(8,128)}, f32[1,32,4096]{2,1,0:T(8,128)S(1)}, u32[]{:S(2)}, u32[]{:S(2)}) collective-permute-start(f32[1,32,4096]{2,1,0:T(8,128)} %get-tuple-element.56), channel_id=1, source_target_pairs={{0,2},{2,4},{4,6},{6,8},{8,10},{10,12},{12,14},{1,3},{3,5},{5,7},{... | collective-permute-start | bytes 1572872 | tf_op jit(solution)/shard_map/ppermute | solution.py:21
  9.4 3.5 %collective-permute-start = (f32[4,1,4096]{2,1,0:T(1,128)S(1)}, f32[4,1,4096]{2,1,0:T(1,128)S(1)}, u32[]{:S(2)}, u32[]{:S(2)}) collective-permute-start(f32[4,1,4096]{2,1,0:T(1,128)S(1)} %get-tuple-element.57), channel_id=1, source_target_pairs={{1,0},{0,1},{3,2},{2,3},{5,4},{4,5},{7,6},{6,7},{9,8},{8,9},{11,10... | collective-permute-start | bytes 196616 | tf_op jit(solution)/shard_map/ppermute | solution.py:24
  9.4 3.4 %collective-permute-start.1 = (f32[4,1,4096]{2,1,0:T(1,128)S(1)}, f32[4,1,4096]{2,1,0:T(1,128)S(1)}, u32[]{:S(2)}, u32[]{:S(2)}) collective-permute-start(f32[4,1,4096]{2,1,0:T(1,128)S(1)} %get-tuple-element.58), channel_id=1, source_target_pairs={{0,1},{1,0},{2,3},{3,2},{4,5},{5,4},{6,7},{7,6},{8,9},{9,8},{10,11... | collective-permute-start | bytes 196616 | tf_op jit(solution)/shard_map/ppermute | solution.py:21
  42.1 28.2 %copy-start.2 = (f32[4,32,4096]{2,1,0:T(8,128)S(1)}, f32[4,32,4096]{2,1,0:T(8,128)}, u32[]{:S(2)}) copy-start(f32[4,32,4096]{2,1,0:T(8,128)} %param.6) | copy-start | bytes 6291460
  42.2 16.7 %collective-permute-start.4 = (f32[1,32,4096]{2,1,0:T(8,128)S(1)}, f32[1,32,4096]{2,1,0:T(8,128)S(1)}, u32[]{:S(2)}, u32[]{:S(2)}) collective-permute-start(f32[1,32,4096]{2,1,0:T(8,128)S(1)} %get-tuple-element.49), channel_id=1, source_target_pairs={{2,0},{4,2},{6,4},{8,6},{10,8},{12,10},{14,12},{3,1},{5,3},{7,5},{... | collective-permute-start | bytes 1572872 | tf_op jit(solution)/shard_map/ppermute | solution.py:24
  43.7 26.6 %collective-permute-start.5 = (f32[1,32,4096]{2,1,0:T(8,128)S(1)}, f32[1,32,4096]{2,1,0:T(8,128)S(1)}, u32[]{:S(2)}, u32[]{:S(2)}) collective-permute-start(f32[1,32,4096]{2,1,0:T(8,128)S(1)} %get-tuple-element.50), channel_id=1, source_target_pairs={{0,2},{2,4},{4,6},{6,8},{8,10},{10,12},{12,14},{1,3},{3,5},{5,7},{... | collective-permute-start | bytes 1572872 | tf_op jit(solution)/shard_map/ppermute | solution.py:21
  48.7 1.3 collective-permute-start.6
  48.8 1.4 collective-permute-start.7
  73.6 16.5 %collective-permute-start.10 = (f32[1,32,4096]{2,1,0:T(8,128)S(1)}, f32[1,32,4096]{2,1,0:T(8,128)S(1)}, u32[]{:S(2)}, u32[]{:S(2)}) collective-permute-start(f32[1,32,4096]{2,1,0:T(8,128)S(1)} %get-tuple-element.37), channel_id=1, source_target_pairs={{2,0},{4,2},{6,4},{8,6},{10,8},{12,10},{14,12},{3,1},{5,3},{7,5},{... | collective-permute-start | bytes 1572872 | tf_op jit(solution)/shard_map/ppermute | solution.py:24
  74.9 26.6 %collective-permute-start.11 = (f32[1,32,4096]{2,1,0:T(8,128)S(1)}, f32[1,32,4096]{2,1,0:T(8,128)S(1)}, u32[]{:S(2)}, u32[]{:S(2)}) collective-permute-start(f32[1,32,4096]{2,1,0:T(8,128)S(1)} %get-tuple-element.38), channel_id=1, source_target_pairs={{0,2},{2,4},{4,6},{6,8},{8,10},{10,12},{12,14},{1,3},{3,5},{5,7},{... | collective-permute-start | bytes 1572872 | tf_op jit(solution)/shard_map/ppermute | solution.py:21
  80.0 1.3 collective-permute-start.8
  80.1 1.4 collective-permute-start.9
  111.3 16.6 %collective-permute-start.12 = (f32[1,32,4096]{2,1,0:T(8,128)S(1)}, f32[1,32,4096]{2,1,0:T(8,128)S(1)}, u32[]{:S(2)}, u32[]{:S(2)}) collective-permute-start(f32[1,32,4096]{2,1,0:T(8,128)S(1)} %get-tuple-element.31), channel_id=1, source_target_pairs={{2,0},{4,2},{6,4},{8,6},{10,8},{12,10},{14,12},{3,1},{5,3},{7,5},{... | collective-permute-start | bytes 1572872 | tf_op jit(solution)/shard_map/ppermute | solution.py:24
  112.6 26.7 %collective-permute-start.13 = (f32[1,32,4096]{2,1,0:T(8,128)S(1)}, f32[1,32,4096]{2,1,0:T(8,128)S(1)}, u32[]{:S(2)}, u32[]{:S(2)}) collective-permute-start(f32[1,32,4096]{2,1,0:T(8,128)S(1)} %get-tuple-element.32), channel_id=1, source_target_pairs={{0,2},{2,4},{4,6},{6,8},{8,10},{10,12},{12,14},{1,3},{3,5},{5,7},{... | collective-permute-start | bytes 1572872 | tf_op jit(solution)/shard_map/ppermute | solution.py:21
  117.8 1.3 collective-permute-start.14
  117.9 1.4 collective-permute-start.15
  141.9 2.4 copy-start.3
  141.9 8.1 %copy-start.4 = (s32[4]{0:T(128)S(1)}, s32[4]{0:T(128)}, u32[]{:S(2)}) copy-start(s32[4]{0:T(128)} %param.7) | copy-start | bytes 52
  144.3 72.2 %collective-permute-start.16 = (f32[3,32,4096]{2,1,0:T(8,128)}, f32[3,32,4096]{2,1,0:T(8,128)S(1)}, u32[]{:S(2)}, u32[]{:S(2)}) collective-permute-start(f32[3,32,4096]{2,1,0:T(8,128)} %get-tuple-element.25), channel_id=1, source_target_pairs={{0,2},{2,4},{4,6},{6,8},{8,10},{10,12},{12,14},{1,3},{3,5},{5,7},{... | collective-permute-start | bytes 4718600 | tf_op jit(solution)/shard_map/ppermute | solution.py:21
  148.7 67.8 %collective-permute-start.17 = (f32[3,32,4096]{2,1,0:T(8,128)}, f32[3,32,4096]{2,1,0:T(8,128)S(1)}, u32[]{:S(2)}, u32[]{:S(2)}) collective-permute-start(f32[3,32,4096]{2,1,0:T(8,128)} %get-tuple-element.26), channel_id=1, source_target_pairs={{2,0},{4,2},{6,4},{8,6},{10,8},{12,10},{14,12},{3,1},{5,3},{7,5},{... | collective-permute-start | bytes 4718600 | tf_op jit(solution)/shard_map/ppermute | solution.py:24
  218.6 2.3 copy-start
  218.6 2.3 copy-start.5
where the time goes:
time: 262 us; the launch traced here: 261 us
  waiting for transfers between devices  147 us (56%)
  starting transfers between devices  33.9 us (13%)
  other arithmetic  28.6 us (11%)
  blocking collectives  27.1 us (10%)
  local copies, waits for them, and re-layouts  23.2 us (9%)
    ppermute x9, waiting for transfers between devices, with_halo(): lax.ppermute(lax.slice_in_dim(block, block.shape[dim] - width, None, axis...  113 us
    ppermute x9, waiting for transfers between devices, with_halo(): lax.ppermute(lax.slice_in_dim(block, 0, width, axis=dim), axis, backward)  34.5 us
    ppermute x9, starting transfers between devices, with_halo(): lax.ppermute(lax.slice_in_dim(block, block.shape[dim] - width, None, axis...  27 us
    unnamed x1, blocking collectives  19.7 us
    reduce_sum x2, other arithmetic, theta_of(): jnp.sum(tangent * tangent, axis=(1, 2))  9.56 us
    ppermute x9, starting transfers between devices, with_halo(): lax.ppermute(lax.slice_in_dim(block, 0, width, axis=dim), axis, backward)  6.86 us
  transfers between devices with their start and end apart: 18, of which 15 were waited for; matrix products, arithmetic and copies ran while one was open for 1% of the time, Pallas kernels for 0%

commit v1 on v0

v1 whole, which is shorter than its diff:
```python
import functools

import jax
import jax.numpy as jnp
from jax import lax
from jax.experimental import pallas as pl
from jax.experimental.pallas import tpu as pltpu
from jax.sharding import PartitionSpec as P

REACH = 2
ITERS = 2
TIME_STEP = 0.002
EPSILON = 1e-06

LANES = 128
SUBLANES = 8
PAIR = 2
LOW = 2 * ITERS + 1
HIGH = 2 * ITERS
EDGE = 2 * ITERS
VMEM_LIMIT = 28 * 1024 * 1024

F32 = jnp.float32


def call(kernel, out_shapes, scratch=(), smem=0, operands=0, aliases=None):
    specs = [pl.BlockSpec(memory_space=pltpu.SMEM)] * smem
    specs += [pl.BlockSpec(memory_space=pltpu.VMEM)] * operands
    return pl.pallas_call(
        kernel,
        out_shape=out_shapes,
        in_specs=specs,
        out_specs=jax.tree.map(lambda _: pl.BlockSpec(memory_space=pltpu.VMEM), out_shapes),
        scratch_shapes=list(scratch),
        compiler_params=pltpu.CompilerParams(vmem_limit_bytes=VMEM_LIMIT),
    )


def pair_position():
    index = lax.axis_index("img")
    return lax.div(index, PAIR), lax.rem(index, PAIR)


def swap_pairs(value):
    count = lax.axis_size("img")
    return lax.ppermute(value, "img", [(i, i ^ 1) for i in range(count)])


def small_sum(value, steps):
    size = lax.axis_size("space")
    if size & (size - 1) == 0:
        step = 1
        while step < size:
            value = value + lax.ppermute(value, "space", [(i, i ^ step) for i in range(size)])
            step *= 2
    else:
        value = lax.psum(value, "space")
    count = lax.axis_size("img")
    for step in steps:
        value = value + lax.ppermute(value, "img", [(i, i ^ step) for i in range(count)])
    return value


def neighbour_rows(block):
    size = lax.axis_size("space")
    top, bottom = block[:, :EDGE], block[:, -EDGE:]
    if size == 1:
        return jnp.concatenate([top, bottom], axis=1)
    if size == 2:
        return lax.ppermute(jnp.concatenate([top, bottom], axis=1), "space", [(0, 1), (1, 0)])
    after = lax.ppermute(top, "space", [(i, (i - 1) % size) for i in range(size)])
    before = lax.ppermute(bottom, "space", [(i, (i + 1) % size) for i in range(size)])
    return jnp.concatenate([after, before], axis=1)


def pack_kernel(x_ref, keep_ref, send_ref):
    _, lo = pair_position()
    columns = x_ref.shape[2]
    half = columns // PAIR
    lane = lax.broadcasted_iota(jnp.int32, (x_ref.shape[1], LANES), 1)

    def body(k, carry):
        for ref, part in ((keep_ref, lo), (send_ref, 1 - lo)):
            begin = pl.multiple_of(part * half, LANES)
            right = pl.multiple_of((1 - part) * half, LANES)
            left = pl.multiple_of((1 - part) * half + half - LANES, LANES)
            ref[k, :, 0:half] = x_ref[k, :, pl.ds(begin, half)]
            ref[k, :, half:] = jnp.where(
                lane < LANES // 2, x_ref[k, :, pl.ds(right, LANES)], x_ref[k, :, pl.ds(left, LANES)]
            )
        return carry

    lax.fori_loop(0, x_ref.shape[0], body, 0)


def sum_of_neighbours(load, tiles, rows, use):
    lane = lax.broadcasted_iota(jnp.int32, (rows, LANES), 1)
    is_first, is_last = lane == 0, lane == LANES - 1
    center = load(0)
    from_left = pltpu.roll(load(tiles - 1), 1, 1)
    to_left = pltpu.roll(center, LANES - 1, 1)
    for t in range(tiles):
        following = load((t + 1) % tiles)
        shifted = pltpu.roll(center, 1, 1)
        next_to_left = pltpu.roll(following, LANES - 1, 1)
        west = jnp.where(is_first, from_left, shifted)
        east = jnp.where(is_last, next_to_left, to_left)
        north = pltpu.roll(center, 1, 0)
        south = pltpu.roll(center, rows - 1, 0)
        use(t, center, (north + south) + (west + east))
        center, from_left, to_left = following, shifted, next_to_left


def tile_of(t):
    return slice(t * LANES, (t + 1) * LANES)


def neighbours_of(k, first, count):
    gid = k + first
    is_first, is_last = gid == 0, gid == count - 1
    before = jnp.where(is_first, k, k - 1)
    after = jnp.where(is_last, k, k + 1)
    stretch = jnp.where(is_first | is_last, F32(count - 1), F32((count - 1) / 2.0))
    return before, after, stretch


def fold(value):
    return jnp.sum(value.reshape(-1, SUBLANES, LANES), axis=0)


def drift_pass(phi, drift, norms, low, high, first, count, own_rows):
    rows = phi.shape[1]
    tiles = phi.shape[2] // LANES

    def body(k, carry):
        before, after, stretch = neighbours_of(k, first, count)
        sums = [jnp.zeros((SUBLANES, LANES), F32), jnp.zeros((SUBLANES, LANES), F32)]

        def use(t, center, total):
            force = total - center * (3.0 + center * center)
            drift[k, :, tile_of(t)] = force
            if t < tiles - 1:
                step = phi[after, 0:own_rows, tile_of(t)] - phi[before, 0:own_rows, tile_of(t)]
                own = force[0:own_rows]
                sums[0] = sums[0] + fold(own * own)
                sums[1] = sums[1] + fold(step * step)

        sum_of_neighbours(lambda t: phi[k, :, tile_of(t)], tiles, rows, use)
        norms[0, pl.ds(k, 1), :] = jnp.sum(sums[0], axis=0, keepdims=True)
        norms[1, pl.ds(k, 1), :] = jnp.sum(sums[1], axis=0, keepdims=True) * (stretch * stretch)
        return carry

    lax.fori_loop(low, high, body, 0)


def speeds_of(norms, speeds):
    force = jnp.sum(norms[0], axis=1, keepdims=True)
    path = jnp.sum(norms[1], axis=1, keepdims=True)
    value = jnp.sqrt(force + EPSILON) / jnp.sqrt(path + EPSILON)
    speeds[...] = jnp.broadcast_to(value, speeds.shape)


def theta_pass(phi, drift, speeds, theta, low, high, first, count):
    tiles = phi.shape[2] // LANES

    def body(k, carry):
        before, after, stretch = neighbours_of(k, first, count)
        scale = speeds[pl.ds(k, 1), :] * stretch
        for t in range(tiles):
            cols = tile_of(t)
            theta[k, :, cols] = scale * (phi[after, :, cols] - phi[before, :, cols]) - drift[k, :, cols]
        return carry

    lax.fori_loop(low, high, body, 0)


def update_pass(phi, speeds, theta, low, high, first, count, store):
    rows = phi.shape[1]
    tiles = phi.shape[2] // LANES

    def body(k, carry):
        before, after, stretch = neighbours_of(k, first, count)
        scale = speeds[pl.ds(k, 1), :] * stretch
        gid = k + first
        inside = (gid > 0) & (gid < count - 1)

        def use(t, center, total):
            cols = tile_of(t)
            value = phi[k, :, cols]
            descent = (
                scale * (theta[after, :, cols] - theta[before, :, cols])
                + total
                - (3.0 * center) * (1.0 + value * value)
            )
            store(k, t, jnp.where(inside, value + TIME_STEP * descent, value))

        sum_of_neighbours(lambda t: theta[k, :, tile_of(t)], tiles, rows, use)
        return carry

    lax.fori_loop(low, high, body, 0)


def start_kernel(*refs, count):
    (keep, recv, near, far, extra_low, extra_high, keep_rows, recv_rows, near_rows, far_rows, extra_rows,
     phi, drift, norms) = refs
    local, rows, _ = keep.shape
    hi, lo = pair_position()
    first = hi * (PAIR * local) - LOW

    def place(source, edge_rows, at, index):
        phi[at, 0:rows, :] = source[index]
        phi[at, rows:, :] = edge_rows[index]

    def body(i, carry):
        place(keep, keep_rows, LOW + lo * local + i, i)
        place(recv, recv_rows, LOW + (1 - lo) * local + i, i)
        low_at, high_at = LOW - local + i, LOW + PAIR * local + i
        place(near, near_rows, jnp.where(lo == 1, low_at, high_at), i)
        place(far, far_rows, jnp.where(lo == 1, high_at, low_at), i)
        return carry

    lax.fori_loop(0, local, body, 0)
    for i in range(LOW - local):

        @pl.when(lo == 0)
        def _():
            phi[i, 0:rows, :] = extra_low[i]

        @pl.when(lo == 1)
        def _():
            phi[i, 0:rows, :] = extra_high[i]

        phi[i, rows:, :] = extra_rows[i]
    norms[...] = jnp.zeros(norms.shape, F32)
    drift_pass(phi, drift, norms, 1, phi.shape[0] - 1, first, count, rows)


def middle_kernel(phi, drift, norms, new_phi, new_drift, new_norms, theta, speeds, *, count, local, rows, done):
    hi, _ = pair_position()
    first = hi * (PAIR * local) - LOW
    window = phi.shape[0]
    speeds_of(norms, speeds)
    theta_pass(phi, drift, speeds, theta, done + 1, window - done - 1, first, count)

    def store(k, t, value):
        new_phi[k, :, tile_of(t)] = value

    update_pass(phi, speeds, theta, done + 2, window - done - 2, first, count, store)
    new_norms[...] = jnp.zeros(new_norms.shape, F32)
    drift_pass(new_phi, new_drift, new_norms, done + 3, window - done - 3, first, count, rows)


def last_kernel(phi, drift, norms, own, down, up, squares, theta, speeds, final, *, count, local, rows, done):
    hi, _ = pair_position()
    first = hi * (PAIR * local) - LOW
    window = phi.shape[0]
    columns = own.shape[2]
    speeds_of(norms, speeds)
    theta_pass(phi, drift, speeds, theta, done + 1, window - done - 1, first, count)

    def store(k, t, value):
        if t < columns // LANES:
            final[k, :, tile_of(t)] = value[0:rows]

    update_pass(phi, speeds, theta, done + 2, window - done - 2, first, count, store)
    position = (
        lax.broadcasted_iota(jnp.int32, squares.shape, 0) * LANES
        + lax.broadcasted_iota(jnp.int32, squares.shape, 1)
    )

    def body(i, total):
        k = LOW + i
        acc = jnp.zeros((SUBLANES, LANES), F32)
        for t in range(columns // LANES):
            value = final[k, :, tile_of(t)]
            own[i, :, tile_of(t)] = value
            diff = value - final[k - 1, :, tile_of(t)]
            acc = acc + fold(diff * diff)
        amount = jnp.sum(jnp.sum(acc, axis=0, keepdims=True), axis=1, keepdims=True)
        return total + jnp.where(position == k + first, amount, 0.0)

    squares[...] = lax.fori_loop(0, PAIR * local, body, jnp.zeros(squares.shape, F32))
    for i in range(REACH + 1):
        down[i] = final[LOW + i]
    for i in range(REACH):
        up[i] = final[LOW + PAIR * local - REACH + i]


def combine_kernel(own_bracket, pair_bracket, own, low, high, squares, keep, send, window, *, count):
    hi, lo = pair_position()
    local = keep.shape[0]
    tiles = own.shape[2] // LANES
    begin = hi * (PAIR * local)
    for i in range(REACH):
        window[i] = low[i]
    for i in range(REACH + 1):
        window[REACH + PAIR * local + i] = high[i]

    def copy(i, carry):
        window[REACH + i] = own[i]
        return carry

    lax.fori_loop(0, PAIR * local, copy, 0)
    position = (
        lax.broadcasted_iota(jnp.int32, squares.shape, 0) * LANES
        + lax.broadcasted_iota(jnp.int32, squares.shape, 1)
    )
    counted = (position >= 1) & (position < count)
    segments = jnp.where(counted, jnp.sqrt(squares[...] + EPSILON), 0.0)

    def total(value):
        return jnp.sum(jnp.sum(value, axis=0, keepdims=True), axis=1, keepdims=True)

    length = total(segments)
    for bracket, part, out in ((own_bracket, lo, keep), (pair_bracket, 1 - lo, send)):

        def body(i, carry):
            b = bracket[i]
            j = begin + part * local + i
            arc = total(jnp.where(position <= b, segments, 0.0))
            segment = total(jnp.where(position == b + 1, segments, 0.0))
            target = length * lax.convert_element_type(j, F32) / F32(count - 1)
            weight = (target - arc) / segment
            at = b - begin + REACH
            for t in range(tiles):
                base = window[at, :, tile_of(t)]
                out[i, :, tile_of(t)] = base + weight * (window[at + 1, :, tile_of(t)] - base)
            return carry

        lax.fori_loop(0, local, body, 0)


def per_device(path, bracket):
    local, rows, columns = path.shape
    devices = lax.axis_size("img")
    count = local * devices
    half = columns // PAIR
    wide = half + LANES
    window = LOW + PAIR * local + HIGH
    if devices & (devices - 1) or local != HIGH or count > SUBLANES * LANES or rows % SUBLANES:
        raise ValueError("unsupported sizes")
    shape = functools.partial(jax.ShapeDtypeStruct, dtype=F32)
    block = shape((local, rows, wide))
    other_bracket = swap_pairs(bracket)
    keep, send = call(pack_kernel, (block, block), operands=1)(path)
    recv = swap_pairs(send)
    ahead = [(i, i + PAIR) for i in range(devices - PAIR)]
    back = [(target, source) for source, target in ahead]
    near = lax.ppermute(keep, "img", [p for p in ahead if p[0] % PAIR == 1] + [p for p in back if p[0] % PAIR == 0])
    far = lax.ppermute(recv, "img", [p for p in ahead if p[0] % PAIR == 0] + [p for p in back if p[0] % PAIR == 1])
    spare = LOW - local
    extra_low = lax.ppermute(keep[-spare:], "img", [p for p in ahead if p[0] % PAIR == 0])
    extra_high = lax.ppermute(recv[-spare:], "img", [p for p in ahead if p[0] % PAIR == 1])
    keep_rows = neighbour_rows(keep)
    late = neighbour_rows(jnp.concatenate([recv, near, far, extra_low + extra_high], axis=0))
    recv_rows, near_rows, far_rows, extra_rows = (
        late[:local], late[local : 2 * local], late[2 * local : 3 * local], late[3 * local :]
    )
    held = shape((window, rows + 2 * EDGE, wide))
    lines = -(-window // SUBLANES) * SUBLANES
    norm_shape = shape((2, lines, LANES))
    phi, drift, norms = call(functools.partial(start_kernel, count=count), (held, held, norm_shape), operands=11)(
        keep, recv, near, far, extra_low, extra_high, keep_rows, recv_rows, near_rows, far_rows, extra_rows
    )
    scratch = [pltpu.VMEM(held.shape, F32), pltpu.VMEM((lines, LANES), F32)]
    for iteration in range(ITERS - 1):
        norms = small_sum(norms, (1,))
        phi, drift, norms = call(
            functools.partial(middle_kernel, count=count, local=local, rows=rows, done=2 * iteration),
            (held, held, norm_shape), scratch=scratch, operands=3,
        )(phi, drift, norms)
    norms = small_sum(norms, (1,))
    half_block = lambda n: shape((n, rows, half))
    own, down, up, squares = call(
        functools.partial(last_kernel, count=count, local=local, rows=rows, done=2 * (ITERS - 1)),
        (half_block(PAIR * local), half_block(REACH + 1), half_block(REACH), shape((SUBLANES, LANES))),
        scratch=scratch + [pltpu.VMEM((window, rows, half), F32)], operands=3,
    )(phi, drift, norms)
    steps = []
    step = 1
    while step < devices:
        steps.append(step)
        step *= 2
    squares = small_sum(squares, steps)
    low = lax.ppermute(up, "img", ahead)
    high = lax.ppermute(down, "img", back)
    mine, theirs = call(
        functools.partial(combine_kernel, count=count), (half_block(local), half_block(local)),
        scratch=[pltpu.VMEM((PAIR * local + 2 * REACH + 1, rows, half), F32)], smem=2, operands=4,
    )(bracket, other_bracket, own, low, high, squares)
    other = swap_pairs(theirs)
    is_low = lax.rem(lax.axis_index("img"), PAIR) == 0
    return jnp.concatenate([jnp.where(is_low, mine, other), jnp.where(is_low, other, mine)], axis=2)


def solution(mesh):
    return jax.shard_map(
        per_device,
        mesh=mesh,
        in_specs=(P(("groups", "img"), "space", None), P(("groups", "img"))),
        out_specs=P(("groups", "img"), "space", None),
        check_vma=False,
    )
```

time: 262 us -> 146 us (0.56)
  waiting for transfers between devices: 147 us -> 97.4 us
  blocking collectives: 27.1 us -> 0 us
  other arithmetic: 28.6 us -> 1.87 us
  local copies, waits for them, and re-layouts: 23.2 us -> 1.75 us
  Pallas kernels: 0 us -> 19.1 us
  starting transfers between devices: 33.9 us -> 24.9 us
    ppermute x18 -> x19, waiting for transfers between devices: 147 us -> 97.4 us  [the longest x3 46.6 us: swap_pairs(): return lax.ppermute(value, 'img', [(i, i ^ 1) for i in range(count)])]
    unnamed x1 -> x0, blocking collectives: 19.7 us -> none
    pallas_call x0 -> x5, Pallas kernels: none -> 19.1 us  [the longest x1 8.43 us: per_device(): call(functools.partial(middle_kernel, count=count, local=local, rows=rows...]
    slice x18 -> x5, local copies, waits for them, and re-layouts: 11.1 us -> 0.15 us  [the longest x1 0.05 us: per_device(): late[2 * local:3 * local]]
    reduce_sum x4 -> x0, other arithmetic: 10.9 us -> none  [the longest x2 9.56 us: theta_of(): jnp.sum(tangent * tangent, axis=(1, 2))]
    ppermute x18 -> x19, starting transfers between devices: 33.9 us -> 24.9 us  [the longest x1 5.05 us: per_device(): low = lax.ppermute(up, 'img', ahead)]
    gather x4 -> x0, local copies, waits for them, and re-layouts: 8.93 us -> none  [the longest x1 4.49 us: per_device(): upper = jnp.take(window, local_pick + 1, axis=0)]
    add x4 -> x9, other arithmetic: 8.35 us -> 0.06 us  [the longest x1 0.03 us: per_device(): extra_low + extra_high]
  transfers between devices with their start and end apart: 18 -> 19, of which waited for: 15 -> 14; matrix products, arithmetic and copies ran while one was open for 1% -> 0% of each run, Pallas kernels for 0% -> 0%
where the time goes in v1:
time: 146 us; the launch traced here: 145 us
  waiting for transfers between devices  97.4 us (67%)
  starting transfers between devices  24.9 us (17%)
  Pallas kernels  19.1 us (13%)
  other arithmetic  1.87 us (1%)
  local copies, waits for them, and re-layouts  1.75 us (1%)
    ppermute x3, waiting for transfers between devices, swap_pairs(): return lax.ppermute(value, 'img', [(i, i ^ 1) for i in range(count)])  46.6 us
    ppermute x1, waiting for transfers between devices, per_device(): lax.ppermute(keep[-spare:], 'img', [p for p in ahead if p[0] % PAIR == 0])  24.7 us
    ppermute x5, waiting for transfers between devices, small_sum(): lax.ppermute(value, 'img', [(i, i ^ step) for i in range(count)])  20.7 us
    pallas_call x1, Pallas kernels, per_device(): call(functools.partial(middle_kernel, count=count, local=local, rows=rows...  8.43 us
    ppermute x1, starting transfers between devices, per_device(): low = lax.ppermute(up, 'img', ahead)  5.05 us
    ppermute x5, starting transfers between devices, small_sum(): lax.ppermute(value, 'img', [(i, i ^ step) for i in range(count)])  4.78 us
    pallas_call x1, Pallas kernels, per_device(): call(functools.partial(start_kernel, count=count), (held, held, norm_shap...  4.62 us
    pallas_call x1, Pallas kernels, per_device(): call(functools.partial(last_kernel, count=count, local=local, rows=rows,...  4.11 us
  transfers between devices with their start and end apart: 19, of which 14 were waited for; matrix products, arithmetic and copies ran while one was open for 0% of the time, Pallas kernels for 0%

profile of v1, /device:TPU:0, one launch (start us, length us, event | category | flops | bytes accessed | tf_op | source)
XLA Modules:
  0.0 145.3 jit_solution(7276283391552308574)
XLA Ops:
  0.0 1.6 %copy-done = f32[4,32,4096]{2,1,0:T(8,128)S(1)} copy-done((f32[4,32,4096]{2,1,0:T(8,128)S(1)}, f32[4,32,4096]{2,1,0:T(8,128)}, u32[]{:S(2)}) %copy-start) | copy-done | bytes 2097176
  1.8 3.1 %collective-permute-start.1 = (f32[4,32,2176]{2,1,0:T(8,128)S(1)}, f32[4,32,2176]{2,1,0:T(8,128)S(1)}, u32[]{:S(2)}, u32[]{:S(2)}) collective-permute-start(f32[4,32,2176]{2,1,0:T(8,128)S(1)} %get-tuple-element.20), channel_id=1, source_target_pairs={{0,2},{2,0},{4,6},{6,4},{8,10},{10,8},{12,14},{14,12},{1,3},{3,1},... | collective-permute-start | bytes 3342344 | tf_op jit(solution)/shard_map/ppermute | solution.py:46
  4.8 1.3 collective-permute-start.2
  6.1 23.3 %collective-permute-done.1.refs_1_ = f32[4,32,2176]{2,1,0:T(8,128)S(1)} collective-permute-done((f32[4,32,2176]{2,1,0:T(8,128)S(1)}, f32[4,32,2176]{2,1,0:T(8,128)S(1)}, u32[]{:S(2)}, u32[]{:S(2)}) %collective-permute-start.1) | collective-permute-done | bytes 1114144 | tf_op jit(solution)/shard_map/ppermute | solution.py:46
  29.4 3.8 %collective-permute-start.3 = (f32[4,32,2176]{2,1,0:T(8,128)S(1)}, f32[4,32,2176]{2,1,0:T(8,128)S(1)}, u32[]{:S(2)}, u32[]{:S(2)}) collective-permute-start(f32[4,32,2176]{2,1,0:T(8,128)S(1)} %collective-permute-done.1.refs_1_), channel_id=1, source_target_pairs={{0,4},{4,8},{8,12},{6,2},{10,6},{14,10},{1,5},{5,9},{9,13},{7,3},{... | collective-permute-start | bytes 3342344 | tf_op jit(solution)/shard_map/ppermute | solution.py:350
  33.2 3.4 %collective-permute-start.4 = (f32[1,32,2176]{2,1,0:T(8,128)S(1)}, f32[1,32,2176]{2,1,0:T(8,128)S(1)}, u32[]{:S(2)}, u32[]{:S(2)}) collective-permute-start(f32[1,32,2176]{2,1,0:T(8,128)S(1)} %slice.30), channel_id=1, source_target_pairs={{0,4},{4,8},{8,12},{1,5},{5,9},{9,13},{16,20},{20,24},{24,28},{17,... | collective-permute-start | bytes 835592 | tf_op jit(solution)/shard_map/ppermute | solution.py:352
  36.6 0.7 collective-permute-start.5
  37.3 24.7 %collective-permute-done.4.refs_4_ = f32[1,32,2176]{2,1,0:T(8,128)S(1)} collective-permute-done((f32[1,32,2176]{2,1,0:T(8,128)S(1)}, f32[1,32,2176]{2,1,0:T(8,128)S(1)}, u32[]{:S(2)}, u32[]{:S(2)}) %collective-permute-start.4) | collective-permute-done | bytes 278560 | tf_op jit(solution)/shard_map/ppermute | solution.py:352
  62.4 0.6 collective-permute-start.6
  62.9 1.8 %collective-permute-done.7 = f32[13,8,2176]{2,1,0:T(8,128)S(1)} collective-permute-done((f32[13,8,2176]{2,1,0:T(8,128)S(1)}, f32[13,8,2176]{2,1,0:T(8,128)S(1)}, u32[]{:S(2)}, u32[]{:S(2)}) %collective-permute-start.7) | collective-permute-done | bytes 905248 | tf_op jit(solution)/shard_map/ppermute | solution.py:70
  64.8 0.3 collective-permute-done.6.refs_6_
  65.1 4.6 %shard_map.29 = (f32[17,40,2176]{2,1,0:T(8,128)S(1)}, f32[17,40,2176]{2,1,0:T(8,128)S(1)}, f32[2,24,128]{2,1,0:T(8,128)S(1)}) custom-call(f32[4,32,2176]{2,1,0:T(8,128)S(1)} %get-tuple-element.19.refs_0_, f32[4,32,2176]{2,1,0:T(8,128)S(1)} %collective-permute-done.1.refs_1_, f32[4,32,2176]{2,1,0:T(8,128)S(1)} %collective-permute-done.2.refs_2_, ...), custom_call_target="tpu_custom_call" | custom-call | tf_op jit(solution)/shard_map/pallas_call | solution.py:362
  69.9 1.1 collective-permute-done.8
  71.0 3.8 %collective-permute-done.9 = f32[2,24,128]{2,1,0:T(8,128)S(1)} collective-permute-done((f32[2,24,128]{2,1,0:T(8,128)S(1)}, f32[2,24,128]{2,1,0:T(8,128)S(1)}, u32[]{:S(2)}, u32[]{:S(2)}) %collective-permute-start.9) | collective-permute-done | bytes 24608 | tf_op jit(solution)/shard_map/ppermute | solution.py:60
  74.8 8.4 %shard_map.30 = (f32[17,40,2176]{2,1,0:T(8,128)S(1)}, f32[17,40,2176]{2,1,0:T(8,128)S(1)}, f32[2,24,128]{2,1,0:T(8,128)S(1)}) custom-call(f32[17,40,2176]{2,1,0:T(8,128)S(1)} %get-tuple-element.21.phi, f32[17,40,2176]{2,1,0:T(8,128)S(1)} %get-tuple-element.22.drift, f32[2,24,128]{2,1,0:T(8,128)S(1)} %add.29.norms), custom_call_target="tpu_custom_call" | custom-call | tf_op jit(solution)/shard_map/pallas_call | solution.py:368
  83.3 1.2 collective-permute-done.10
  84.5 3.8 %collective-permute-done.11 = f32[2,24,128]{2,1,0:T(8,128)S(1)} collective-permute-done((f32[2,24,128]{2,1,0:T(8,128)S(1)}, f32[2,24,128]{2,1,0:T(8,128)S(1)}, u32[]{:S(2)}, u32[]{:S(2)}) %collective-permute-start.11) | collective-permute-done | bytes 24608 | tf_op jit(solution)/shard_map/ppermute | solution.py:60
  88.4 4.1 %shard_map.31 = (f32[8,32,2048]{2,1,0:T(8,128)S(1)}, f32[3,32,2048]{2,1,0:T(8,128)S(1)}, f32[2,32,2048]{2,1,0:T(8,128)S(1)}, f32[8,128]{1,0:T(8,128)S(1)}) custom-call(f32[17,40,2176]{2,1,0:T(8,128)S(1)} %get-tuple-element.24.phi, f32[17,40,2176]{2,1,0:T(8,128)S(1)} %get-tuple-element.25.drift, f32[2,24,128]{2,1,0:T(8,128)S(1)} %add.31.norms), custom_call_target="tpu_custom_call" | custom-call | tf_op jit(solution)/shard_map/pallas_call | solution.py:374
  92.5 1.3 collective-permute-start.13
  93.8 5.0 %collective-permute-start.12 = (f32[2,32,2048]{2,1,0:T(8,128)S(1)}, f32[2,32,2048]{2,1,0:T(8,128)S(1)}, u32[]{:S(2)}, u32[]{:S(2)}) collective-permute-start(f32[2,32,2048]{2,1,0:T(8,128)S(1)} %get-tuple-element.28), channel_id=1, source_target_pairs={{0,4},{2,6},{4,8},{6,10},{8,12},{10,14},{1,5},{3,7},{5,9},{7,11},{... | collective-permute-start | bytes 1572872 | tf_op jit(solution)/shard_map/ppermute | solution.py:385
  98.9 1.2 collective-permute-done.14
  100.1 3.6 %collective-permute-done.15 = f32[8,128]{1,0:T(8,128)S(1)} collective-permute-done((f32[8,128]{1,0:T(8,128)S(1)}, f32[8,128]{1,0:T(8,128)S(1)}, u32[]{:S(2)}, u32[]{:S(2)}) %collective-permute-start.15) | collective-permute-done | bytes 4128 | tf_op jit(solution)/shard_map/ppermute | solution.py:60
  103.7 2.0 %collective-permute-start.16 = (f32[8,128]{1,0:T(8,128)S(1)}, f32[8,128]{1,0:T(8,128)S(1)}, u32[]{:S(2)}, u32[]{:S(2)}) collective-permute-start(f32[8,128]{1,0:T(8,128)S(1)} %add.33), channel_id=1, source_target_pairs={{0,4},{2,6},{4,0},{6,2},{8,12},{10,14},{12,8},{14,10},{1,5},{3,7},... | collective-permute-start | bytes 12296 | tf_op jit(solution)/shard_map/ppermute | solution.py:60
  105.7 8.0 %collective-permute-done.16 = f32[8,128]{1,0:T(8,128)S(1)} collective-permute-done((f32[8,128]{1,0:T(8,128)S(1)}, f32[8,128]{1,0:T(8,128)S(1)}, u32[]{:S(2)}, u32[]{:S(2)}) %collective-permute-start.16) | collective-permute-done | bytes 4128 | tf_op jit(solution)/shard_map/ppermute | solution.py:60
  113.7 2.8 %collective-permute-start.17 = (f32[8,128]{1,0:T(8,128)S(1)}, f32[8,128]{1,0:T(8,128)S(1)}, u32[]{:S(2)}, u32[]{:S(2)}) collective-permute-start(f32[8,128]{1,0:T(8,128)S(1)} %add.34), channel_id=1, source_target_pairs={{0,8},{2,10},{4,12},{6,14},{8,0},{10,2},{12,4},{14,6},{1,9},{3,11}... | collective-permute-start | bytes 12296 | tf_op jit(solution)/shard_map/ppermute | solution.py:60
  116.5 0.3 collective-permute-start
  116.8 1.4 collective-permute-done.17
  118.2 1.9 %collective-permute-done.pair_bracket = s32[4]{0:T(128)S(1)} collective-permute-done((s32[4]{0:T(128)S(1)}, s32[4]{0:T(128)S(1)}, u32[]{:S(2)}, u32[]{:S(2)}) %collective-permute-start) | collective-permute-done | bytes 48 | tf_op jit(solution)/shard_map/ppermute | solution.py:46
  120.0 1.8 %shard_map.32 = (f32[4,32,2048]{2,1,0:T(8,128)S(1)}, f32[4,32,2048]{2,1,0:T(8,128)S(1)}) custom-call(s32[4]{0:T(128)S(1)} %copy-done.1, s32[4]{0:T(128)S(1)} %collective-permute-done.pair_bracket, f32[8,32,2048]{2,1,0:T(8,128)S(1)} %get-tuple-element.27.own, f32[2,32,2048]{2,1,0:T(8,128)S(1)} %collective-permute-done.12.low, ...), custom_call_target="tpu_custom_call" | custom-call | tf_op jit(solution)/shard_map/pallas_call | solution.py:387
  121.8 0.3 collective-permute-start.18
  122.2 21.5 %collective-permute-done.18 = f32[4,32,2048]{2,1,0:T(8,128)S(1)} collective-permute-done((f32[4,32,2048]{2,1,0:T(8,128)S(1)}, f32[4,32,2048]{2,1,0:T(8,128)S(1)}, u32[]{:S(2)}, u32[]{:S(2)}) %collective-permute-start.18) | collective-permute-done | bytes 1048608 | tf_op jit(solution)/shard_map/ppermute | solution.py:46
  143.8 1.5 %pad_maximum_fusion = f32[4,32,4096]{2,1,0:T(8,128)} fusion(f32[4,32,2048]{2,1,0:T(8,128)S(1)} %get-tuple-element.34, f32[4,32,2048]{2,1,0:T(8,128)S(1)} %get-tuple-element.33), kind=kLoop, calls=%fused_computation | loop fusion | flops 524288 | bytes 4194304 | tf_op jit(solution)/shard_map/concatenate | solution.py:393
  (33 shorter events, 1.2 us)
Async XLA Ops:
  0.0 1.6 %copy-start = (f32[4,32,4096]{2,1,0:T(8,128)S(1)}, f32[4,32,4096]{2,1,0:T(8,128)}, u32[]{:S(2)}) copy-start(f32[4,32,4096]{2,1,0:T(8,128)} %x_ref.1) | copy-start | bytes 6291460
  1.8 27.6 %collective-permute-start.1 = (f32[4,32,2176]{2,1,0:T(8,128)S(1)}, f32[4,32,2176]{2,1,0:T(8,128)S(1)}, u32[]{:S(2)}, u32[]{:S(2)}) collective-permute-start(f32[4,32,2176]{2,1,0:T(8,128)S(1)} %get-tuple-element.20), channel_id=1, source_target_pairs={{0,2},{2,0},{4,6},{6,4},{8,10},{10,8},{12,14},{14,12},{1,3},{3,1},... | collective-permute-start | bytes 3342344 | tf_op jit(solution)/shard_map/ppermute | solution.py:46
  4.8 57.2 %collective-permute-start.2 = (f32[4,32,2176]{2,1,0:T(8,128)S(1)}, f32[4,32,2176]{2,1,0:T(8,128)S(1)}, u32[]{:S(2)}, u32[]{:S(2)}) collective-permute-start(f32[4,32,2176]{2,1,0:T(8,128)S(1)} %get-tuple-element.19.refs_0_), channel_id=1, source_target_pairs={{2,6},{6,10},{10,14},{4,0},{8,4},{12,8},{3,7},{7,11},{11,15},{5,1}... | collective-permute-start | bytes 3342344 | tf_op jit(solution)/shard_map/ppermute | solution.py:349
  29.4 32.7 %collective-permute-start.3 = (f32[4,32,2176]{2,1,0:T(8,128)S(1)}, f32[4,32,2176]{2,1,0:T(8,128)S(1)}, u32[]{:S(2)}, u32[]{:S(2)}) collective-permute-start(f32[4,32,2176]{2,1,0:T(8,128)S(1)} %collective-permute-done.1.refs_1_), channel_id=1, source_target_pairs={{0,4},{4,8},{8,12},{6,2},{10,6},{14,10},{1,5},{5,9},{9,13},{7,3},{... | collective-permute-start | bytes 3342344 | tf_op jit(solution)/shard_map/ppermute | solution.py:350
  33.2 28.8 %collective-permute-start.4 = (f32[1,32,2176]{2,1,0:T(8,128)S(1)}, f32[1,32,2176]{2,1,0:T(8,128)S(1)}, u32[]{:S(2)}, u32[]{:S(2)}) collective-permute-start(f32[1,32,2176]{2,1,0:T(8,128)S(1)} %slice.30), channel_id=1, source_target_pairs={{0,4},{4,8},{8,12},{1,5},{5,9},{9,13},{16,20},{20,24},{24,28},{17,... | collective-permute-start | bytes 835592 | tf_op jit(solution)/shard_map/ppermute | solution.py:352
  36.6 25.4 %collective-permute-start.5 = (f32[1,32,2176]{2,1,0:T(8,128)S(1)}, f32[1,32,2176]{2,1,0:T(8,128)S(1)}, u32[]{:S(2)}, u32[]{:S(2)}) collective-permute-start(f32[1,32,2176]{2,1,0:T(8,128)S(1)} %slice.40), channel_id=1, source_target_pairs={{2,6},{6,10},{10,14},{3,7},{7,11},{11,15},{18,22},{22,26},{26,30},... | collective-permute-start | bytes 835592 | tf_op jit(solution)/shard_map/ppermute | solution.py:353
  62.2 2.5 %collective-permute-start.7 = (f32[13,8,2176]{2,1,0:T(8,128)S(1)}, f32[13,8,2176]{2,1,0:T(8,128)S(1)}, u32[]{:S(2)}, u32[]{:S(2)}) collective-permute-start(f32[13,8,2176]{2,1,0:T(8,128)S(1)} %fusion), channel_id=1, source_target_pairs={{0,1},{1,0},{2,3},{3,2},{4,5},{5,4},{6,7},{7,6},{8,9},{9,8},{10,11... | collective-permute-start | bytes 2715656 | tf_op jit(solution)/shard_map/ppermute | solution.py:70
  62.4 2.7 %collective-permute-start.6 = (f32[4,8,2176]{2,1,0:T(8,128)S(1)}, f32[4,8,2176]{2,1,0:T(8,128)S(1)}, u32[]{:S(2)}, u32[]{:S(2)}) collective-permute-start(f32[4,8,2176]{2,1,0:T(8,128)S(1)} %pad_maximum_fusion.1), channel_id=1, source_target_pairs={{0,1},{1,0},{2,3},{3,2},{4,5},{5,4},{6,7},{7,6},{8,9},{9,8},{10,11... | collective-permute-start | bytes 835592 | tf_op jit(solution)/shard_map/ppermute | solution.py:70
  69.7 1.3 collective-permute-start.8
  71.0 3.8 %collective-permute-start.9 = (f32[2,24,128]{2,1,0:T(8,128)S(1)}, f32[2,24,128]{2,1,0:T(8,128)S(1)}, u32[]{:S(2)}, u32[]{:S(2)}) collective-permute-start(f32[2,24,128]{2,1,0:T(8,128)S(1)} %add.28), channel_id=1, source_target_pairs={{0,2},{2,0},{4,6},{6,4},{8,10},{10,8},{12,14},{14,12},{1,3},{3,1},... | collective-permute-start | bytes 73736 | tf_op jit(solution)/shard_map/ppermute | solution.py:60
  83.3 1.3 collective-permute-start.10
  84.5 3.8 %collective-permute-start.11 = (f32[2,24,128]{2,1,0:T(8,128)S(1)}, f32[2,24,128]{2,1,0:T(8,128)S(1)}, u32[]{:S(2)}, u32[]{:S(2)}) collective-permute-start(f32[2,24,128]{2,1,0:T(8,128)S(1)} %add.30), channel_id=1, source_target_pairs={{0,2},{2,0},{4,6},{6,4},{8,10},{10,8},{12,14},{14,12},{1,3},{3,1},... | collective-permute-start | bytes 73736 | tf_op jit(solution)/shard_map/ppermute | solution.py:60
  88.4 28.1 %copy-start.1 = (s32[4]{0:T(128)S(1)}, s32[4]{0:T(128)}, u32[]{:S(2)}) copy-start(s32[4]{0:T(128)} %own_bracket.1) | copy-start | bytes 52
  92.5 27.6 %collective-permute-start.13 = (f32[3,32,2048]{2,1,0:T(8,128)S(1)}, f32[3,32,2048]{2,1,0:T(8,128)S(1)}, u32[]{:S(2)}, u32[]{:S(2)}) collective-permute-start(f32[3,32,2048]{2,1,0:T(8,128)S(1)} %get-tuple-element.29), channel_id=1, source_target_pairs={{4,0},{6,2},{8,4},{10,6},{12,8},{14,10},{5,1},{7,3},{9,5},{11,7},{... | collective-permute-start | bytes 2359304 | tf_op jit(solution)/shard_map/ppermute | solution.py:386
  93.8 26.3 %collective-permute-start.12 = (f32[2,32,2048]{2,1,0:T(8,128)S(1)}, f32[2,32,2048]{2,1,0:T(8,128)S(1)}, u32[]{:S(2)}, u32[]{:S(2)}) collective-permute-start(f32[2,32,2048]{2,1,0:T(8,128)S(1)} %get-tuple-element.28), channel_id=1, source_target_pairs={{0,4},{2,6},{4,8},{6,10},{8,12},{10,14},{1,5},{3,7},{5,9},{7,11},{... | collective-permute-start | bytes 1572872 | tf_op jit(solution)/shard_map/ppermute | solution.py:385
  98.8 1.2 collective-permute-start.14
  100.1 3.6 %collective-permute-start.15 = (f32[8,128]{1,0:T(8,128)S(1)}, f32[8,128]{1,0:T(8,128)S(1)}, u32[]{:S(2)}, u32[]{:S(2)}) collective-permute-start(f32[8,128]{1,0:T(8,128)S(1)} %add.32), channel_id=1, source_target_pairs={{0,2},{2,0},{4,6},{6,4},{8,10},{10,8},{12,14},{14,12},{1,3},{3,1},... | collective-permute-start | bytes 12296 | tf_op jit(solution)/shard_map/ppermute | solution.py:60
  103.7 10.0 %collective-permute-start.16 = (f32[8,128]{1,0:T(8,128)S(1)}, f32[8,128]{1,0:T(8,128)S(1)}, u32[]{:S(2)}, u32[]{:S(2)}) collective-permute-start(f32[8,128]{1,0:T(8,128)S(1)} %add.33), channel_id=1, source_target_pairs={{0,4},{2,6},{4,0},{6,2},{8,12},{10,14},{12,8},{14,10},{1,5},{3,7},... | collective-permute-start | bytes 12296 | tf_op jit(solution)/shard_map/ppermute | solution.py:60
  113.7 4.5 %collective-permute-start.17 = (f32[8,128]{1,0:T(8,128)S(1)}, f32[8,128]{1,0:T(8,128)S(1)}, u32[]{:S(2)}, u32[]{:S(2)}) collective-permute-start(f32[8,128]{1,0:T(8,128)S(1)} %add.34), channel_id=1, source_target_pairs={{0,8},{2,10},{4,12},{6,14},{8,0},{10,2},{12,4},{14,6},{1,9},{3,11}... | collective-permute-start | bytes 12296 | tf_op jit(solution)/shard_map/ppermute | solution.py:60
  116.5 3.6 %collective-permute-start = (s32[4]{0:T(128)S(1)}, s32[4]{0:T(128)S(1)}, u32[]{:S(2)}, u32[]{:S(2)}) collective-permute-start(s32[4]{0:T(128)S(1)} %copy-done.1), channel_id=1, source_target_pairs={{0,2},{2,0},{4,6},{6,4},{8,10},{10,8},{12,14},{14,12},{1,3},{3,1},... | collective-permute-start | bytes 56 | tf_op jit(solution)/shard_map/ppermute | solution.py:46
  121.8 21.8 %collective-permute-start.18 = (f32[4,32,2048]{2,1,0:T(8,128)S(1)}, f32[4,32,2048]{2,1,0:T(8,128)S(1)}, u32[]{:S(2)}, u32[]{:S(2)}) collective-permute-start(f32[4,32,2048]{2,1,0:T(8,128)S(1)} %get-tuple-element.32), channel_id=1, source_target_pairs={{0,2},{2,0},{4,6},{6,4},{8,10},{10,8},{12,14},{14,12},{1,3},{3,1},... | collective-permute-start | bytes 3145736 | tf_op jit(solution)/shard_map/ppermute | solution.py:46

commit v2 on v1

--- a/solution.py
+++ b/solution.py
@@ -7,6 +7,7 @@
 from jax.experimental.pallas import tpu as pltpu
 from jax.sharding import PartitionSpec as P
 
+
 REACH = 2
 ITERS = 2
 TIME_STEP = 0.002
@@ -15,15 +16,17 @@
 LANES = 128
 SUBLANES = 8
 PAIR = 2
-LOW = 2 * ITERS + 1
-HIGH = 2 * ITERS
+LOW = 2 * ITERS + REACH
+HIGH = 2 * ITERS + REACH + 1
+FAR = 3
 EDGE = 2 * ITERS
-VMEM_LIMIT = 28 * 1024 * 1024
+CHUNKS = (0, 1, 2, 3)
+VMEM_LIMIT = 12 * 1024 * 1024
 
 F32 = jnp.float32
 
 
-def call(kernel, out_shapes, scratch=(), smem=0, operands=0, aliases=None):
+def call(kernel, out_shapes, scratch=(), smem=0, operands=0):
     specs = [pl.BlockSpec(memory_space=pltpu.SMEM)] * smem
     specs += [pl.BlockSpec(memory_space=pltpu.VMEM)] * operands
     return pl.pallas_call(
@@ -61,9 +64,10 @@
     return value
 
 
-def neighbour_rows(block):
+def neighbour_rows(blocks):
     size = lax.axis_size("space")
-    top, bottom = block[:, :EDGE], block[:, -EDGE:]
+    top = jnp.concatenate([block[:, :EDGE] for block in blocks], axis=0)
+    bottom = jnp.concatenate([block[:, -EDGE:] for block in blocks], axis=0)
     if size == 1:
         return jnp.concatenate([top, bottom], axis=1)
     if size == 2:
@@ -79,18 +83,21 @@
     half = columns // PAIR
     lane = lax.broadcasted_iota(jnp.int32, (x_ref.shape[1], LANES), 1)
 
-    def body(k, carry):
+    local = x_ref.shape[0]
+
+    def body(q, carry):
+        k = jnp.where(lo == 0, q, local - 1 - q)
         for ref, part in ((keep_ref, lo), (send_ref, 1 - lo)):
             begin = pl.multiple_of(part * half, LANES)
             right = pl.multiple_of((1 - part) * half, LANES)
             left = pl.multiple_of((1 - part) * half + half - LANES, LANES)
-            ref[k, :, 0:half] = x_ref[k, :, pl.ds(begin, half)]
-            ref[k, :, half:] = jnp.where(
+            ref[q, :, 0:half] = x_ref[k, :, pl.ds(begin, half)]
+            ref[q, :, half:] = jnp.where(
                 lane < LANES // 2, x_ref[k, :, pl.ds(right, LANES)], x_ref[k, :, pl.ds(left, LANES)]
             )
         return carry
 
-    lax.fori_loop(0, x_ref.shape[0], body, 0)
+    lax.fori_loop(0, local, body, 0)
 
 
 def sum_of_neighbours(load, tiles, rows, use):
@@ -200,37 +207,53 @@
     lax.fori_loop(low, high, body, 0)
 
 
-def start_kernel(*refs, count):
-    (keep, recv, near, far, extra_low, extra_high, keep_rows, recv_rows, near_rows, far_rows, extra_rows,
-     phi, drift, norms) = refs
+def start_kernel(*refs, count, splits):
+    refs = list(refs)
+    pick = lambda n: [refs.pop(0) for _ in range(n)]
+    keep, near_early, far_early = pick(3)
+    recv, near_late = pick(len(splits)), pick(len(splits))
+    far_late, far_last = pick(2)
+    rows_early, rows_late, phi, drift, norms = pick(5)
     local, rows, _ = keep.shape
     hi, lo = pair_position()
     first = hi * (PAIR * local) - LOW
-
-    def place(source, edge_rows, at, index):
-        phi[at, 0:rows, :] = source[index]
-        phi[at, rows:, :] = edge_rows[index]
-
-    def body(i, carry):
-        place(keep, keep_rows, LOW + lo * local + i, i)
-        place(recv, recv_rows, LOW + (1 - lo) * local + i, i)
-        low_at, high_at = LOW - local + i, LOW + PAIR * local + i
-        place(near, near_rows, jnp.where(lo == 1, low_at, high_at), i)
-        place(far, far_rows, jnp.where(lo == 1, high_at, low_at), i)
-        return carry
-
-    lax.fori_loop(0, local, body, 0)
-    for i in range(LOW - local):
+    top = LOW + PAIR * local
+
+    def place(at, image, edge_rows):
+        phi[at, 0:rows, :] = image
+        phi[at, rows:, :] = edge_rows
+
+    def own_at(part, q):
+        return LOW + part * local + jnp.where(part == 0, q, local - 1 - q)
+
+    for q in range(local):
+        chunk = max(c for c in range(len(splits)) if splits[c] <= q)
+        at = q - splits[chunk]
+        place(own_at(lo, q), keep[q], rows_early[q])
+        place(own_at(1 - lo, q), recv[chunk][at], rows_late[q])
+        low_at, high_at = LOW - 1 - q, top + q
+        place(jnp.where(lo == 1, low_at, high_at), near_early[q], rows_early[local + q])
+        place(jnp.where(lo == 1, high_at, low_at), near_late[chunk][at], rows_late[local + q])
+    for i in range(FAR):
+        low_at, high_at = LOW - 1 - local - i, top + local + i
+        late = far_late.at[1 - i] if i < 2 else far_last.at[0]
+        late_rows = rows_late.at[2 * local + i]
+        early, early_rows = far_early.at[FAR - 1 - i], rows_early.at[2 * local + i]
+
+        @pl.when(lo == 1)
+        def _():
+            if high_at < phi.shape[0]:
+                place(high_at, early[...], early_rows[...])
+            if low_at >= 0:
+                place(low_at, late[...], late_rows[...])
 
         @pl.when(lo == 0)
         def _():
-            phi[i, 0:rows, :] = extra_low[i]
-
-        @pl.when(lo == 1)
-        def _():
-            phi[i, 0:rows, :] = extra_high[i]
-
-        phi[i, rows:, :] = extra_rows[i]
+            if high_at < phi.shape[0]:
+                place(high_at, late[...], late_rows[...])
+            if low_at >= 0:
+                place(low_at, early[...], early_rows[...])
+
     norms[...] = jnp.zeros(norms.shape, F32)
     drift_pass(phi, drift, norms, 1, phi.shape[0] - 1, first, count, rows)
 
@@ -250,57 +273,43 @@
     drift_pass(new_phi, new_drift, new_norms, done + 3, window - done - 3, first, count, rows)
 
 
-def last_kernel(phi, drift, norms, own, down, up, squares, theta, speeds, final, *, count, local, rows, done):
+def last_kernel(phi, drift, norms, final, squares, theta, speeds, *, count, local, rows, done):
     hi, _ = pair_position()
     first = hi * (PAIR * local) - LOW
     window = phi.shape[0]
-    columns = own.shape[2]
+    tiles = final.shape[2] // LANES
+    shift = LOW - REACH
     speeds_of(norms, speeds)
     theta_pass(phi, drift, speeds, theta, done + 1, window - done - 1, first, count)
 
     def store(k, t, value):
-        if t < columns // LANES:
-            final[k, :, tile_of(t)] = value[0:rows]
-
-    update_pass(phi, speeds, theta, done + 2, window - done - 2, first, count, store)
+        if t < tiles:
+            final[k - shift, :, tile_of(t)] = value[0:rows]
+
+    update_pass(phi, speeds, theta, shift, shift + final.shape[0], first, count, store)
     position = (
         lax.broadcasted_iota(jnp.int32, squares.shape, 0) * LANES
         + lax.broadcasted_iota(jnp.int32, squares.shape, 1)
     )
 
     def body(i, total):
-        k = LOW + i
+        k = REACH + i
         acc = jnp.zeros((SUBLANES, LANES), F32)
-        for t in range(columns // LANES):
-            value = final[k, :, tile_of(t)]
-            own[i, :, tile_of(t)] = value
-            diff = value - final[k - 1, :, tile_of(t)]
+        for t in range(tiles):
+            diff = final[k, :, tile_of(t)] - final[k - 1, :, tile_of(t)]
             acc = acc + fold(diff * diff)
         amount = jnp.sum(jnp.sum(acc, axis=0, keepdims=True), axis=1, keepdims=True)
-        return total + jnp.where(position == k + first, amount, 0.0)
+        return total + jnp.where(position == LOW + i + first, amount, 0.0)
 
     squares[...] = lax.fori_loop(0, PAIR * local, body, jnp.zeros(squares.shape, F32))
-    for i in range(REACH + 1):
-        down[i] = final[LOW + i]
-    for i in range(REACH):
-        up[i] = final[LOW + PAIR * local - REACH + i]
-
-
-def combine_kernel(own_bracket, pair_bracket, own, low, high, squares, keep, send, window, *, count):
+
+
+def combine_kernel(bracket, window, squares, out, *, count, own):
     hi, lo = pair_position()
-    local = keep.shape[0]
-    tiles = own.shape[2] // LANES
+    part = lo if own else 1 - lo
+    local = out.shape[0]
+    tiles = out.shape[2] // LANES
     begin = hi * (PAIR * local)
-    for i in range(REACH):
-        window[i] = low[i]
-    for i in range(REACH + 1):
-        window[REACH + PAIR * local + i] = high[i]
-
-    def copy(i, carry):
-        window[REACH + i] = own[i]
-        return carry
-
-    lax.fori_loop(0, PAIR * local, copy, 0)
     position = (
         lax.broadcasted_iota(jnp.int32, squares.shape, 0) * LANES
         + lax.broadcasted_iota(jnp.int32, squares.shape, 1)
@@ -312,22 +321,19 @@
         return jnp.sum(jnp.sum(value, axis=0, keepdims=True), axis=1, keepdims=True)
 
     length = total(segments)
-    for bracket, part, out in ((own_bracket, lo, keep), (pair_bracket, 1 - lo, send)):
-
-        def body(i, carry):
-            b = bracket[i]
-            j = begin + part * local + i
-            arc = total(jnp.where(position <= b, segments, 0.0))
-            segment = total(jnp.where(position == b + 1, segments, 0.0))
-            target = length * lax.convert_element_type(j, F32) / F32(count - 1)
-            weight = (target - arc) / segment
-            at = b - begin + REACH
-            for t in range(tiles):
-                base = window[at, :, tile_of(t)]
-                out[i, :, tile_of(t)] = base + weight * (window[at + 1, :, tile_of(t)] - base)
-            return carry
-
-        lax.fori_loop(0, local, body, 0)
+    weights = []
+    for i in range(local):
+        b = bracket[i]
+        j = begin + part * local + i
+        arc = total(jnp.where(position <= b, segments, 0.0))
+        segment = total(jnp.where(position == b + 1, segments, 0.0))
+        target = length * lax.convert_element_type(j, F32) / F32(count - 1)
+        weights.append((target - arc) / segment)
+    for i in range(local):
+        at = bracket[i] - begin + REACH
+        for t in range(tiles):
+            base = window[at, :, tile_of(t)]
+            out[i, :, tile_of(t)] = base + weights[i] * (window[at + 1, :, tile_of(t)] - base)
 
 
 def per_device(path, bracket):
@@ -337,31 +343,39 @@
     half = columns // PAIR
     wide = half + LANES
     window = LOW + PAIR * local + HIGH
-    if devices & (devices - 1) or local != HIGH or count > SUBLANES * LANES or rows % SUBLANES:
+    if devices & (devices - 1) or local != 2 * ITERS or count > SUBLANES * LANES or rows % SUBLANES:
         raise ValueError("unsupported sizes")
     shape = functools.partial(jax.ShapeDtypeStruct, dtype=F32)
     block = shape((local, rows, wide))
+    ahead = [(i, i + PAIR) for i in range(devices - PAIR)]
+    back = [(target, source) for source, target in ahead]
+    move = lambda value, up, down: lax.ppermute(
+        value, "img",
+        [p for p in ahead if p[0] % PAIR in up] + [p for p in back if p[0] % PAIR in down],
+    )
     other_bracket = swap_pairs(bracket)
     keep, send = call(pack_kernel, (block, block), operands=1)(path)
-    recv = swap_pairs(send)
-    ahead = [(i, i + PAIR) for i in range(devices - PAIR)]
-    back = [(target, source) for source, target in ahead]
-    near = lax.ppermute(keep, "img", [p for p in ahead if p[0] % PAIR == 1] + [p for p in back if p[0] % PAIR == 0])
-    far = lax.ppermute(recv, "img", [p for p in ahead if p[0] % PAIR == 0] + [p for p in back if p[0] % PAIR == 1])
-    spare = LOW - local
-    extra_low = lax.ppermute(keep[-spare:], "img", [p for p in ahead if p[0] % PAIR == 0])
-    extra_high = lax.ppermute(recv[-spare:], "img", [p for p in ahead if p[0] % PAIR == 1])
-    keep_rows = neighbour_rows(keep)
-    late = neighbour_rows(jnp.concatenate([recv, near, far, extra_low + extra_high], axis=0))
-    recv_rows, near_rows, far_rows, extra_rows = (
-        late[:local], late[local : 2 * local], late[2 * local : 3 * local], late[3 * local :]
-    )
+    splits = CHUNKS
+    ends = splits[1:] + (local,)
+    recv = [swap_pairs(send[a:b]) for a, b in zip(splits, ends)]
+    near_early = move(keep, (1,), (0,))
+    far_early = move(keep[local - FAR :], (0,), (1,))
+    near_late = [move(value, (0,), (1,)) for value in recv]
+    images = jnp.concatenate(recv, axis=0)
+    far_last = move(images[local - FAR : local - 2], (), (0,))
+    far_late = move(images[local - 2 :], (1,), (0,))
+    flip = lambda value: jnp.concatenate([value[i : i + 1] for i in reversed(range(value.shape[0]))], axis=0)
+    rows_early = neighbour_rows([keep, near_early, flip(far_early)])
+    rows_late = neighbour_rows(recv + near_late + [flip(far_late), far_last])
     held = shape((window, rows + 2 * EDGE, wide))
     lines = -(-window // SUBLANES) * SUBLANES
     norm_shape = shape((2, lines, LANES))
-    phi, drift, norms = call(functools.partial(start_kernel, count=count), (held, held, norm_shape), operands=11)(
-        keep, recv, near, far, extra_low, extra_high, keep_rows, recv_rows, near_rows, far_rows, extra_rows
-    )
+    operands = [keep, near_early, far_early] + recv + near_late + [far_late, far_last, rows_early, rows_late]
+    phi, drift, norms = call(
+        functools.partial(start_kernel, count=count, splits=splits), (held, held, norm_shape),
+        operands=len(operands),
+    )(*operands)
+    other_bracket, norms = lax.optimization_barrier((other_bracket, norms))
     scratch = [pltpu.VMEM(held.shape, F32), pltpu.VMEM((lines, LANES), F32)]
     for iteration in range(ITERS - 1):
         norms = small_sum(norms, (1,))
@@ -370,11 +384,10 @@
             (held, held, norm_shape), scratch=scratch, operands=3,
         )(phi, drift, norms)
     norms = small_sum(norms, (1,))
-    half_block = lambda n: shape((n, rows, half))
-    own, down, up, squares = call(
+    final, squares = call(
         functools.partial(last_kernel, count=count, local=local, rows=rows, done=2 * (ITERS - 1)),
-        (half_block(PAIR * local), half_block(REACH + 1), half_block(REACH), shape((SUBLANES, LANES))),
-        scratch=scratch + [pltpu.VMEM((window, rows, half), F32)], operands=3,
+        (shape((PAIR * local + 2 * REACH + 1, rows, half)), shape((SUBLANES, LANES))),
+        scratch=scratch, operands=3,
     )(phi, drift, norms)
     steps = []
     step = 1
@@ -382,13 +395,11 @@
         steps.append(step)
         step *= 2
     squares = small_sum(squares, steps)
-    low = lax.ppermute(up, "img", ahead)
-    high = lax.ppermute(down, "img", back)
-    mine, theirs = call(
-        functools.partial(combine_kernel, count=count), (half_block(local), half_block(local)),
-        scratch=[pltpu.VMEM((PAIR * local + 2 * REACH + 1, rows, half), F32)], smem=2, operands=4,
-    )(bracket, other_bracket, own, low, high, squares)
-    other = swap_pairs(theirs)
+    combine = lambda chosen, own: call(
+        functools.partial(combine_kernel, count=count, own=own), shape((local, rows, half)), smem=1, operands=2
+    )(chosen, final, squares)
+    other = swap_pairs(combine(other_bracket, False))
+    mine = combine(bracket, True)
     is_low = lax.rem(lax.axis_index("img"), PAIR) == 0
     return jnp.concatenate([jnp.where(is_low, mine, other), jnp.where(is_low, other, mine)], axis=2)
 

time: 146 us -> 151 us (1.034)
  waiting for transfers between devices: 97.4 us -> 83.4 us
  starting transfers between devices: 24.9 us -> 36.1 us
  Pallas kernels: 19.1 us -> 25.1 us
    ppermute x6 -> x8, starting transfers between devices: 15.5 us -> 24.9 us  [per_device(): lax.ppermute(value, 'img', [p for p in ahead if p[0] % PAIR in up] + [p f...]
    ppermute x3 -> x6, waiting for transfers between devices: 46.6 us -> 38.6 us  [swap_pairs(): return lax.ppermute(value, 'img', [(i, i ^ 1) for i in range(count)])]
    ppermute x5, waiting for transfers between devices: 20.7 us -> 14.4 us  [small_sum(): lax.ppermute(value, 'img', [(i, i ^ step) for i in range(count)])]
    pallas_call x1, Pallas kernels: 8.43 us -> 11.1 us  [per_device(): call(functools.partial(middle_kernel, count=count, local=local, rows=rows...]
    pallas_call x2 -> x3, Pallas kernels: 6.41 us -> 8.39 us  [the longest x1 5.85 us: per_device(): call(functools.partial(start_kernel, count=count, splits=splits), (held,...]
    ppermute x3 -> x6, starting transfers between devices: 3.69 us -> 5.17 us  [swap_pairs(): return lax.ppermute(value, 'img', [(i, i ^ 1) for i in range(count)])]
    ppermute x6 -> x8, waiting for transfers between devices: 24.7 us -> 24.5 us  [per_device(): lax.ppermute(value, 'img', [p for p in ahead if p[0] % PAIR in up] + [p f...]
  transfers between devices with their start and end apart: 19 -> 24, of which waited for: 14 -> 18; matrix products, arithmetic and copies ran while one was open for 0% -> 1% of each run, Pallas kernels for 0% -> 4%
where the time goes in v2:
time: 151 us; the launch traced here: 150 us
  waiting for transfers between devices  83.4 us (55%)
  starting transfers between devices  36.1 us (24%)
  Pallas kernels  25.1 us (17%)
  other arithmetic  3.29 us (2%)
  local copies, waits for them, and re-layouts  2.12 us (1%)
    ppermute x6, waiting for transfers between devices, swap_pairs(): return lax.ppermute(value, 'img', [(i, i ^ 1) for i in range(count)])  38.6 us
    ppermute x8, starting transfers between devices, per_device(): lax.ppermute(value, 'img', [p for p in ahead if p[0] % PAIR in up] + [p f...  24.9 us
    ppermute x8, waiting for transfers between devices, per_device(): lax.ppermute(value, 'img', [p for p in ahead if p[0] % PAIR in up] + [p f...  24.5 us
    ppermute x5, waiting for transfers between devices, small_sum(): lax.ppermute(value, 'img', [(i, i ^ step) for i in range(count)])  14.4 us
    pallas_call x1, Pallas kernels, per_device(): call(functools.partial(middle_kernel, count=count, local=local, rows=rows...  11.1 us
    pallas_call x1, Pallas kernels, per_device(): call(functools.partial(start_kernel, count=count, splits=splits), (held,...  5.85 us
    pallas_call x1, Pallas kernels, per_device(): call(functools.partial(last_kernel, count=count, local=local, rows=rows,...  5.39 us
    ppermute x6, starting transfers between devices, swap_pairs(): return lax.ppermute(value, 'img', [(i, i ^ 1) for i in range(count)])  5.17 us
  transfers between devices with their start and end apart: 24, of which 18 were waited for; matrix products, arithmetic and copies ran while one was open for 1% of the time, Pallas kernels for 4%

profile of v2, /device:TPU:0, one launch (start us, length us, event | category | flops | bytes accessed | tf_op | source)
XLA Modules:
  0.0 150.2 jit_solution(15294646317116820715)
XLA Ops:
  0.0 1.6 %copy-done = f32[4,32,4096]{2,1,0:T(8,128)S(1)} copy-done((f32[4,32,4096]{2,1,0:T(8,128)S(1)}, f32[4,32,4096]{2,1,0:T(8,128)}, u32[]{:S(2)}) %copy-start) | copy-done | bytes 2097176
  1.8 3.1 %collective-permute-start.2 = (f32[1,32,2176]{2,1,0:T(8,128)S(1)}, f32[1,32,2176]{2,1,0:T(8,128)S(1)}, u32[]{:S(2)}, u32[]{:S(2)}) collective-permute-start(f32[1,32,2176]{2,1,0:T(8,128)S(1)} %get-tuple-element.38), channel_id=1, source_target_pairs={{0,2},{2,0},{4,6},{6,4},{8,10},{10,8},{12,14},{14,12},{1,3},{3,1},... | collective-permute-start | bytes 835592 | tf_op jit(solution)/shard_map/ppermute | solution.py:49
  5.0 1.9 %collective-permute-start.4 = (f32[1,32,2176]{2,1,0:T(8,128)S(1)}, f32[1,32,2176]{2,1,0:T(8,128)S(1)}, u32[]{:S(2)}, u32[]{:S(2)}) collective-permute-start(f32[1,32,2176]{2,1,0:T(8,128)S(1)} %get-tuple-element.36), channel_id=1, source_target_pairs={{0,2},{2,0},{4,6},{6,4},{8,10},{10,8},{12,14},{14,12},{1,3},{3,1},... | collective-permute-start | bytes 835592 | tf_op jit(solution)/shard_map/ppermute | solution.py:49
  7.0 1.3 collective-permute-start
  8.4 15.9 %collective-permute-done.4.refs_5_ = f32[1,32,2176]{2,1,0:T(8,128)S(1)} collective-permute-done((f32[1,32,2176]{2,1,0:T(8,128)S(1)}, f32[1,32,2176]{2,1,0:T(8,128)S(1)}, u32[]{:S(2)}, u32[]{:S(2)}) %collective-permute-start.4) | collective-permute-done | bytes 278560 | tf_op jit(solution)/shard_map/ppermute | solution.py:49
  24.4 4.0 %collective-permute-start.1 = (f32[3,32,2176]{2,1,0:T(8,128)S(1)}, f32[3,32,2176]{2,1,0:T(8,128)S(1)}, u32[]{:S(2)}, u32[]{:S(2)}) collective-permute-start(f32[3,32,2176]{2,1,0:T(8,128)S(1)} %slice.108), channel_id=1, source_target_pairs={{0,4},{4,8},{8,12},{6,2},{10,6},{14,10},{1,5},{5,9},{9,13},{7,3},{... | collective-permute-start | bytes 2506760 | tf_op jit(solution)/shard_map/ppermute | solution.py:352
  29.5 1.3 collective-permute-start.10
  30.8 4.6 %collective-permute-start.6 = (f32[1,32,2176]{2,1,0:T(8,128)S(1)}, f32[1,32,2176]{2,1,0:T(8,128)S(1)}, u32[]{:S(2)}, u32[]{:S(2)}) collective-permute-start(f32[1,32,2176]{2,1,0:T(8,128)S(1)} %collective-permute-done.2.refs_3_), channel_id=1, source_target_pairs={{0,4},{4,8},{8,12},{6,2},{10,6},{14,10},{1,5},{5,9},{9,13},{7,3},{... | collective-permute-start | bytes 835592 | tf_op jit(solution)/shard_map/ppermute | solution.py:352
  35.4 3.7 %collective-permute-start.7 = (f32[1,32,2176]{2,1,0:T(8,128)S(1)}, f32[1,32,2176]{2,1,0:T(8,128)S(1)}, u32[]{:S(2)}, u32[]{:S(2)}) collective-permute-start(f32[1,32,2176]{2,1,0:T(8,128)S(1)} %collective-permute-done.3.refs_4_), channel_id=1, source_target_pairs={{0,4},{4,8},{8,12},{6,2},{10,6},{14,10},{1,5},{5,9},{9,13},{7,3},{... | collective-permute-start | bytes 835592 | tf_op jit(solution)/shard_map/ppermute | solution.py:352
  39.2 14.0 %collective-permute-done.6.refs_7_ = f32[1,32,2176]{2,1,0:T(8,128)S(1)} collective-permute-done((f32[1,32,2176]{2,1,0:T(8,128)S(1)}, f32[1,32,2176]{2,1,0:T(8,128)S(1)}, u32[]{:S(2)}, u32[]{:S(2)}) %collective-permute-start.6) | collective-permute-done | bytes 278560 | tf_op jit(solution)/shard_map/ppermute | solution.py:352
  53.3 4.4 %collective-permute-start.8 = (f32[1,32,2176]{2,1,0:T(8,128)S(1)}, f32[1,32,2176]{2,1,0:T(8,128)S(1)}, u32[]{:S(2)}, u32[]{:S(2)}) collective-permute-start(f32[1,32,2176]{2,1,0:T(8,128)S(1)} %collective-permute-done.4.refs_5_), channel_id=1, source_target_pairs={{0,4},{4,8},{8,12},{6,2},{10,6},{14,10},{1,5},{5,9},{9,13},{7,3},{... | collective-permute-start | bytes 835592 | tf_op jit(solution)/shard_map/ppermute | solution.py:352
  57.7 1.5 %collective-permute-done.7.refs_8_ = f32[1,32,2176]{2,1,0:T(8,128)S(1)} collective-permute-done((f32[1,32,2176]{2,1,0:T(8,128)S(1)}, f32[1,32,2176]{2,1,0:T(8,128)S(1)}, u32[]{:S(2)}, u32[]{:S(2)}) %collective-permute-start.7) | collective-permute-done | bytes 278560 | tf_op jit(solution)/shard_map/ppermute | solution.py:352
  59.2 4.4 %collective-permute-start.9 = (f32[1,32,2176]{2,1,0:T(8,128)S(1)}, f32[1,32,2176]{2,1,0:T(8,128)S(1)}, u32[]{:S(2)}, u32[]{:S(2)}) collective-permute-start(f32[1,32,2176]{2,1,0:T(8,128)S(1)} %collective-permute-done.5.refs_6_), channel_id=1, source_target_pairs={{0,4},{4,8},{8,12},{6,2},{10,6},{14,10},{1,5},{5,9},{9,13},{7,3},{... | collective-permute-start | bytes 835592 | tf_op jit(solution)/shard_map/ppermute | solution.py:352
  63.7 1.4 collective-permute-done.8.refs_9_
  65.1 1.3 collective-permute-start.11
  66.4 1.7 %collective-permute-done.9.refs_10_ = f32[1,32,2176]{2,1,0:T(8,128)S(1)} collective-permute-done((f32[1,32,2176]{2,1,0:T(8,128)S(1)}, f32[1,32,2176]{2,1,0:T(8,128)S(1)}, u32[]{:S(2)}, u32[]{:S(2)}) %collective-permute-start.9) | collective-permute-done | bytes 278560 | tf_op jit(solution)/shard_map/ppermute | solution.py:352
  68.2 5.8 %collective-permute-done.11.refs_12_ = f32[1,32,2176]{2,1,0:T(8,128)S(1)} collective-permute-done((f32[1,32,2176]{2,1,0:T(8,128)S(1)}, f32[1,32,2176]{2,1,0:T(8,128)S(1)}, u32[]{:S(2)}, u32[]{:S(2)}) %collective-permute-start.11) | collective-permute-done | bytes 278560 | tf_op jit(solution)/shard_map/ppermute | solution.py:352
  75.1 1.4 collective-permute-done.13.refs_14_
  77.6 5.8 %shard_map.29 = (f32[21,40,2176]{2,1,0:T(8,128)S(1)}, f32[21,40,2176]{2,1,0:T(8,128)S(1)}, f32[2,24,128]{2,1,0:T(8,128)S(1)}) custom-call(f32[4,32,2176]{2,1,0:T(8,128)S(1)} %get-tuple-element.17.refs_0_, f32[4,32,2176]{2,1,0:T(8,128)S(1)} %collective-permute-done.refs_1_, f32[3,32,2176]{2,1,0:T(8,128)S(1)} %collective-permute-done.1.refs_2_, ...), custom_call_target="tpu_custom_call" | custom-call | tf_op jit(solution)/shard_map/pallas_call | solution.py:374
  84.7 3.8 %collective-permute-done.16 = f32[2,24,128]{2,1,0:T(8,128)S(1)} collective-permute-done((f32[2,24,128]{2,1,0:T(8,128)S(1)}, f32[2,24,128]{2,1,0:T(8,128)S(1)}, u32[]{:S(2)}, u32[]{:S(2)}) %collective-permute-start.16) | collective-permute-done | bytes 24608 | tf_op jit(solution)/shard_map/ppermute | solution.py:63
  88.5 11.1 %shard_map.30 = (f32[21,40,2176]{2,1,0:T(8,128)S(1)}, f32[21,40,2176]{2,1,0:T(8,128)S(1)}, f32[2,24,128]{2,1,0:T(8,128)S(1)}) custom-call(f32[21,40,2176]{2,1,0:T(8,128)S(1)} %get-tuple-element.19.phi, f32[21,40,2176]{2,1,0:T(8,128)S(1)} %get-tuple-element.20.drift, f32[2,24,128]{2,1,0:T(8,128)S(1)} %add.25.norms), custom_call_target="tpu_custom_call" | custom-call | tf_op jit(solution)/shard_map/pallas_call | solution.py:382
  100.9 3.8 %collective-permute-done.18 = f32[2,24,128]{2,1,0:T(8,128)S(1)} collective-permute-done((f32[2,24,128]{2,1,0:T(8,128)S(1)}, f32[2,24,128]{2,1,0:T(8,128)S(1)}, u32[]{:S(2)}, u32[]{:S(2)}) %collective-permute-start.18) | collective-permute-done | bytes 24608 | tf_op jit(solution)/shard_map/ppermute | solution.py:63
  104.8 5.4 %shard_map.31 = (f32[13,32,2048]{2,1,0:T(8,128)S(1)}, f32[8,128]{1,0:T(8,128)S(1)}) custom-call(f32[21,40,2176]{2,1,0:T(8,128)S(1)} %get-tuple-element.23.phi, f32[21,40,2176]{2,1,0:T(8,128)S(1)} %get-tuple-element.24.drift, f32[2,24,128]{2,1,0:T(8,128)S(1)} %add.27.norms), custom_call_target="tpu_custom_call" | custom-call | tf_op jit(solution)/shard_map/pallas_call | solution.py:387
  111.3 3.6 %collective-permute-done.20 = f32[8,128]{1,0:T(8,128)S(1)} collective-permute-done((f32[8,128]{1,0:T(8,128)S(1)}, f32[8,128]{1,0:T(8,128)S(1)}, u32[]{:S(2)}, u32[]{:S(2)}) %collective-permute-start.20) | collective-permute-done | bytes 4128 | tf_op jit(solution)/shard_map/ppermute | solution.py:63
  114.9 2.0 %collective-permute-start.21 = (f32[8,128]{1,0:T(8,128)S(1)}, f32[8,128]{1,0:T(8,128)S(1)}, u32[]{:S(2)}, u32[]{:S(2)}) collective-permute-start(f32[8,128]{1,0:T(8,128)S(1)} %add.29), channel_id=1, source_target_pairs={{0,4},{2,6},{4,0},{6,2},{8,12},{10,14},{12,8},{14,10},{1,5},{3,7},... | collective-permute-start | bytes 12296 | tf_op jit(solution)/shard_map/ppermute | solution.py:63
  117.0 1.6 %collective-permute-done.21 = f32[8,128]{1,0:T(8,128)S(1)} collective-permute-done((f32[8,128]{1,0:T(8,128)S(1)}, f32[8,128]{1,0:T(8,128)S(1)}, u32[]{:S(2)}, u32[]{:S(2)}) %collective-permute-start.21) | collective-permute-done | bytes 4128 | tf_op jit(solution)/shard_map/ppermute | solution.py:63
  118.6 3.0 %collective-permute-start.22 = (f32[8,128]{1,0:T(8,128)S(1)}, f32[8,128]{1,0:T(8,128)S(1)}, u32[]{:S(2)}, u32[]{:S(2)}) collective-permute-start(f32[8,128]{1,0:T(8,128)S(1)} %add.30), channel_id=1, source_target_pairs={{0,8},{2,10},{4,12},{6,14},{8,0},{10,2},{12,4},{14,6},{1,9},{3,11}... | collective-permute-start | bytes 12296 | tf_op jit(solution)/shard_map/ppermute | solution.py:63
  121.6 1.6 %collective-permute-done.22 = f32[8,128]{1,0:T(8,128)S(1)} collective-permute-done((f32[8,128]{1,0:T(8,128)S(1)}, f32[8,128]{1,0:T(8,128)S(1)}, u32[]{:S(2)}, u32[]{:S(2)}) %collective-permute-start.22) | collective-permute-done | bytes 4128 | tf_op jit(solution)/shard_map/ppermute | solution.py:63
  123.2 1.8 %shard_map.33 = f32[4,32,2048]{2,1,0:T(8,128)} custom-call(s32[4]{0:T(128)S(1)} %collective-permute-done.14.bracket, f32[13,32,2048]{2,1,0:T(8,128)S(1)} %get-tuple-element.26.window, f32[8,128]{1,0:T(8,128)S(1)} %add.31.squares), custom_call_target="tpu_custom_call" | custom-call | tf_op jit(solution)/shard_map/pallas_call | solution.py:398
  125.7 21.6 %collective-permute-done.23 = f32[4,32,2048]{2,1,0:T(8,128)} collective-permute-done((f32[4,32,2048]{2,1,0:T(8,128)}, f32[4,32,2048]{2,1,0:T(8,128)}, u32[]{:S(2)}, u32[]{:S(2)}) %collective-permute-start.23) | collective-permute-done | bytes 1048608 | tf_op jit(solution)/shard_map/ppermute | solution.py:49
  147.3 1.4 broadcast_select_fusion.1
  148.7 1.5 pad_maximum_fusion
  (55 shorter events, 8.5 us)
Async XLA Ops:
  0.0 1.6 %copy-start = (f32[4,32,4096]{2,1,0:T(8,128)S(1)}, f32[4,32,4096]{2,1,0:T(8,128)}, u32[]{:S(2)}) copy-start(f32[4,32,4096]{2,1,0:T(8,128)} %x_ref.1) | copy-start | bytes 6291460
  1.8 29.0 %collective-permute-start.2 = (f32[1,32,2176]{2,1,0:T(8,128)S(1)}, f32[1,32,2176]{2,1,0:T(8,128)S(1)}, u32[]{:S(2)}, u32[]{:S(2)}) collective-permute-start(f32[1,32,2176]{2,1,0:T(8,128)S(1)} %get-tuple-element.38), channel_id=1, source_target_pairs={{0,2},{2,0},{4,6},{6,4},{8,10},{10,8},{12,14},{14,12},{1,3},{3,1},... | collective-permute-start | bytes 835592 | tf_op jit(solution)/shard_map/ppermute | solution.py:49
  4.9 30.5 %collective-permute-start.3 = (f32[1,32,2176]{2,1,0:T(8,128)S(1)}, f32[1,32,2176]{2,1,0:T(8,128)S(1)}, u32[]{:S(2)}, u32[]{:S(2)}) collective-permute-start(f32[1,32,2176]{2,1,0:T(8,128)S(1)} %get-tuple-element.37), channel_id=1, source_target_pairs={{0,2},{2,0},{4,6},{6,4},{8,10},{10,8},{12,14},{14,12},{1,3},{3,1},... | collective-permute-start | bytes 835592 | tf_op jit(solution)/shard_map/ppermute | solution.py:49
  5.0 19.4 %collective-permute-start.4 = (f32[1,32,2176]{2,1,0:T(8,128)S(1)}, f32[1,32,2176]{2,1,0:T(8,128)S(1)}, u32[]{:S(2)}, u32[]{:S(2)}) collective-permute-start(f32[1,32,2176]{2,1,0:T(8,128)S(1)} %get-tuple-element.36), channel_id=1, source_target_pairs={{0,2},{2,0},{4,6},{6,4},{8,10},{10,8},{12,14},{14,12},{1,3},{3,1},... | collective-permute-start | bytes 835592 | tf_op jit(solution)/shard_map/ppermute | solution.py:49
  6.9 22.5 %collective-permute-start.5 = (f32[1,32,2176]{2,1,0:T(8,128)S(1)}, f32[1,32,2176]{2,1,0:T(8,128)S(1)}, u32[]{:S(2)}, u32[]{:S(2)}) collective-permute-start(f32[1,32,2176]{2,1,0:T(8,128)S(1)} %get-tuple-element.35), channel_id=1, source_target_pairs={{0,2},{2,0},{4,6},{6,4},{8,10},{10,8},{12,14},{14,12},{1,3},{3,1},... | collective-permute-start | bytes 835592 | tf_op jit(solution)/shard_map/ppermute | solution.py:49
  7.0 67.3 %collective-permute-start = (f32[4,32,2176]{2,1,0:T(8,128)S(1)}, f32[4,32,2176]{2,1,0:T(8,128)S(1)}, u32[]{:S(2)}, u32[]{:S(2)}) collective-permute-start(f32[4,32,2176]{2,1,0:T(8,128)S(1)} %get-tuple-element.17.refs_0_), channel_id=1, source_target_pairs={{2,6},{6,10},{10,14},{4,0},{8,4},{12,8},{3,7},{7,11},{11,15},{5,1}... | collective-permute-start | bytes 3342344 | tf_op jit(solution)/shard_map/ppermute | solution.py:352
  24.4 49.9 %collective-permute-start.1 = (f32[3,32,2176]{2,1,0:T(8,128)S(1)}, f32[3,32,2176]{2,1,0:T(8,128)S(1)}, u32[]{:S(2)}, u32[]{:S(2)}) collective-permute-start(f32[3,32,2176]{2,1,0:T(8,128)S(1)} %slice.108), channel_id=1, source_target_pairs={{0,4},{4,8},{8,12},{6,2},{10,6},{14,10},{1,5},{5,9},{9,13},{7,3},{... | collective-permute-start | bytes 2506760 | tf_op jit(solution)/shard_map/ppermute | solution.py:352
  29.5 38.6 %collective-permute-start.10 = (f32[2,32,2176]{2,1,0:T(8,128)S(1)}, f32[2,32,2176]{2,1,0:T(8,128)S(1)}, u32[]{:S(2)}, u32[]{:S(2)}) collective-permute-start(f32[2,32,2176]{2,1,0:T(8,128)S(1)} %pad_maximum_fusion.2), channel_id=1, source_target_pairs={{2,6},{6,10},{10,14},{4,0},{8,4},{12,8},{3,7},{7,11},{11,15},{5,1}... | collective-permute-start | bytes 1671176 | tf_op jit(solution)/shard_map/ppermute | solution.py:352
  30.8 22.4 %collective-permute-start.6 = (f32[1,32,2176]{2,1,0:T(8,128)S(1)}, f32[1,32,2176]{2,1,0:T(8,128)S(1)}, u32[]{:S(2)}, u32[]{:S(2)}) collective-permute-start(f32[1,32,2176]{2,1,0:T(8,128)S(1)} %collective-permute-done.2.refs_3_), channel_id=1, source_target_pairs={{0,4},{4,8},{8,12},{6,2},{10,6},{14,10},{1,5},{5,9},{9,13},{7,3},{... | collective-permute-start | bytes 835592 | tf_op jit(solution)/shard_map/ppermute | solution.py:352
  35.4 23.8 %collective-permute-start.7 = (f32[1,32,2176]{2,1,0:T(8,128)S(1)}, f32[1,32,2176]{2,1,0:T(8,128)S(1)}, u32[]{:S(2)}, u32[]{:S(2)}) collective-permute-start(f32[1,32,2176]{2,1,0:T(8,128)S(1)} %collective-permute-done.3.refs_4_), channel_id=1, source_target_pairs={{0,4},{4,8},{8,12},{6,2},{10,6},{14,10},{1,5},{5,9},{9,13},{7,3},{... | collective-permute-start | bytes 835592 | tf_op jit(solution)/shard_map/ppermute | solution.py:352
  53.3 11.8 %collective-permute-start.8 = (f32[1,32,2176]{2,1,0:T(8,128)S(1)}, f32[1,32,2176]{2,1,0:T(8,128)S(1)}, u32[]{:S(2)}, u32[]{:S(2)}) collective-permute-start(f32[1,32,2176]{2,1,0:T(8,128)S(1)} %collective-permute-done.4.refs_5_), channel_id=1, source_target_pairs={{0,4},{4,8},{8,12},{6,2},{10,6},{14,10},{1,5},{5,9},{9,13},{7,3},{... | collective-permute-start | bytes 835592 | tf_op jit(solution)/shard_map/ppermute | solution.py:352
  59.2 8.8 %collective-permute-start.9 = (f32[1,32,2176]{2,1,0:T(8,128)S(1)}, f32[1,32,2176]{2,1,0:T(8,128)S(1)}, u32[]{:S(2)}, u32[]{:S(2)}) collective-permute-start(f32[1,32,2176]{2,1,0:T(8,128)S(1)} %collective-permute-done.5.refs_6_), channel_id=1, source_target_pairs={{0,4},{4,8},{8,12},{6,2},{10,6},{14,10},{1,5},{5,9},{9,13},{7,3},{... | collective-permute-start | bytes 835592 | tf_op jit(solution)/shard_map/ppermute | solution.py:352
  65.1 8.9 %collective-permute-start.11 = (f32[1,32,2176]{2,1,0:T(8,128)S(1)}, f32[1,32,2176]{2,1,0:T(8,128)S(1)}, u32[]{:S(2)}, u32[]{:S(2)}) collective-permute-start(f32[1,32,2176]{2,1,0:T(8,128)S(1)} %collective-permute-done.3.refs_4_), channel_id=1, source_target_pairs={{4,0},{8,4},{12,8},{5,1},{9,5},{13,9},{20,16},{24,20},{28,24},{21,... | collective-permute-start | bytes 835592 | tf_op jit(solution)/shard_map/ppermute | solution.py:352
  74.2 0.9 copy-start.1
  74.2 2.3 %collective-permute-start.13 = (f32[11,8,2176]{2,1,0:T(8,128)S(1)}, f32[11,8,2176]{2,1,0:T(8,128)S(1)}, u32[]{:S(2)}, u32[]{:S(2)}) collective-permute-start(f32[11,8,2176]{2,1,0:T(8,128)S(1)} %pad_maximum_fusion.1), channel_id=1, source_target_pairs={{0,1},{1,0},{2,3},{3,2},{4,5},{5,4},{6,7},{7,6},{8,9},{9,8},{10,11... | collective-permute-start | bytes 2297864 | tf_op jit(solution)/shard_map/ppermute | solution.py:74
  74.5 3.0 %collective-permute-start.12 = (f32[11,8,2176]{2,1,0:T(8,128)S(1)}, f32[11,8,2176]{2,1,0:T(8,128)S(1)}, u32[]{:S(2)}, u32[]{:S(2)}) collective-permute-start(f32[11,8,2176]{2,1,0:T(8,128)S(1)} %fusion.1), channel_id=1, source_target_pairs={{0,1},{1,0},{2,3},{3,2},{4,5},{5,4},{6,7},{7,6},{8,9},{9,8},{10,11... | collective-permute-start | bytes 2297864 | tf_op jit(solution)/shard_map/ppermute | solution.py:74
  75.1 8.4 %collective-permute-start.14 = (s32[4]{0:T(128)S(1)}, s32[4]{0:T(128)S(1)}, u32[]{:S(2)}, u32[]{:S(2)}) collective-permute-start(s32[4]{0:T(128)S(1)} %copy-done.1), channel_id=1, source_target_pairs={{0,2},{2,0},{4,6},{6,4},{8,10},{10,8},{12,14},{14,12},{1,3},{3,1},... | collective-permute-start | bytes 56 | tf_op jit(solution)/shard_map/ppermute | solution.py:49
  83.4 1.3 collective-permute-start.15
  84.7 3.8 %collective-permute-start.16 = (f32[2,24,128]{2,1,0:T(8,128)S(1)}, f32[2,24,128]{2,1,0:T(8,128)S(1)}, u32[]{:S(2)}, u32[]{:S(2)}) collective-permute-start(f32[2,24,128]{2,1,0:T(8,128)S(1)} %add.24), channel_id=1, source_target_pairs={{0,2},{2,0},{4,6},{6,4},{8,10},{10,8},{12,14},{14,12},{1,3},{3,1},... | collective-permute-start | bytes 73736 | tf_op jit(solution)/shard_map/ppermute | solution.py:63
  99.7 1.3 collective-permute-start.17
  100.9 3.8 %collective-permute-start.18 = (f32[2,24,128]{2,1,0:T(8,128)S(1)}, f32[2,24,128]{2,1,0:T(8,128)S(1)}, u32[]{:S(2)}, u32[]{:S(2)}) collective-permute-start(f32[2,24,128]{2,1,0:T(8,128)S(1)} %add.26), channel_id=1, source_target_pairs={{0,2},{2,0},{4,6},{6,4},{8,10},{10,8},{12,14},{14,12},{1,3},{3,1},... | collective-permute-start | bytes 73736 | tf_op jit(solution)/shard_map/ppermute | solution.py:63
  110.2 1.2 collective-permute-start.19
  111.3 3.6 %collective-permute-start.20 = (f32[8,128]{1,0:T(8,128)S(1)}, f32[8,128]{1,0:T(8,128)S(1)}, u32[]{:S(2)}, u32[]{:S(2)}) collective-permute-start(f32[8,128]{1,0:T(8,128)S(1)} %add.28), channel_id=1, source_target_pairs={{0,2},{2,0},{4,6},{6,4},{8,10},{10,8},{12,14},{14,12},{1,3},{3,1},... | collective-permute-start | bytes 12296 | tf_op jit(solution)/shard_map/ppermute | solution.py:63
  114.9 3.6 %collective-permute-start.21 = (f32[8,128]{1,0:T(8,128)S(1)}, f32[8,128]{1,0:T(8,128)S(1)}, u32[]{:S(2)}, u32[]{:S(2)}) collective-permute-start(f32[8,128]{1,0:T(8,128)S(1)} %add.29), channel_id=1, source_target_pairs={{0,4},{2,6},{4,0},{6,2},{8,12},{10,14},{12,8},{14,10},{1,5},{3,7},... | collective-permute-start | bytes 12296 | tf_op jit(solution)/shard_map/ppermute | solution.py:63
  118.6 4.6 %collective-permute-start.22 = (f32[8,128]{1,0:T(8,128)S(1)}, f32[8,128]{1,0:T(8,128)S(1)}, u32[]{:S(2)}, u32[]{:S(2)}) collective-permute-start(f32[8,128]{1,0:T(8,128)S(1)} %add.30), channel_id=1, source_target_pairs={{0,8},{2,10},{4,12},{6,14},{8,0},{10,2},{12,4},{14,6},{1,9},{3,11}... | collective-permute-start | bytes 12296 | tf_op jit(solution)/shard_map/ppermute | solution.py:63
  124.9 22.4 %collective-permute-start.23 = (f32[4,32,2048]{2,1,0:T(8,128)}, f32[4,32,2048]{2,1,0:T(8,128)}, u32[]{:S(2)}, u32[]{:S(2)}) collective-permute-start(f32[4,32,2048]{2,1,0:T(8,128)} %shard_map.33), channel_id=1, source_target_pairs={{0,2},{2,0},{4,6},{6,4},{8,10},{10,8},{12,14},{14,12},{1,3},{3,1},... | collective-permute-start | bytes 3145736 | tf_op jit(solution)/shard_map/ppermute | solution.py:49

commit v3 on v2

--- a/solution.py
+++ b/solution.py
@@ -20,7 +20,7 @@
 HIGH = 2 * ITERS + REACH + 1
 FAR = 3
 EDGE = 2 * ITERS
-CHUNKS = (0, 1, 2, 3)
+CHUNKS = (0, 3)
 VMEM_LIMIT = 12 * 1024 * 1024
 
 F32 = jnp.float32
@@ -212,7 +212,7 @@
     pick = lambda n: [refs.pop(0) for _ in range(n)]
     keep, near_early, far_early = pick(3)
     recv, near_late = pick(len(splits)), pick(len(splits))
-    far_late, far_last = pick(2)
+    far_late = pick(len(splits))
     rows_early, rows_late, phi, drift, norms = pick(5)
     local, rows, _ = keep.shape
     hi, lo = pair_position()
@@ -223,11 +223,14 @@
         phi[at, 0:rows, :] = image
         phi[at, rows:, :] = edge_rows
 
+    def chunk_of(q):
+        return max(c for c in range(len(splits)) if splits[c] <= q)
+
     def own_at(part, q):
         return LOW + part * local + jnp.where(part == 0, q, local - 1 - q)
 
     for q in range(local):
-        chunk = max(c for c in range(len(splits)) if splits[c] <= q)
+        chunk = chunk_of(q)
         at = q - splits[chunk]
         place(own_at(lo, q), keep[q], rows_early[q])
         place(own_at(1 - lo, q), recv[chunk][at], rows_late[q])
@@ -236,7 +239,8 @@
         place(jnp.where(lo == 1, high_at, low_at), near_late[chunk][at], rows_late[local + q])
     for i in range(FAR):
         low_at, high_at = LOW - 1 - local - i, top + local + i
-        late = far_late.at[1 - i] if i < 2 else far_last.at[0]
+        q = local - 1 - i
+        late = far_late[chunk_of(q)].at[q - max(splits[chunk_of(q)], local - FAR)]
         late_rows = rows_late.at[2 * local + i]
         early, early_rows = far_early.at[FAR - 1 - i], rows_early.at[2 * local + i]
 
@@ -304,11 +308,12 @@
     squares[...] = lax.fori_loop(0, PAIR * local, body, jnp.zeros(squares.shape, F32))
 
 
-def combine_kernel(bracket, window, squares, out, *, count, own):
+def combine_kernel(bracket, window, squares, out, *scratch, count, own):
     hi, lo = pair_position()
     part = lo if own else 1 - lo
-    local = out.shape[0]
-    tiles = out.shape[2] // LANES
+    whole, out = out, scratch[0] if own else out
+    local, _, half = out.shape
+    tiles = half // LANES
     begin = hi * (PAIR * local)
     position = (
         lax.broadcasted_iota(jnp.int32, squares.shape, 0) * LANES
@@ -334,6 +339,20 @@
         for t in range(tiles):
             base = window[at, :, tile_of(t)]
             out[i, :, tile_of(t)] = base + weights[i] * (window[at + 1, :, tile_of(t)] - base)
+    if own:
+        copy_half(out, whole, lo, scratch[1])
+
+
+def copy_half(half_ref, whole, part, sem):
+    half = half_ref.shape[2]
+    copy = pltpu.make_async_copy(half_ref, whole.at[:, :, pl.ds(pl.multiple_of(part * half, LANES), half)], sem)
+    copy.start()
+    copy.wait()
+
+
+def finish_kernel(whole_in, other, whole, sem):
+    _, lo = pair_position()
+    copy_half(other, whole, 1 - lo, sem)
 
 
 def per_device(path, bracket):
@@ -361,16 +380,17 @@
     near_early = move(keep, (1,), (0,))
     far_early = move(keep[local - FAR :], (0,), (1,))
     near_late = [move(value, (0,), (1,)) for value in recv]
-    images = jnp.concatenate(recv, axis=0)
-    far_last = move(images[local - FAR : local - 2], (), (0,))
-    far_late = move(images[local - 2 :], (1,), (0,))
+    far_late = [
+        move(value[max(0, local - FAR - a) :], (1,), (0,))
+        for a, value in zip(splits, recv)
+    ]
     flip = lambda value: jnp.concatenate([value[i : i + 1] for i in reversed(range(value.shape[0]))], axis=0)
     rows_early = neighbour_rows([keep, near_early, flip(far_early)])
-    rows_late = neighbour_rows(recv + near_late + [flip(far_late), far_last])
+    rows_late = neighbour_rows(recv + near_late + [flip(value) for value in reversed(far_late)])
     held = shape((window, rows + 2 * EDGE, wide))
     lines = -(-window // SUBLANES) * SUBLANES
     norm_shape = shape((2, lines, LANES))
-    operands = [keep, near_early, far_early] + recv + near_late + [far_late, far_last, rows_early, rows_late]
+    operands = [keep, near_early, far_early] + recv + near_late + far_late + [rows_early, rows_late]
     phi, drift, norms = call(
         functools.partial(start_kernel, count=count, splits=splits), (held, held, norm_shape),
         operands=len(operands),
@@ -395,13 +415,31 @@
         steps.append(step)
         step *= 2
     squares = small_sum(squares, steps)
-    combine = lambda chosen, own: call(
-        functools.partial(combine_kernel, count=count, own=own), shape((local, rows, half)), smem=1, operands=2
-    )(chosen, final, squares)
-    other = swap_pairs(combine(other_bracket, False))
-    mine = combine(bracket, True)
-    is_low = lax.rem(lax.axis_index("img"), PAIR) == 0
-    return jnp.concatenate([jnp.where(is_low, mine, other), jnp.where(is_low, other, mine)], axis=2)
+    half_block = (local, rows, half)
+    whole = shape((local, rows, columns))
+    in_smem, in_vmem, in_hbm = (pl.BlockSpec(memory_space=m) for m in (pltpu.SMEM, pltpu.VMEM, pl.ANY))
+    other = swap_pairs(
+        call(functools.partial(combine_kernel, count=count, own=False), shape(half_block), smem=1, operands=2)(
+            other_bracket, final, squares
+        )
+    )
+    mine = pl.pallas_call(
+        functools.partial(combine_kernel, count=count, own=True),
+        out_shape=whole,
+        in_specs=[in_smem, in_vmem, in_vmem],
+        out_specs=in_hbm,
+        scratch_shapes=[pltpu.VMEM(half_block, F32), pltpu.SemaphoreType.DMA],
+        compiler_params=pltpu.CompilerParams(vmem_limit_bytes=VMEM_LIMIT),
+    )(bracket, final, squares)
+    return pl.pallas_call(
+        finish_kernel,
+        out_shape=whole,
+        in_specs=[in_hbm, in_vmem],
+        out_specs=in_hbm,
+        scratch_shapes=[pltpu.SemaphoreType.DMA],
+        input_output_aliases={0: 0},
+        compiler_params=pltpu.CompilerParams(vmem_limit_bytes=VMEM_LIMIT),
+    )(mine, other)
 
 
 def solution(mesh):

time: 151 us -> 132 us (0.87)
  waiting for transfers between devices: 83.4 us -> 65.7 us
  other arithmetic: 3.29 us -> 0.37 us
    ppermute x8 -> x6, waiting for transfers between devices: 24.5 us -> 16.5 us  [per_device(): lax.ppermute(value, 'img', [p for p in ahead if p[0] % PAIR in up] + [p f...]
    ppermute x8 -> x6, starting transfers between devices: 24.9 us -> 17.7 us  [per_device(): lax.ppermute(value, 'img', [p for p in ahead if p[0] % PAIR in up] + [p f...]
    ppermute x5, starting transfers between devices: 5.07 us -> 10.4 us  [small_sum(): lax.ppermute(value, 'img', [(i, i ^ step) for i in range(count)])]
    ppermute x5, waiting for transfers between devices: 14.4 us -> 9.13 us  [small_sum(): lax.ppermute(value, 'img', [(i, i ^ step) for i in range(count)])]
    ppermute x6 -> x4, starting transfers between devices: 5.17 us -> 8.8 us  [swap_pairs(): return lax.ppermute(value, 'img', [(i, i ^ 1) for i in range(count)])]
    ppermute x2, waiting for transfers between devices: 2.49 us -> 0.01 us  [neighbour_rows(): lax.ppermute(jnp.concatenate([top, bottom], axis=1), 'space', [(0, 1), (1...]
    ppermute x6 -> x4, waiting for transfers between devices: 38.6 us -> 36.7 us  [swap_pairs(): return lax.ppermute(value, 'img', [(i, i ^ 1) for i in range(count)])]
    pallas_call x2 -> x3, Pallas kernels: 2.54 us -> 3.52 us  [the longest x1 1.76 us: per_device(): pl.pallas_call(functools.partial(combine_kernel, count=count, own=True),...]
  transfers between devices with their start and end apart: 24 -> 20, of which waited for: 18 -> 12; matrix products, arithmetic and copies ran while one was open for 1% -> 1% of each run, Pallas kernels for 4% -> 6%
where the time goes in v3:
time: 132 us
  waiting for transfers between devices  65.7 us (50%)
  starting transfers between devices  37.3 us (28%)
  Pallas kernels  26 us (20%)
  local copies, waits for them, and re-layouts  2.12 us (2%)
    ppermute x4, waiting for transfers between devices, swap_pairs(): return lax.ppermute(value, 'img', [(i, i ^ 1) for i in range(count)])  36.7 us
    ppermute x6, starting transfers between devices, per_device(): lax.ppermute(value, 'img', [p for p in ahead if p[0] % PAIR in up] + [p f...  17.7 us
    ppermute x6, waiting for transfers between devices, per_device(): lax.ppermute(value, 'img', [p for p in ahead if p[0] % PAIR in up] + [p f...  16.5 us
    pallas_call x1, Pallas kernels, per_device(): call(functools.partial(middle_kernel, count=count, local=local, rows=rows...  11.1 us
    ppermute x5, starting transfers between devices, small_sum(): lax.ppermute(value, 'img', [(i, i ^ step) for i in range(count)])  10.4 us
    ppermute x5, waiting for transfers between devices, small_sum(): lax.ppermute(value, 'img', [(i, i ^ step) for i in range(count)])  9.13 us
    ppermute x4, starting transfers between devices, swap_pairs(): return lax.ppermute(value, 'img', [(i, i ^ 1) for i in range(count)])  8.8 us
    pallas_call x1, Pallas kernels, per_device(): call(functools.partial(start_kernel, count=count, splits=splits), (held,...  5.84 us
  transfers between devices with their start and end apart: 20, of which 12 were waited for; matrix products, arithmetic and copies ran while one was open for 1% of the time, Pallas kernels for 6%

profile of v3, /device:TPU:0, one launch (start us, length us, event | category | flops | bytes accessed | tf_op | source)
XLA Modules:
  0.0 131.8 jit_solution(2351466140774047092)
XLA Ops:
  0.0 1.6 %copy-done = f32[4,32,4096]{2,1,0:T(8,128)S(1)} copy-done((f32[4,32,4096]{2,1,0:T(8,128)S(1)}, f32[4,32,4096]{2,1,0:T(8,128)}, u32[]{:S(2)}) %copy-start) | copy-done | bytes 2097176
  1.8 3.1 %collective-permute-start.2 = (f32[3,32,2176]{2,1,0:T(8,128)S(1)}, f32[3,32,2176]{2,1,0:T(8,128)S(1)}, u32[]{:S(2)}, u32[]{:S(2)}) collective-permute-start(f32[3,32,2176]{2,1,0:T(8,128)S(1)} %slice.82), channel_id=1, source_target_pairs={{0,2},{2,0},{4,6},{6,4},{8,10},{10,8},{12,14},{14,12},{1,3},{3,1},... | collective-permute-start | bytes 2506760 | tf_op jit(solution)/shard_map/ppermute | solution.py:49
  5.0 1.3 collective-permute-start
  6.4 4.6 %collective-permute-start.1 = (f32[3,32,2176]{2,1,0:T(8,128)S(1)}, f32[3,32,2176]{2,1,0:T(8,128)S(1)}, u32[]{:S(2)}, u32[]{:S(2)}) collective-permute-start(f32[3,32,2176]{2,1,0:T(8,128)S(1)} %slice.81), channel_id=1, source_target_pairs={{0,4},{4,8},{8,12},{6,2},{10,6},{14,10},{1,5},{5,9},{9,13},{7,3},{... | collective-permute-start | bytes 2506760 | tf_op jit(solution)/shard_map/ppermute | solution.py:371
  11.1 18.4 %collective-permute-done.3.refs_4_ = f32[1,32,2176]{2,1,0:T(8,128)S(1)} collective-permute-done((f32[1,32,2176]{2,1,0:T(8,128)S(1)}, f32[1,32,2176]{2,1,0:T(8,128)S(1)}, u32[]{:S(2)}, u32[]{:S(2)}) %collective-permute-start.3) | collective-permute-done | bytes 278560 | tf_op jit(solution)/shard_map/ppermute | solution.py:49
  29.4 1.3 collective-permute-start.7
  30.7 4.6 %collective-permute-start.5 = (f32[1,32,2176]{2,1,0:T(8,128)S(1)}, f32[1,32,2176]{2,1,0:T(8,128)S(1)}, u32[]{:S(2)}, u32[]{:S(2)}) collective-permute-start(f32[1,32,2176]{2,1,0:T(8,128)S(1)} %collective-permute-done.3.refs_4_), channel_id=1, source_target_pairs={{0,4},{4,8},{8,12},{6,2},{10,6},{14,10},{1,5},{5,9},{9,13},{7,3},{... | collective-permute-start | bytes 835592 | tf_op jit(solution)/shard_map/ppermute | solution.py:371
  35.4 1.3 collective-permute-start.6
  36.8 4.6 %collective-permute-start.4 = (f32[3,32,2176]{2,1,0:T(8,128)S(1)}, f32[3,32,2176]{2,1,0:T(8,128)S(1)}, u32[]{:S(2)}, u32[]{:S(2)}) collective-permute-start(f32[3,32,2176]{2,1,0:T(8,128)S(1)} %collective-permute-done.2.refs_3_), channel_id=1, source_target_pairs={{0,4},{4,8},{8,12},{6,2},{10,6},{14,10},{1,5},{5,9},{9,13},{7,3},{... | collective-permute-start | bytes 2506760 | tf_op jit(solution)/shard_map/ppermute | solution.py:371
  41.7 9.4 %collective-permute-done.6.refs_7_ = f32[2,32,2176]{2,1,0:T(8,128)S(1)} collective-permute-done((f32[2,32,2176]{2,1,0:T(8,128)S(1)}, f32[2,32,2176]{2,1,0:T(8,128)S(1)}, u32[]{:S(2)}, u32[]{:S(2)}) %collective-permute-start.6) | collective-permute-done | bytes 557088 | tf_op jit(solution)/shard_map/ppermute | solution.py:371
  51.1 7.1 %collective-permute-done.4.refs_5_ = f32[3,32,2176]{2,1,0:T(8,128)S(1)} collective-permute-done((f32[3,32,2176]{2,1,0:T(8,128)S(1)}, f32[3,32,2176]{2,1,0:T(8,128)S(1)}, u32[]{:S(2)}, u32[]{:S(2)}) %collective-permute-start.4) | collective-permute-done | bytes 835616 | tf_op jit(solution)/shard_map/ppermute | solution.py:371
  58.7 3.6 %collective-permute-start.10 = (s32[4]{0:T(128)S(1)}, s32[4]{0:T(128)S(1)}, u32[]{:S(2)}, u32[]{:S(2)}) collective-permute-start(s32[4]{0:T(128)S(1)} %copy-done.1), channel_id=1, source_target_pairs={{0,2},{2,0},{4,6},{6,4},{8,10},{10,8},{12,14},{14,12},{1,3},{3,1},... | collective-permute-start | bytes 56 | tf_op jit(solution)/shard_map/ppermute | solution.py:49
  62.2 5.8 %shard_map.29 = (f32[21,40,2176]{2,1,0:T(8,128)S(1)}, f32[21,40,2176]{2,1,0:T(8,128)S(1)}, f32[2,24,128]{2,1,0:T(8,128)S(1)}) custom-call(f32[4,32,2176]{2,1,0:T(8,128)S(1)} %get-tuple-element.17.refs_0_, f32[4,32,2176]{2,1,0:T(8,128)S(1)} %collective-permute-done.refs_1_, f32[3,32,2176]{2,1,0:T(8,128)S(1)} %collective-permute-done.1.refs_2_, ...), custom_call_target="tpu_custom_call" | custom-call | tf_op jit(solution)/shard_map/pallas_call | solution.py:394
  68.3 1.1 collective-permute-done.11
  69.4 2.2 %collective-permute-start.12 = (f32[2,24,128]{2,1,0:T(8,128)S(1)}, f32[2,24,128]{2,1,0:T(8,128)S(1)}, u32[]{:S(2)}, u32[]{:S(2)}) collective-permute-start(f32[2,24,128]{2,1,0:T(8,128)S(1)} %add.24), channel_id=1, source_target_pairs={{0,2},{2,0},{4,6},{6,4},{8,10},{10,8},{12,14},{14,12},{1,3},{3,1},... | collective-permute-start | bytes 73736 | tf_op jit(solution)/shard_map/ppermute | solution.py:63
  71.5 1.8 %collective-permute-done.12 = f32[2,24,128]{2,1,0:T(8,128)S(1)} collective-permute-done((f32[2,24,128]{2,1,0:T(8,128)S(1)}, f32[2,24,128]{2,1,0:T(8,128)S(1)}, u32[]{:S(2)}, u32[]{:S(2)}) %collective-permute-start.12) | collective-permute-done | bytes 24608 | tf_op jit(solution)/shard_map/ppermute | solution.py:63
  73.3 11.1 %shard_map.30 = (f32[21,40,2176]{2,1,0:T(8,128)S(1)}, f32[21,40,2176]{2,1,0:T(8,128)S(1)}, f32[2,24,128]{2,1,0:T(8,128)S(1)}) custom-call(f32[21,40,2176]{2,1,0:T(8,128)S(1)} %get-tuple-element.19.phi, f32[21,40,2176]{2,1,0:T(8,128)S(1)} %get-tuple-element.20.drift, f32[2,24,128]{2,1,0:T(8,128)S(1)} %add.25.norms), custom_call_target="tpu_custom_call" | custom-call | tf_op jit(solution)/shard_map/pallas_call | solution.py:402
  84.6 1.2 collective-permute-done.13
  85.7 2.0 %collective-permute-start.14 = (f32[2,24,128]{2,1,0:T(8,128)S(1)}, f32[2,24,128]{2,1,0:T(8,128)S(1)}, u32[]{:S(2)}, u32[]{:S(2)}) collective-permute-start(f32[2,24,128]{2,1,0:T(8,128)S(1)} %add.26), channel_id=1, source_target_pairs={{0,2},{2,0},{4,6},{6,4},{8,10},{10,8},{12,14},{14,12},{1,3},{3,1},... | collective-permute-start | bytes 73736 | tf_op jit(solution)/shard_map/ppermute | solution.py:63
  87.8 1.8 %collective-permute-done.14 = f32[2,24,128]{2,1,0:T(8,128)S(1)} collective-permute-done((f32[2,24,128]{2,1,0:T(8,128)S(1)}, f32[2,24,128]{2,1,0:T(8,128)S(1)}, u32[]{:S(2)}, u32[]{:S(2)}) %collective-permute-start.14) | collective-permute-done | bytes 24608 | tf_op jit(solution)/shard_map/ppermute | solution.py:63
  89.6 5.4 %shard_map.31 = (f32[13,32,2048]{2,1,0:T(8,128)S(1)}, f32[8,128]{1,0:T(8,128)S(1)}) custom-call(f32[21,40,2176]{2,1,0:T(8,128)S(1)} %get-tuple-element.23.phi, f32[21,40,2176]{2,1,0:T(8,128)S(1)} %get-tuple-element.24.drift, f32[2,24,128]{2,1,0:T(8,128)S(1)} %add.27.norms), custom_call_target="tpu_custom_call" | custom-call | tf_op jit(solution)/shard_map/pallas_call | solution.py:407
  95.0 1.2 collective-permute-done.15
  96.1 2.0 %collective-permute-start.16 = (f32[8,128]{1,0:T(8,128)S(1)}, f32[8,128]{1,0:T(8,128)S(1)}, u32[]{:S(2)}, u32[]{:S(2)}) collective-permute-start(f32[8,128]{1,0:T(8,128)S(1)} %add.28), channel_id=1, source_target_pairs={{0,2},{2,0},{4,6},{6,4},{8,10},{10,8},{12,14},{14,12},{1,3},{3,1},... | collective-permute-start | bytes 12296 | tf_op jit(solution)/shard_map/ppermute | solution.py:63
  98.2 1.6 %collective-permute-done.16 = f32[8,128]{1,0:T(8,128)S(1)} collective-permute-done((f32[8,128]{1,0:T(8,128)S(1)}, f32[8,128]{1,0:T(8,128)S(1)}, u32[]{:S(2)}, u32[]{:S(2)}) %collective-permute-start.16) | collective-permute-done | bytes 4128 | tf_op jit(solution)/shard_map/ppermute | solution.py:63
  99.7 1.6 %collective-permute-start.17 = (f32[8,128]{1,0:T(8,128)S(1)}, f32[8,128]{1,0:T(8,128)S(1)}, u32[]{:S(2)}, u32[]{:S(2)}) collective-permute-start(f32[8,128]{1,0:T(8,128)S(1)} %add.29), channel_id=1, source_target_pairs={{0,4},{2,6},{4,0},{6,2},{8,12},{10,14},{12,8},{14,10},{1,5},{3,7},... | collective-permute-start | bytes 12296 | tf_op jit(solution)/shard_map/ppermute | solution.py:63
  101.3 2.0 %collective-permute-done.17 = f32[8,128]{1,0:T(8,128)S(1)} collective-permute-done((f32[8,128]{1,0:T(8,128)S(1)}, f32[8,128]{1,0:T(8,128)S(1)}, u32[]{:S(2)}, u32[]{:S(2)}) %collective-permute-start.17) | collective-permute-done | bytes 4128 | tf_op jit(solution)/shard_map/ppermute | solution.py:63
  103.4 2.6 %collective-permute-start.18 = (f32[8,128]{1,0:T(8,128)S(1)}, f32[8,128]{1,0:T(8,128)S(1)}, u32[]{:S(2)}, u32[]{:S(2)}) collective-permute-start(f32[8,128]{1,0:T(8,128)S(1)} %add.30), channel_id=1, source_target_pairs={{0,8},{2,10},{4,12},{6,14},{8,0},{10,2},{12,4},{14,6},{1,9},{3,11}... | collective-permute-start | bytes 12296 | tf_op jit(solution)/shard_map/ppermute | solution.py:63
  105.9 1.9 %collective-permute-done.18 = f32[8,128]{1,0:T(8,128)S(1)} collective-permute-done((f32[8,128]{1,0:T(8,128)S(1)}, f32[8,128]{1,0:T(8,128)S(1)}, u32[]{:S(2)}, u32[]{:S(2)}) %collective-permute-start.18) | collective-permute-done | bytes 4128 | tf_op jit(solution)/shard_map/ppermute | solution.py:63
  108.7 2.1 %collective-permute-start.19 = (f32[4,32,2048]{2,1,0:T(8,128)S(1)}, f32[4,32,2048]{2,1,0:T(8,128)S(1)}, u32[]{:S(2)}, u32[]{:S(2)}) collective-permute-start(f32[4,32,2048]{2,1,0:T(8,128)S(1)} %shard_map.33), channel_id=1, source_target_pairs={{0,2},{2,0},{4,6},{6,4},{8,10},{10,8},{12,14},{14,12},{1,3},{3,1},... | collective-permute-start | bytes 3145736 | tf_op jit(solution)/shard_map/ppermute | solution.py:49
  110.7 1.8 %shard_map.32.whole_in = f32[4,32,4096]{2,1,0:T(8,128)} custom-call(s32[4]{0:T(128)S(1)} %copy-done.1, f32[13,32,2048]{2,1,0:T(8,128)S(1)} %get-tuple-element.26.window, f32[8,128]{1,0:T(8,128)S(1)} %add.31.squares), custom_call_target="tpu_custom_call" | custom-call | tf_op jit(solution)/shard_map/pallas_call | solution.py:426
  112.5 18.3 %collective-permute-done.19.other = f32[4,32,2048]{2,1,0:T(8,128)S(1)} collective-permute-done((f32[4,32,2048]{2,1,0:T(8,128)S(1)}, f32[4,32,2048]{2,1,0:T(8,128)S(1)}, u32[]{:S(2)}, u32[]{:S(2)}) %collective-permute-start.19) | collective-permute-done | bytes 1048608 | tf_op jit(solution)/shard_map/ppermute | solution.py:49
  130.8 1.0 shard_map.34
  (43 shorter events, 2.4 us)
Async XLA Ops:
  0.0 1.6 %copy-start = (f32[4,32,4096]{2,1,0:T(8,128)S(1)}, f32[4,32,4096]{2,1,0:T(8,128)}, u32[]{:S(2)}) copy-start(f32[4,32,4096]{2,1,0:T(8,128)} %x_ref.1) | copy-start | bytes 6291460
  1.8 33.5 %collective-permute-start.2 = (f32[3,32,2176]{2,1,0:T(8,128)S(1)}, f32[3,32,2176]{2,1,0:T(8,128)S(1)}, u32[]{:S(2)}, u32[]{:S(2)}) collective-permute-start(f32[3,32,2176]{2,1,0:T(8,128)S(1)} %slice.82), channel_id=1, source_target_pairs={{0,2},{2,0},{4,6},{6,4},{8,10},{10,8},{12,14},{14,12},{1,3},{3,1},... | collective-permute-start | bytes 2506760 | tf_op jit(solution)/shard_map/ppermute | solution.py:49
  4.9 24.5 %collective-permute-start.3 = (f32[1,32,2176]{2,1,0:T(8,128)S(1)}, f32[1,32,2176]{2,1,0:T(8,128)S(1)}, u32[]{:S(2)}, u32[]{:S(2)}) collective-permute-start(f32[1,32,2176]{2,1,0:T(8,128)S(1)} %slice.83), channel_id=1, source_target_pairs={{0,2},{2,0},{4,6},{6,4},{8,10},{10,8},{12,14},{14,12},{1,3},{3,1},... | collective-permute-start | bytes 835592 | tf_op jit(solution)/shard_map/ppermute | solution.py:49
  5.0 36.4 %collective-permute-start = (f32[4,32,2176]{2,1,0:T(8,128)S(1)}, f32[4,32,2176]{2,1,0:T(8,128)S(1)}, u32[]{:S(2)}, u32[]{:S(2)}) collective-permute-start(f32[4,32,2176]{2,1,0:T(8,128)S(1)} %get-tuple-element.17.refs_0_), channel_id=1, source_target_pairs={{2,6},{6,10},{10,14},{4,0},{8,4},{12,8},{3,7},{7,11},{11,15},{5,1}... | collective-permute-start | bytes 3342344 | tf_op jit(solution)/shard_map/ppermute | solution.py:371
  6.4 30.4 %collective-permute-start.1 = (f32[3,32,2176]{2,1,0:T(8,128)S(1)}, f32[3,32,2176]{2,1,0:T(8,128)S(1)}, u32[]{:S(2)}, u32[]{:S(2)}) collective-permute-start(f32[3,32,2176]{2,1,0:T(8,128)S(1)} %slice.81), channel_id=1, source_target_pairs={{0,4},{4,8},{8,12},{6,2},{10,6},{14,10},{1,5},{5,9},{9,13},{7,3},{... | collective-permute-start | bytes 2506760 | tf_op jit(solution)/shard_map/ppermute | solution.py:371
  29.4 28.9 %collective-permute-start.7 = (f32[1,32,2176]{2,1,0:T(8,128)S(1)}, f32[1,32,2176]{2,1,0:T(8,128)S(1)}, u32[]{:S(2)}, u32[]{:S(2)}) collective-permute-start(f32[1,32,2176]{2,1,0:T(8,128)S(1)} %collective-permute-done.3.refs_4_), channel_id=1, source_target_pairs={{2,6},{6,10},{10,14},{4,0},{8,4},{12,8},{3,7},{7,11},{11,15},{5,1}... | collective-permute-start | bytes 835592 | tf_op jit(solution)/shard_map/ppermute | solution.py:371
  30.7 27.6 %collective-permute-start.5 = (f32[1,32,2176]{2,1,0:T(8,128)S(1)}, f32[1,32,2176]{2,1,0:T(8,128)S(1)}, u32[]{:S(2)}, u32[]{:S(2)}) collective-permute-start(f32[1,32,2176]{2,1,0:T(8,128)S(1)} %collective-permute-done.3.refs_4_), channel_id=1, source_target_pairs={{0,4},{4,8},{8,12},{6,2},{10,6},{14,10},{1,5},{5,9},{9,13},{7,3},{... | collective-permute-start | bytes 835592 | tf_op jit(solution)/shard_map/ppermute | solution.py:371
  35.4 15.7 %collective-permute-start.6 = (f32[2,32,2176]{2,1,0:T(8,128)S(1)}, f32[2,32,2176]{2,1,0:T(8,128)S(1)}, u32[]{:S(2)}, u32[]{:S(2)}) collective-permute-start(f32[2,32,2176]{2,1,0:T(8,128)S(1)} %slice.108), channel_id=1, source_target_pairs={{2,6},{6,10},{10,14},{4,0},{8,4},{12,8},{3,7},{7,11},{11,15},{5,1}... | collective-permute-start | bytes 1671176 | tf_op jit(solution)/shard_map/ppermute | solution.py:371
  36.8 21.5 %collective-permute-start.4 = (f32[3,32,2176]{2,1,0:T(8,128)S(1)}, f32[3,32,2176]{2,1,0:T(8,128)S(1)}, u32[]{:S(2)}, u32[]{:S(2)}) collective-permute-start(f32[3,32,2176]{2,1,0:T(8,128)S(1)} %collective-permute-done.2.refs_3_), channel_id=1, source_target_pairs={{0,4},{4,8},{8,12},{6,2},{10,6},{14,10},{1,5},{5,9},{9,13},{7,3},{... | collective-permute-start | bytes 2506760 | tf_op jit(solution)/shard_map/ppermute | solution.py:371
  41.6 17.0 %copy-start.1 = (s32[4]{0:T(128)S(1)}, s32[4]{0:T(128)}, u32[]{:S(2)}) copy-start(s32[4]{0:T(128)} %bracket.1) | copy-start | bytes 52
  41.7 20.6 %collective-permute-start.8 = (f32[11,8,2176]{2,1,0:T(8,128)S(1)}, f32[11,8,2176]{2,1,0:T(8,128)S(1)}, u32[]{:S(2)}, u32[]{:S(2)}) collective-permute-start(f32[11,8,2176]{2,1,0:T(8,128)S(1)} %fusion.1), channel_id=1, source_target_pairs={{0,1},{1,0},{2,3},{3,2},{4,5},{5,4},{6,7},{7,6},{8,9},{9,8},{10,11... | collective-permute-start | bytes 2297864 | tf_op jit(solution)/shard_map/ppermute | solution.py:74
  58.6 3.7 %collective-permute-start.9 = (f32[11,8,2176]{2,1,0:T(8,128)S(1)}, f32[11,8,2176]{2,1,0:T(8,128)S(1)}, u32[]{:S(2)}, u32[]{:S(2)}) collective-permute-start(f32[11,8,2176]{2,1,0:T(8,128)S(1)} %pad_maximum_fusion), channel_id=1, source_target_pairs={{0,1},{1,0},{2,3},{3,2},{4,5},{5,4},{6,7},{7,6},{8,9},{9,8},{10,11... | collective-permute-start | bytes 2297864 | tf_op jit(solution)/shard_map/ppermute | solution.py:74
  58.7 9.4 %collective-permute-start.10 = (s32[4]{0:T(128)S(1)}, s32[4]{0:T(128)S(1)}, u32[]{:S(2)}, u32[]{:S(2)}) collective-permute-start(s32[4]{0:T(128)S(1)} %copy-done.1), channel_id=1, source_target_pairs={{0,2},{2,0},{4,6},{6,4},{8,10},{10,8},{12,14},{14,12},{1,3},{3,1},... | collective-permute-start | bytes 56 | tf_op jit(solution)/shard_map/ppermute | solution.py:49
  68.1 1.3 collective-permute-start.11
  69.4 4.0 %collective-permute-start.12 = (f32[2,24,128]{2,1,0:T(8,128)S(1)}, f32[2,24,128]{2,1,0:T(8,128)S(1)}, u32[]{:S(2)}, u32[]{:S(2)}) collective-permute-start(f32[2,24,128]{2,1,0:T(8,128)S(1)} %add.24), channel_id=1, source_target_pairs={{0,2},{2,0},{4,6},{6,4},{8,10},{10,8},{12,14},{14,12},{1,3},{3,1},... | collective-permute-start | bytes 73736 | tf_op jit(solution)/shard_map/ppermute | solution.py:63
  84.5 1.3 collective-permute-start.13
  85.7 3.8 %collective-permute-start.14 = (f32[2,24,128]{2,1,0:T(8,128)S(1)}, f32[2,24,128]{2,1,0:T(8,128)S(1)}, u32[]{:S(2)}, u32[]{:S(2)}) collective-permute-start(f32[2,24,128]{2,1,0:T(8,128)S(1)} %add.26), channel_id=1, source_target_pairs={{0,2},{2,0},{4,6},{6,4},{8,10},{10,8},{12,14},{14,12},{1,3},{3,1},... | collective-permute-start | bytes 73736 | tf_op jit(solution)/shard_map/ppermute | solution.py:63
  95.0 1.2 collective-permute-start.15
  96.1 3.6 %collective-permute-start.16 = (f32[8,128]{1,0:T(8,128)S(1)}, f32[8,128]{1,0:T(8,128)S(1)}, u32[]{:S(2)}, u32[]{:S(2)}) collective-permute-start(f32[8,128]{1,0:T(8,128)S(1)} %add.28), channel_id=1, source_target_pairs={{0,2},{2,0},{4,6},{6,4},{8,10},{10,8},{12,14},{14,12},{1,3},{3,1},... | collective-permute-start | bytes 12296 | tf_op jit(solution)/shard_map/ppermute | solution.py:63
  99.7 3.6 %collective-permute-start.17 = (f32[8,128]{1,0:T(8,128)S(1)}, f32[8,128]{1,0:T(8,128)S(1)}, u32[]{:S(2)}, u32[]{:S(2)}) collective-permute-start(f32[8,128]{1,0:T(8,128)S(1)} %add.29), channel_id=1, source_target_pairs={{0,4},{2,6},{4,0},{6,2},{8,12},{10,14},{12,8},{14,10},{1,5},{3,7},... | collective-permute-start | bytes 12296 | tf_op jit(solution)/shard_map/ppermute | solution.py:63
  103.4 4.5 %collective-permute-start.18 = (f32[8,128]{1,0:T(8,128)S(1)}, f32[8,128]{1,0:T(8,128)S(1)}, u32[]{:S(2)}, u32[]{:S(2)}) collective-permute-start(f32[8,128]{1,0:T(8,128)S(1)} %add.30), channel_id=1, source_target_pairs={{0,8},{2,10},{4,12},{6,14},{8,0},{10,2},{12,4},{14,6},{1,9},{3,11}... | collective-permute-start | bytes 12296 | tf_op jit(solution)/shard_map/ppermute | solution.py:63
  108.7 22.1 %collective-permute-start.19 = (f32[4,32,2048]{2,1,0:T(8,128)S(1)}, f32[4,32,2048]{2,1,0:T(8,128)S(1)}, u32[]{:S(2)}, u32[]{:S(2)}) collective-permute-start(f32[4,32,2048]{2,1,0:T(8,128)S(1)} %shard_map.33), channel_id=1, source_target_pairs={{0,2},{2,0},{4,6},{6,4},{8,10},{10,8},{12,14},{14,12},{1,3},{3,1},... | collective-permute-start | bytes 3145736 | tf_op jit(solution)/shard_map/ppermute | solution.py:49

commit v4 on v3

--- a/solution.py
+++ b/solution.py
@@ -20,13 +20,13 @@
 HIGH = 2 * ITERS + REACH + 1
 FAR = 3
 EDGE = 2 * ITERS
-CHUNKS = (0, 3)
+CHUNKS = (0, 1, 3)
 VMEM_LIMIT = 12 * 1024 * 1024
 
 F32 = jnp.float32
 
 
-def call(kernel, out_shapes, scratch=(), smem=0, operands=0):
+def call(kernel, out_shapes, scratch=(), smem=0, operands=0, aliases=None):
     specs = [pl.BlockSpec(memory_space=pltpu.SMEM)] * smem
     specs += [pl.BlockSpec(memory_space=pltpu.VMEM)] * operands
     return pl.pallas_call(
@@ -35,6 +35,7 @@
         in_specs=specs,
         out_specs=jax.tree.map(lambda _: pl.BlockSpec(memory_space=pltpu.VMEM), out_shapes),
         scratch_shapes=list(scratch),
+        input_output_aliases=aliases or {},
         compiler_params=pltpu.CompilerParams(vmem_limit_bytes=VMEM_LIMIT),
     )
 
@@ -64,16 +65,28 @@
     return value
 
 
+def pick_kernel(*refs):
+    *blocks, picked = refs
+    at = 0
+    for block in blocks:
+        for i in range(block.shape[0]):
+            picked[at, 0:EDGE, :] = block[i, 0:EDGE, :]
+            picked[at, EDGE:, :] = block[i, block.shape[1] - EDGE :, :]
+            at += 1
+
+
 def neighbour_rows(blocks):
     size = lax.axis_size("space")
-    top = jnp.concatenate([block[:, :EDGE] for block in blocks], axis=0)
-    bottom = jnp.concatenate([block[:, -EDGE:] for block in blocks], axis=0)
+    count = sum(block.shape[0] for block in blocks)
+    picked = call(
+        pick_kernel, jax.ShapeDtypeStruct((count, 2 * EDGE, blocks[0].shape[2]), F32), operands=len(blocks)
+    )(*blocks)
     if size == 1:
-        return jnp.concatenate([top, bottom], axis=1)
+        return picked
     if size == 2:
-        return lax.ppermute(jnp.concatenate([top, bottom], axis=1), "space", [(0, 1), (1, 0)])
-    after = lax.ppermute(top, "space", [(i, (i - 1) % size) for i in range(size)])
-    before = lax.ppermute(bottom, "space", [(i, (i + 1) % size) for i in range(size)])
+        return lax.ppermute(picked, "space", [(0, 1), (1, 0)])
+    after = lax.ppermute(picked[:, :EDGE], "space", [(i, (i - 1) % size) for i in range(size)])
+    before = lax.ppermute(picked[:, EDGE:], "space", [(i, (i + 1) % size) for i in range(size)])
     return jnp.concatenate([after, before], axis=1)
 
 
@@ -135,7 +148,7 @@
     return jnp.sum(value.reshape(-1, SUBLANES, LANES), axis=0)
 
 
-def drift_pass(phi, drift, norms, low, high, first, count, own_rows):
+def drift_pass(phi, drift, norms, low, high, first, count, own_rows, shift=0):
     rows = phi.shape[1]
     tiles = phi.shape[2] // LANES
 
@@ -146,15 +159,16 @@
         def use(t, center, total):
             force = total - center * (3.0 + center * center)
             drift[k, :, tile_of(t)] = force
-            if t < tiles - 1:
+            if t < tiles - 1 and norms is not None:
                 step = phi[after, 0:own_rows, tile_of(t)] - phi[before, 0:own_rows, tile_of(t)]
                 own = force[0:own_rows]
                 sums[0] = sums[0] + fold(own * own)
                 sums[1] = sums[1] + fold(step * step)
 
         sum_of_neighbours(lambda t: phi[k, :, tile_of(t)], tiles, rows, use)
-        norms[0, pl.ds(k, 1), :] = jnp.sum(sums[0], axis=0, keepdims=True)
-        norms[1, pl.ds(k, 1), :] = jnp.sum(sums[1], axis=0, keepdims=True) * (stretch * stretch)
+        if norms is not None:
+            norms[0, pl.ds(k - shift, 1), :] = jnp.sum(sums[0], axis=0, keepdims=True)
+            norms[1, pl.ds(k - shift, 1), :] = jnp.sum(sums[1], axis=0, keepdims=True) * (stretch * stretch)
         return carry
 
     lax.fori_loop(low, high, body, 0)
@@ -207,59 +221,81 @@
     lax.fori_loop(low, high, body, 0)
 
 
-def start_kernel(*refs, count, splits):
+def chunk_of(q):
+    return max(c for c in range(len(CHUNKS)) if CHUNKS[c] <= q)
+
+
+def place(phi, at, image, edge_rows):
+    rows = image.shape[0]
+    phi[at, 0:rows, :] = image
+    phi[at, rows:, :] = edge_rows
+
+
+def inner_kernel(*refs, count):
     refs = list(refs)
     pick = lambda n: [refs.pop(0) for _ in range(n)]
-    keep, near_early, far_early = pick(3)
-    recv, near_late = pick(len(splits)), pick(len(splits))
-    far_late = pick(len(splits))
-    rows_early, rows_late, phi, drift, norms = pick(5)
+    (keep,), recv = pick(1), pick(len(CHUNKS))
+    near_early, near_late, edge_rows, phi, drift, norms = pick(6)
     local, rows, _ = keep.shape
     hi, lo = pair_position()
     first = hi * (PAIR * local) - LOW
     top = LOW + PAIR * local
 
-    def place(at, image, edge_rows):
-        phi[at, 0:rows, :] = image
-        phi[at, rows:, :] = edge_rows
-
-    def chunk_of(q):
-        return max(c for c in range(len(splits)) if splits[c] <= q)
-
     def own_at(part, q):
         return LOW + part * local + jnp.where(part == 0, q, local - 1 - q)
 
     for q in range(local):
-        chunk = chunk_of(q)
-        at = q - splits[chunk]
-        place(own_at(lo, q), keep[q], rows_early[q])
-        place(own_at(1 - lo, q), recv[chunk][at], rows_late[q])
+        place(phi, own_at(lo, q), keep[q], edge_rows[q])
+        place(phi, own_at(1 - lo, q), recv[chunk_of(q)][q - CHUNKS[chunk_of(q)]], edge_rows[local + q])
+    phi[jnp.where(lo == 1, LOW - 1, top), 0:rows, :] = near_early[0]
+    phi[jnp.where(lo == 1, top, LOW - 1), 0:rows, :] = near_late[0]
+    drift_pass(phi, drift, norms, LOW, top, first, count, rows, LOW)
+
+
+def outer_kernel(*refs, count):
+    refs = list(refs)
+    pick = lambda n: [refs.pop(0) for _ in range(n)]
+    _, _, near_early, far_early = pick(4)
+    near_late, far_late = pick(len(CHUNKS)), pick(len([c for c in range(len(CHUNKS)) if far_count(c)]))
+    rows_early, rows_late, phi, drift = pick(4)
+    local, rows, _ = near_early.shape
+    hi, lo = pair_position()
+    first = hi * (PAIR * local) - LOW
+    top = LOW + PAIR * local
+    skipped = len(CHUNKS) - len(far_late)
+    for q in range(local):
         low_at, high_at = LOW - 1 - q, top + q
-        place(jnp.where(lo == 1, low_at, high_at), near_early[q], rows_early[local + q])
-        place(jnp.where(lo == 1, high_at, low_at), near_late[chunk][at], rows_late[local + q])
+        place(phi, jnp.where(lo == 1, low_at, high_at), near_early[q], rows_early[PAIR * local + q])
+        late = near_late[chunk_of(q)][q - CHUNKS[chunk_of(q)]]
+        place(phi, jnp.where(lo == 1, high_at, low_at), late, rows_late[q])
     for i in range(FAR):
         low_at, high_at = LOW - 1 - local - i, top + local + i
         q = local - 1 - i
-        late = far_late[chunk_of(q)].at[q - max(splits[chunk_of(q)], local - FAR)]
-        late_rows = rows_late.at[2 * local + i]
-        early, early_rows = far_early.at[FAR - 1 - i], rows_early.at[2 * local + i]
+        late = far_late[chunk_of(q) - skipped].at[q - max(CHUNKS[chunk_of(q)], local - FAR)]
+        late_rows = rows_late.at[local + FAR - 1 - i]
+        early, early_rows = far_early.at[FAR - 1 - i], rows_early.at[(PAIR + 1) * local + FAR - 1 - i]
 
         @pl.when(lo == 1)
         def _():
             if high_at < phi.shape[0]:
-                place(high_at, early[...], early_rows[...])
+                place(phi, high_at, early[...], early_rows[...])
             if low_at >= 0:
-                place(low_at, late[...], late_rows[...])
+                place(phi, low_at, late[...], late_rows[...])
 
         @pl.when(lo == 0)
         def _():
             if high_at < phi.shape[0]:
-                place(high_at, late[...], late_rows[...])
+                place(phi, high_at, late[...], late_rows[...])
             if low_at >= 0:
-                place(low_at, early[...], early_rows[...])
-
-    norms[...] = jnp.zeros(norms.shape, F32)
-    drift_pass(phi, drift, norms, 1, phi.shape[0] - 1, first, count, rows)
+                place(phi, low_at, early[...], early_rows[...])
+
+    drift_pass(phi, drift, None, 1, LOW, first, count, rows)
+    drift_pass(phi, drift, None, top, phi.shape[0] - 1, first, count, rows)
+
+
+def far_count(chunk):
+    ends = CHUNKS[1:] + (CHUNKS[-1] + FAR,)
+    return max(0, ends[chunk] - max(CHUNKS[chunk], 2 * ITERS - FAR))
 
 
 def middle_kernel(phi, drift, norms, new_phi, new_drift, new_norms, theta, speeds, *, count, local, rows, done):
@@ -372,33 +408,40 @@
         value, "img",
         [p for p in ahead if p[0] % PAIR in up] + [p for p in back if p[0] % PAIR in down],
     )
+    keep, send = call(pack_kernel, (block, block), operands=1)(path)
+    ends = CHUNKS[1:] + (local,)
+    recv = [swap_pairs(send[a:b]) for a, b in zip(CHUNKS, ends)]
     other_bracket = swap_pairs(bracket)
-    keep, send = call(pack_kernel, (block, block), operands=1)(path)
-    splits = CHUNKS
-    ends = splits[1:] + (local,)
-    recv = [swap_pairs(send[a:b]) for a, b in zip(splits, ends)]
     near_early = move(keep, (1,), (0,))
     far_early = move(keep[local - FAR :], (0,), (1,))
     near_late = [move(value, (0,), (1,)) for value in recv]
     far_late = [
         move(value[max(0, local - FAR - a) :], (1,), (0,))
-        for a, value in zip(splits, recv)
+        for i, (a, value) in enumerate(zip(CHUNKS, recv)) if far_count(i)
     ]
-    flip = lambda value: jnp.concatenate([value[i : i + 1] for i in reversed(range(value.shape[0]))], axis=0)
-    rows_early = neighbour_rows([keep, near_early, flip(far_early)])
-    rows_late = neighbour_rows(recv + near_late + [flip(value) for value in reversed(far_late)])
+    rows_early = neighbour_rows([keep] + recv + [near_early, far_early])
+    rows_late = neighbour_rows(near_late + far_late)
     held = shape((window, rows + 2 * EDGE, wide))
     lines = -(-window // SUBLANES) * SUBLANES
     norm_shape = shape((2, lines, LANES))
-    operands = [keep, near_early, far_early] + recv + near_late + far_late + [rows_early, rows_late]
+    operands = [keep] + recv + [near_early, near_late[0], rows_early]
     phi, drift, norms = call(
-        functools.partial(start_kernel, count=count, splits=splits), (held, held, norm_shape),
+        functools.partial(inner_kernel, count=count), (held, held, shape((2, PAIR * local, LANES))),
         operands=len(operands),
     )(*operands)
-    other_bracket, norms = lax.optimization_barrier((other_bracket, norms))
+    norms = small_sum(norms, (1,))
+    low_norms = lax.ppermute(norms, "img", ahead)
+    high_norms = lax.ppermute(norms, "img", back)
+    operands = [phi, drift, near_early, far_early] + near_late + far_late + [rows_early, rows_late]
+    phi, drift = call(
+        functools.partial(outer_kernel, count=count), (held, held), operands=len(operands), aliases={0: 0, 1: 1}
+    )(*operands)
+    pad = jnp.zeros((2, lines - window, LANES), F32)
+    norms = jnp.concatenate([low_norms[:, PAIR * local - LOW :], norms, high_norms[:, :HIGH], pad], axis=1)
     scratch = [pltpu.VMEM(held.shape, F32), pltpu.VMEM((lines, LANES), F32)]
     for iteration in range(ITERS - 1):
-        norms = small_sum(norms, (1,))
+        if iteration:
+            norms = small_sum(norms, (1,))
         phi, drift, norms = call(
             functools.partial(middle_kernel, count=count, local=local, rows=rows, done=2 * iteration),
             (held, held, norm_shape), scratch=scratch, operands=3,

time: 132 us -> 139 us (1.053)
  starting transfers between devices: 37.3 us -> 44.1 us
    ppermute x2 -> x4, starting transfers between devices: 0.14 us -> 4.43 us  [the longest x1 3 us: per_device(): low_norms = lax.ppermute(norms, 'img', ahead)]
    ppermute x4 -> x5, starting transfers between devices: 8.8 us -> 11 us  [swap_pairs(): return lax.ppermute(value, 'img', [(i, i ^ 1) for i in range(count)])]
    ppermute x4 -> x5, waiting for transfers between devices: 36.7 us -> 38.4 us  [swap_pairs(): return lax.ppermute(value, 'img', [(i, i ^ 1) for i in range(count)])]
    ppermute x6 -> x7, waiting for transfers between devices: 16.5 us -> 15.1 us  [per_device(): lax.ppermute(value, 'img', [p for p in ahead if p[0] % PAIR in up] + [p f...]
    ppermute x6 -> x7, starting transfers between devices: 17.7 us -> 18.8 us  [per_device(): lax.ppermute(value, 'img', [p for p in ahead if p[0] % PAIR in up] + [p f...]
    pallas_call x1 -> x4, Pallas kernels: 5.84 us -> 5.95 us  [the longest x1 3.19 us: per_device(): call(functools.partial(outer_kernel, count=count), (held, held), operands...]
  transfers between devices with their start and end apart: 20 -> 24, of which waited for: 12 -> 14; matrix products, arithmetic and copies ran while one was open for 1% -> 0% of each run, Pallas kernels for 6% -> 5%
where the time goes in v4:
time: 139 us; the launch traced here: 138 us
  waiting for transfers between devices  65.8 us (47%)
  starting transfers between devices  44.1 us (32%)
  Pallas kernels  26.1 us (19%)
  local copies, waits for them, and re-layouts  1.81 us (1%)
    ppermute x5, waiting for transfers between devices, swap_pairs(): return lax.ppermute(value, 'img', [(i, i ^ 1) for i in range(count)])  38.4 us
    ppermute x7, starting transfers between devices, per_device(): lax.ppermute(value, 'img', [p for p in ahead if p[0] % PAIR in up] + [p f...  18.8 us
    ppermute x7, waiting for transfers between devices, per_device(): lax.ppermute(value, 'img', [p for p in ahead if p[0] % PAIR in up] + [p f...  15.1 us
    pallas_call x1, Pallas kernels, per_device(): call(functools.partial(middle_kernel, count=count, local=local, rows=rows...  11.1 us
    ppermute x5, starting transfers between devices, swap_pairs(): return lax.ppermute(value, 'img', [(i, i ^ 1) for i in range(count)])  11 us
    ppermute x5, starting transfers between devices, small_sum(): lax.ppermute(value, 'img', [(i, i ^ step) for i in range(count)])  9.29 us
    ppermute x5, waiting for transfers between devices, small_sum(): lax.ppermute(value, 'img', [(i, i ^ step) for i in range(count)])  8.16 us
    pallas_call x1, Pallas kernels, per_device(): call(functools.partial(last_kernel, count=count, local=local, rows=rows,...  5.38 us
  transfers between devices with their start and end apart: 24, of which 14 were waited for; matrix products, arithmetic and copies ran while one was open for 0% of the time, Pallas kernels for 5%

profile of v4, /device:TPU:0, one launch (start us, length us, event | category | flops | bytes accessed | tf_op | source)
XLA Modules:
  0.0 138.3 jit_solution(10131879083758521463)
XLA Ops:
  0.0 1.6 %copy-done = f32[4,32,4096]{2,1,0:T(8,128)S(1)} copy-done((f32[4,32,4096]{2,1,0:T(8,128)S(1)}, f32[4,32,4096]{2,1,0:T(8,128)}, u32[]{:S(2)}) %copy-start) | copy-done | bytes 2097176
  3.1 5.3 %collective-permute-start.1 = (f32[2,32,2176]{2,1,0:T(8,128)S(1)}, f32[2,32,2176]{2,1,0:T(8,128)S(1)}, u32[]{:S(2)}, u32[]{:S(2)}) collective-permute-start(f32[2,32,2176]{2,1,0:T(8,128)S(1)} %slice.19), channel_id=1, source_target_pairs={{0,2},{2,0},{4,6},{6,4},{8,10},{10,8},{12,14},{14,12},{1,3},{3,1},... | collective-permute-start | bytes 1671176 | tf_op jit(solution)/shard_map/ppermute | solution.py:50
  8.5 3.5 %collective-permute-start.5 = (f32[3,32,2176]{2,1,0:T(8,128)S(1)}, f32[3,32,2176]{2,1,0:T(8,128)S(1)}, u32[]{:S(2)}, u32[]{:S(2)}) collective-permute-start(f32[3,32,2176]{2,1,0:T(8,128)S(1)} %slice.21), channel_id=1, source_target_pairs={{0,4},{4,8},{8,12},{6,2},{10,6},{14,10},{1,5},{5,9},{9,13},{7,3},{... | collective-permute-start | bytes 2506760 | tf_op jit(solution)/shard_map/ppermute | solution.py:407
  12.1 2.0 %collective-permute-start.2 = (f32[1,32,2176]{2,1,0:T(8,128)S(1)}, f32[1,32,2176]{2,1,0:T(8,128)S(1)}, u32[]{:S(2)}, u32[]{:S(2)}) collective-permute-start(f32[1,32,2176]{2,1,0:T(8,128)S(1)} %get-tuple-element.29), channel_id=1, source_target_pairs={{0,2},{2,0},{4,6},{6,4},{8,10},{10,8},{12,14},{14,12},{1,3},{3,1},... | collective-permute-start | bytes 835592 | tf_op jit(solution)/shard_map/ppermute | solution.py:50
  14.1 13.8 %collective-permute-done.refs_1_ = f32[1,32,2176]{2,1,0:T(8,128)S(1)} collective-permute-done((f32[1,32,2176]{2,1,0:T(8,128)S(1)}, f32[1,32,2176]{2,1,0:T(8,128)S(1)}, u32[]{:S(2)}, u32[]{:S(2)}) %collective-permute-start) | collective-permute-done | bytes 278560 | tf_op jit(solution)/shard_map/ppermute | solution.py:50
  27.9 4.8 %collective-permute-done.2.refs_3_ = f32[1,32,2176]{2,1,0:T(8,128)S(1)} collective-permute-done((f32[1,32,2176]{2,1,0:T(8,128)S(1)}, f32[1,32,2176]{2,1,0:T(8,128)S(1)}, u32[]{:S(2)}, u32[]{:S(2)}) %collective-permute-start.2) | collective-permute-done | bytes 278560 | tf_op jit(solution)/shard_map/ppermute | solution.py:50
  33.0 3.4 %collective-permute-start.4 = (f32[1,32,2176]{2,1,0:T(8,128)S(1)}, f32[1,32,2176]{2,1,0:T(8,128)S(1)}, u32[]{:S(2)}, u32[]{:S(2)}) collective-permute-start(f32[1,32,2176]{2,1,0:T(8,128)S(1)} %collective-permute-done.refs_1_), channel_id=1, source_target_pairs={{0,4},{4,8},{8,12},{6,2},{10,6},{14,10},{1,5},{5,9},{9,13},{7,3},{... | collective-permute-start | bytes 835592 | tf_op jit(solution)/shard_map/ppermute | solution.py:407
  36.4 3.5 %collective-permute-start.7 = (f32[2,32,2176]{2,1,0:T(8,128)S(1)}, f32[2,32,2176]{2,1,0:T(8,128)S(1)}, u32[]{:S(2)}, u32[]{:S(2)}) collective-permute-start(f32[2,32,2176]{2,1,0:T(8,128)S(1)} %collective-permute-done.1.refs_2_), channel_id=1, source_target_pairs={{0,4},{4,8},{8,12},{6,2},{10,6},{14,10},{1,5},{5,9},{9,13},{7,3},{... | collective-permute-start | bytes 1671176 | tf_op jit(solution)/shard_map/ppermute | solution.py:407
  39.9 1.3 collective-permute-start.9
  41.2 4.6 %collective-permute-start.8 = (f32[1,32,2176]{2,1,0:T(8,128)S(1)}, f32[1,32,2176]{2,1,0:T(8,128)S(1)}, u32[]{:S(2)}, u32[]{:S(2)}) collective-permute-start(f32[1,32,2176]{2,1,0:T(8,128)S(1)} %collective-permute-done.2.refs_3_), channel_id=1, source_target_pairs={{0,4},{4,8},{8,12},{6,2},{10,6},{14,10},{1,5},{5,9},{9,13},{7,3},{... | collective-permute-start | bytes 835592 | tf_op jit(solution)/shard_map/ppermute | solution.py:407
  45.8 1.3 collective-permute-start.10
  47.1 13.7 %collective-permute-done.8.refs_2_.refs_6_ = f32[1,32,2176]{2,1,0:T(8,128)S(1)} collective-permute-done((f32[1,32,2176]{2,1,0:T(8,128)S(1)}, f32[1,32,2176]{2,1,0:T(8,128)S(1)}, u32[]{:S(2)}, u32[]{:S(2)}) %collective-permute-start.8) | collective-permute-done | bytes 278560 | tf_op jit(solution)/shard_map/ppermute | solution.py:407
  60.9 1.4 %collective-permute-done.10.refs_4_.refs_8_ = f32[1,32,2176]{2,1,0:T(8,128)S(1)} collective-permute-done((f32[1,32,2176]{2,1,0:T(8,128)S(1)}, f32[1,32,2176]{2,1,0:T(8,128)S(1)}, u32[]{:S(2)}, u32[]{:S(2)}) %collective-permute-start.10) | collective-permute-done | bytes 278560 | tf_op jit(solution)/shard_map/ppermute | solution.py:407
  62.4 2.5 %shard_map.30 = (f32[21,40,2176]{2,1,0:T(8,128)S(1)}, f32[21,40,2176]{2,1,0:T(8,128)S(1)}, f32[2,8,128]{2,1,0:T(8,128)S(1)}) custom-call(f32[4,32,2176]{2,1,0:T(8,128)S(1)} %get-tuple-element.17.refs_0_, f32[1,32,2176]{2,1,0:T(8,128)S(1)} %collective-permute-done.refs_1_, f32[2,32,2176]{2,1,0:T(8,128)S(1)} %collective-permute-done.1.refs_2_, ...), custom_call_target="tpu_custom_call" | custom-call | tf_op jit(solution)/shard_map/pallas_call | solution.py:428
  66.3 1.3 collective-permute-start.13
  67.7 2.3 %collective-permute-done.13 = f32[2,8,128]{2,1,0:T(8,128)S(1)} collective-permute-done((f32[2,8,128]{2,1,0:T(8,128)S(1)}, f32[2,8,128]{2,1,0:T(8,128)S(1)}, u32[]{:S(2)}, u32[]{:S(2)}) %collective-permute-start.13) | collective-permute-done | bytes 8224 | tf_op jit(solution)/shard_map/ppermute | solution.py:64
  70.0 3.0 %collective-permute-start.14 = (f32[2,8,128]{2,1,0:T(8,128)S(1)}, f32[2,8,128]{2,1,0:T(8,128)S(1)}, u32[]{:S(2)}, u32[]{:S(2)}) collective-permute-start(f32[2,8,128]{2,1,0:T(8,128)S(1)} %add.25), channel_id=1, source_target_pairs={{0,4},{2,6},{4,8},{6,10},{8,12},{10,14},{1,5},{3,7},{5,9},{7,11},{... | collective-permute-start | bytes 24584 | tf_op jit(solution)/shard_map/ppermute | solution.py:433
  74.4 3.2 %shard_map.32 = (f32[21,40,2176]{2,1,0:T(8,128)S(1)}, f32[21,40,2176]{2,1,0:T(8,128)S(1)}) custom-call(f32[21,40,2176]{2,1,0:T(8,128)S(1)} %get-tuple-element.19.refs_0_, f32[21,40,2176]{2,1,0:T(8,128)S(1)} %get-tuple-element.20.refs_1_, f32[4,32,2176]{2,1,0:T(8,128)S(1)} %collective-permute-done.3.refs_4_.refs_2_, ...), custom_call_target="tpu_custom_call", output_to_operand_aliasing={{0}: (0, {}), {1}: (1, {})} | custom-call | tf_op jit(solution)/shard_map/pallas_call | solution.py:436
  78.6 11.1 %shard_map.33 = (f32[21,40,2176]{2,1,0:T(8,128)S(1)}, f32[21,40,2176]{2,1,0:T(8,128)S(1)}, f32[2,24,128]{2,1,0:T(8,128)S(1)}) custom-call(f32[21,40,2176]{2,1,0:T(8,128)S(1)} %get-tuple-element.21.phi, f32[21,40,2176]{2,1,0:T(8,128)S(1)} %get-tuple-element.22.drift, f32[2,24,128]{2,1,0:T(8,128)S(1)} %maximum_maximum_fusion.norms), custom_call_target="tpu_custom_call" | custom-call | tf_op jit(solution)/shard_map/pallas_call | solution.py:445
  91.0 1.7 %collective-permute-start.17 = (f32[2,24,128]{2,1,0:T(8,128)S(1)}, f32[2,24,128]{2,1,0:T(8,128)S(1)}, u32[]{:S(2)}, u32[]{:S(2)}) collective-permute-start(f32[2,24,128]{2,1,0:T(8,128)S(1)} %add.26), channel_id=1, source_target_pairs={{0,2},{2,0},{4,6},{6,4},{8,10},{10,8},{12,14},{14,12},{1,3},{3,1},... | collective-permute-start | bytes 73736 | tf_op jit(solution)/shard_map/ppermute | solution.py:64
  92.7 2.1 %collective-permute-done.17 = f32[2,24,128]{2,1,0:T(8,128)S(1)} collective-permute-done((f32[2,24,128]{2,1,0:T(8,128)S(1)}, f32[2,24,128]{2,1,0:T(8,128)S(1)}, u32[]{:S(2)}, u32[]{:S(2)}) %collective-permute-start.17) | collective-permute-done | bytes 24608 | tf_op jit(solution)/shard_map/ppermute | solution.py:64
  94.8 5.4 %shard_map.34 = (f32[13,32,2048]{2,1,0:T(8,128)S(1)}, f32[8,128]{1,0:T(8,128)S(1)}) custom-call(f32[21,40,2176]{2,1,0:T(8,128)S(1)} %get-tuple-element.24.phi, f32[21,40,2176]{2,1,0:T(8,128)S(1)} %get-tuple-element.25.drift, f32[2,24,128]{2,1,0:T(8,128)S(1)} %add.27.norms), custom_call_target="tpu_custom_call" | custom-call | tf_op jit(solution)/shard_map/pallas_call | solution.py:450
  101.4 1.7 %collective-permute-start.19 = (f32[8,128]{1,0:T(8,128)S(1)}, f32[8,128]{1,0:T(8,128)S(1)}, u32[]{:S(2)}, u32[]{:S(2)}) collective-permute-start(f32[8,128]{1,0:T(8,128)S(1)} %add.28), channel_id=1, source_target_pairs={{0,2},{2,0},{4,6},{6,4},{8,10},{10,8},{12,14},{14,12},{1,3},{3,1},... | collective-permute-start | bytes 12296 | tf_op jit(solution)/shard_map/ppermute | solution.py:64
  103.1 1.9 %collective-permute-done.19 = f32[8,128]{1,0:T(8,128)S(1)} collective-permute-done((f32[8,128]{1,0:T(8,128)S(1)}, f32[8,128]{1,0:T(8,128)S(1)}, u32[]{:S(2)}, u32[]{:S(2)}) %collective-permute-start.19) | collective-permute-done | bytes 4128 | tf_op jit(solution)/shard_map/ppermute | solution.py:64
  105.0 1.7 %collective-permute-start.20 = (f32[8,128]{1,0:T(8,128)S(1)}, f32[8,128]{1,0:T(8,128)S(1)}, u32[]{:S(2)}, u32[]{:S(2)}) collective-permute-start(f32[8,128]{1,0:T(8,128)S(1)} %add.29), channel_id=1, source_target_pairs={{0,4},{2,6},{4,0},{6,2},{8,12},{10,14},{12,8},{14,10},{1,5},{3,7},... | collective-permute-start | bytes 12296 | tf_op jit(solution)/shard_map/ppermute | solution.py:64
  106.7 1.9 %collective-permute-done.20 = f32[8,128]{1,0:T(8,128)S(1)} collective-permute-done((f32[8,128]{1,0:T(8,128)S(1)}, f32[8,128]{1,0:T(8,128)S(1)}, u32[]{:S(2)}, u32[]{:S(2)}) %collective-permute-start.20) | collective-permute-done | bytes 4128 | tf_op jit(solution)/shard_map/ppermute | solution.py:64
  108.6 2.8 %collective-permute-start.21 = (f32[8,128]{1,0:T(8,128)S(1)}, f32[8,128]{1,0:T(8,128)S(1)}, u32[]{:S(2)}, u32[]{:S(2)}) collective-permute-start(f32[8,128]{1,0:T(8,128)S(1)} %add.30), channel_id=1, source_target_pairs={{0,8},{2,10},{4,12},{6,14},{8,0},{10,2},{12,4},{14,6},{1,9},{3,11}... | collective-permute-start | bytes 12296 | tf_op jit(solution)/shard_map/ppermute | solution.py:64
  111.4 1.7 %collective-permute-start.22 = (s32[4]{0:T(128)S(1)}, s32[4]{0:T(128)S(1)}, u32[]{:S(2)}, u32[]{:S(2)}) collective-permute-start(s32[4]{0:T(128)S(1)} %copy-done.1), channel_id=1, source_target_pairs={{0,2},{2,0},{4,6},{6,4},{8,10},{10,8},{12,14},{14,12},{1,3},{3,1},... | collective-permute-start | bytes 56 | tf_op jit(solution)/shard_map/ppermute | solution.py:50
  113.1 1.8 %collective-permute-done.22.bracket = s32[4]{0:T(128)S(1)} collective-permute-done((s32[4]{0:T(128)S(1)}, s32[4]{0:T(128)S(1)}, u32[]{:S(2)}, u32[]{:S(2)}) %collective-permute-start.22) | collective-permute-done | bytes 48 | tf_op jit(solution)/shard_map/ppermute | solution.py:50
  115.7 1.8 %collective-permute-start.23 = (f32[4,32,2048]{2,1,0:T(8,128)S(1)}, f32[4,32,2048]{2,1,0:T(8,128)S(1)}, u32[]{:S(2)}, u32[]{:S(2)}) collective-permute-start(f32[4,32,2048]{2,1,0:T(8,128)S(1)} %shard_map.36), channel_id=1, source_target_pairs={{0,2},{2,0},{4,6},{6,4},{8,10},{10,8},{12,14},{14,12},{1,3},{3,1},... | collective-permute-start | bytes 3145736 | tf_op jit(solution)/shard_map/ppermute | solution.py:50
  117.5 1.8 %shard_map.35.whole_in = f32[4,32,4096]{2,1,0:T(8,128)} custom-call(s32[4]{0:T(128)S(1)} %copy-done.1, f32[13,32,2048]{2,1,0:T(8,128)S(1)} %get-tuple-element.27.window, f32[8,128]{1,0:T(8,128)S(1)} %add.31.squares), custom_call_target="tpu_custom_call" | custom-call | tf_op jit(solution)/shard_map/pallas_call | solution.py:469
  119.3 18.0 %collective-permute-done.23.other = f32[4,32,2048]{2,1,0:T(8,128)S(1)} collective-permute-done((f32[4,32,2048]{2,1,0:T(8,128)S(1)}, f32[4,32,2048]{2,1,0:T(8,128)S(1)}, u32[]{:S(2)}, u32[]{:S(2)}) %collective-permute-start.23) | collective-permute-done | bytes 1048608 | tf_op jit(solution)/shard_map/ppermute | solution.py:50
  (45 shorter events, 10.1 us)
Async XLA Ops:
  0.0 1.6 %copy-start = (f32[4,32,4096]{2,1,0:T(8,128)S(1)}, f32[4,32,4096]{2,1,0:T(8,128)}, u32[]{:S(2)}) copy-start(f32[4,32,4096]{2,1,0:T(8,128)} %x_ref.1) | copy-start | bytes 6291460
  1.8 31.0 %collective-permute-start.3 = (f32[4,32,2176]{2,1,0:T(8,128)S(1)}, f32[4,32,2176]{2,1,0:T(8,128)S(1)}, u32[]{:S(2)}, u32[]{:S(2)}) collective-permute-start(f32[4,32,2176]{2,1,0:T(8,128)S(1)} %get-tuple-element.17.refs_0_), channel_id=1, source_target_pairs={{2,6},{6,10},{10,14},{4,0},{8,4},{12,8},{3,7},{7,11},{11,15},{5,1}... | collective-permute-start | bytes 3342344 | tf_op jit(solution)/shard_map/ppermute | solution.py:407
  3.1 29.6 %collective-permute-start.1 = (f32[2,32,2176]{2,1,0:T(8,128)S(1)}, f32[2,32,2176]{2,1,0:T(8,128)S(1)}, u32[]{:S(2)}, u32[]{:S(2)}) collective-permute-start(f32[2,32,2176]{2,1,0:T(8,128)S(1)} %slice.19), channel_id=1, source_target_pairs={{0,2},{2,0},{4,6},{6,4},{8,10},{10,8},{12,14},{14,12},{1,3},{3,1},... | collective-permute-start | bytes 1671176 | tf_op jit(solution)/shard_map/ppermute | solution.py:50
  8.5 24.2 %collective-permute-start.5 = (f32[3,32,2176]{2,1,0:T(8,128)S(1)}, f32[3,32,2176]{2,1,0:T(8,128)S(1)}, u32[]{:S(2)}, u32[]{:S(2)}) collective-permute-start(f32[3,32,2176]{2,1,0:T(8,128)S(1)} %slice.21), channel_id=1, source_target_pairs={{0,4},{4,8},{8,12},{6,2},{10,6},{14,10},{1,5},{5,9},{9,13},{7,3},{... | collective-permute-start | bytes 2506760 | tf_op jit(solution)/shard_map/ppermute | solution.py:407
  12.0 15.9 %collective-permute-start = (f32[1,32,2176]{2,1,0:T(8,128)S(1)}, f32[1,32,2176]{2,1,0:T(8,128)S(1)}, u32[]{:S(2)}, u32[]{:S(2)}) collective-permute-start(f32[1,32,2176]{2,1,0:T(8,128)S(1)} %get-tuple-element.30), channel_id=1, source_target_pairs={{0,2},{2,0},{4,6},{6,4},{8,10},{10,8},{12,14},{14,12},{1,3},{3,1},... | collective-permute-start | bytes 835592 | tf_op jit(solution)/shard_map/ppermute | solution.py:50
  12.1 20.6 %collective-permute-start.2 = (f32[1,32,2176]{2,1,0:T(8,128)S(1)}, f32[1,32,2176]{2,1,0:T(8,128)S(1)}, u32[]{:S(2)}, u32[]{:S(2)}) collective-permute-start(f32[1,32,2176]{2,1,0:T(8,128)S(1)} %get-tuple-element.29), channel_id=1, source_target_pairs={{0,2},{2,0},{4,6},{6,4},{8,10},{10,8},{12,14},{14,12},{1,3},{3,1},... | collective-permute-start | bytes 835592 | tf_op jit(solution)/shard_map/ppermute | solution.py:50
  32.9 29.5 %collective-permute-start.6 = (f32[15,8,2176]{2,1,0:T(8,128)S(1)}, f32[15,8,2176]{2,1,0:T(8,128)S(1)}, u32[]{:S(2)}, u32[]{:S(2)}) collective-permute-start(f32[15,8,2176]{2,1,0:T(8,128)S(1)} %shard_map.29), channel_id=1, source_target_pairs={{0,1},{1,0},{2,3},{3,2},{4,5},{5,4},{6,7},{7,6},{8,9},{9,8},{10,11... | collective-permute-start | bytes 3133448 | tf_op jit(solution)/shard_map/ppermute | solution.py:87
  33.0 12.8 %collective-permute-start.4 = (f32[1,32,2176]{2,1,0:T(8,128)S(1)}, f32[1,32,2176]{2,1,0:T(8,128)S(1)}, u32[]{:S(2)}, u32[]{:S(2)}) collective-permute-start(f32[1,32,2176]{2,1,0:T(8,128)S(1)} %collective-permute-done.refs_1_), channel_id=1, source_target_pairs={{0,4},{4,8},{8,12},{6,2},{10,6},{14,10},{1,5},{5,9},{9,13},{7,3},{... | collective-permute-start | bytes 835592 | tf_op jit(solution)/shard_map/ppermute | solution.py:407
  36.4 25.8 %collective-permute-start.7 = (f32[2,32,2176]{2,1,0:T(8,128)S(1)}, f32[2,32,2176]{2,1,0:T(8,128)S(1)}, u32[]{:S(2)}, u32[]{:S(2)}) collective-permute-start(f32[2,32,2176]{2,1,0:T(8,128)S(1)} %collective-permute-done.1.refs_2_), channel_id=1, source_target_pairs={{0,4},{4,8},{8,12},{6,2},{10,6},{14,10},{1,5},{5,9},{9,13},{7,3},{... | collective-permute-start | bytes 1671176 | tf_op jit(solution)/shard_map/ppermute | solution.py:407
  39.9 22.3 %collective-permute-start.9 = (f32[2,32,2176]{2,1,0:T(8,128)S(1)}, f32[2,32,2176]{2,1,0:T(8,128)S(1)}, u32[]{:S(2)}, u32[]{:S(2)}) collective-permute-start(f32[2,32,2176]{2,1,0:T(8,128)S(1)} %collective-permute-done.1.refs_2_), channel_id=1, source_target_pairs={{2,6},{6,10},{10,14},{4,0},{8,4},{12,8},{3,7},{7,11},{11,15},{5,1}... | collective-permute-start | bytes 1671176 | tf_op jit(solution)/shard_map/ppermute | solution.py:407
  41.2 19.6 %collective-permute-start.8 = (f32[1,32,2176]{2,1,0:T(8,128)S(1)}, f32[1,32,2176]{2,1,0:T(8,128)S(1)}, u32[]{:S(2)}, u32[]{:S(2)}) collective-permute-start(f32[1,32,2176]{2,1,0:T(8,128)S(1)} %collective-permute-done.2.refs_3_), channel_id=1, source_target_pairs={{0,4},{4,8},{8,12},{6,2},{10,6},{14,10},{1,5},{5,9},{9,13},{7,3},{... | collective-permute-start | bytes 835592 | tf_op jit(solution)/shard_map/ppermute | solution.py:407
  45.8 16.4 %collective-permute-start.10 = (f32[1,32,2176]{2,1,0:T(8,128)S(1)}, f32[1,32,2176]{2,1,0:T(8,128)S(1)}, u32[]{:S(2)}, u32[]{:S(2)}) collective-permute-start(f32[1,32,2176]{2,1,0:T(8,128)S(1)} %collective-permute-done.2.refs_3_), channel_id=1, source_target_pairs={{2,6},{6,10},{10,14},{4,0},{8,4},{12,8},{3,7},{7,11},{11,15},{5,1}... | collective-permute-start | bytes 835592 | tf_op jit(solution)/shard_map/ppermute | solution.py:407
  62.4 12.0 %collective-permute-start.11 = (f32[7,8,2176]{2,1,0:T(8,128)S(1)}, f32[7,8,2176]{2,1,0:T(8,128)S(1)}, u32[]{:S(2)}, u32[]{:S(2)}) collective-permute-start(f32[7,8,2176]{2,1,0:T(8,128)S(1)} %shard_map.31), channel_id=1, source_target_pairs={{0,1},{1,0},{2,3},{3,2},{4,5},{5,4},{6,7},{7,6},{8,9},{9,8},{10,11... | collective-permute-start | bytes 1462280 | tf_op jit(solution)/shard_map/ppermute | solution.py:87
  64.9 1.4 collective-permute-start.12
  66.3 3.7 %collective-permute-start.13 = (f32[2,8,128]{2,1,0:T(8,128)S(1)}, f32[2,8,128]{2,1,0:T(8,128)S(1)}, u32[]{:S(2)}, u32[]{:S(2)}) collective-permute-start(f32[2,8,128]{2,1,0:T(8,128)S(1)} %add.24), channel_id=1, source_target_pairs={{0,2},{2,0},{4,6},{6,4},{8,10},{10,8},{12,14},{14,12},{1,3},{3,1},... | collective-permute-start | bytes 24584 | tf_op jit(solution)/shard_map/ppermute | solution.py:64
  70.0 7.6 %collective-permute-start.14 = (f32[2,8,128]{2,1,0:T(8,128)S(1)}, f32[2,8,128]{2,1,0:T(8,128)S(1)}, u32[]{:S(2)}, u32[]{:S(2)}) collective-permute-start(f32[2,8,128]{2,1,0:T(8,128)S(1)} %add.25), channel_id=1, source_target_pairs={{0,4},{2,6},{4,8},{6,10},{8,12},{10,14},{1,5},{3,7},{5,9},{7,11},{... | collective-permute-start | bytes 24584 | tf_op jit(solution)/shard_map/ppermute | solution.py:433
  73.0 5.5 %collective-permute-start.15 = (f32[2,8,128]{2,1,0:T(8,128)S(1)}, f32[2,8,128]{2,1,0:T(8,128)S(1)}, u32[]{:S(2)}, u32[]{:S(2)}) collective-permute-start(f32[2,8,128]{2,1,0:T(8,128)S(1)} %add.25), channel_id=1, source_target_pairs={{4,0},{6,2},{8,4},{10,6},{12,8},{14,10},{5,1},{7,3},{9,5},{11,7},{... | collective-permute-start | bytes 24584 | tf_op jit(solution)/shard_map/ppermute | solution.py:434
  89.7 1.3 collective-permute-start.16
  91.0 3.8 %collective-permute-start.17 = (f32[2,24,128]{2,1,0:T(8,128)S(1)}, f32[2,24,128]{2,1,0:T(8,128)S(1)}, u32[]{:S(2)}, u32[]{:S(2)}) collective-permute-start(f32[2,24,128]{2,1,0:T(8,128)S(1)} %add.26), channel_id=1, source_target_pairs={{0,2},{2,0},{4,6},{6,4},{8,10},{10,8},{12,14},{14,12},{1,3},{3,1},... | collective-permute-start | bytes 73736 | tf_op jit(solution)/shard_map/ppermute | solution.py:64
  94.8 16.5 %copy-start.1 = (s32[4]{0:T(128)S(1)}, s32[4]{0:T(128)}, u32[]{:S(2)}) copy-start(s32[4]{0:T(128)} %bracket.1) | copy-start | bytes 52
  100.2 1.2 collective-permute-start.18
  101.4 3.6 %collective-permute-start.19 = (f32[8,128]{1,0:T(8,128)S(1)}, f32[8,128]{1,0:T(8,128)S(1)}, u32[]{:S(2)}, u32[]{:S(2)}) collective-permute-start(f32[8,128]{1,0:T(8,128)S(1)} %add.28), channel_id=1, source_target_pairs={{0,2},{2,0},{4,6},{6,4},{8,10},{10,8},{12,14},{14,12},{1,3},{3,1},... | collective-permute-start | bytes 12296 | tf_op jit(solution)/shard_map/ppermute | solution.py:64
  105.0 3.6 %collective-permute-start.20 = (f32[8,128]{1,0:T(8,128)S(1)}, f32[8,128]{1,0:T(8,128)S(1)}, u32[]{:S(2)}, u32[]{:S(2)}) collective-permute-start(f32[8,128]{1,0:T(8,128)S(1)} %add.29), channel_id=1, source_target_pairs={{0,4},{2,6},{4,0},{6,2},{8,12},{10,14},{12,8},{14,10},{1,5},{3,7},... | collective-permute-start | bytes 12296 | tf_op jit(solution)/shard_map/ppermute | solution.py:64
  108.6 4.5 %collective-permute-start.21 = (f32[8,128]{1,0:T(8,128)S(1)}, f32[8,128]{1,0:T(8,128)S(1)}, u32[]{:S(2)}, u32[]{:S(2)}) collective-permute-start(f32[8,128]{1,0:T(8,128)S(1)} %add.30), channel_id=1, source_target_pairs={{0,8},{2,10},{4,12},{6,14},{8,0},{10,2},{12,4},{14,6},{1,9},{3,11}... | collective-permute-start | bytes 12296 | tf_op jit(solution)/shard_map/ppermute | solution.py:64
  111.4 3.6 %collective-permute-start.22 = (s32[4]{0:T(128)S(1)}, s32[4]{0:T(128)S(1)}, u32[]{:S(2)}, u32[]{:S(2)}) collective-permute-start(s32[4]{0:T(128)S(1)} %copy-done.1), channel_id=1, source_target_pairs={{0,2},{2,0},{4,6},{6,4},{8,10},{10,8},{12,14},{14,12},{1,3},{3,1},... | collective-permute-start | bytes 56 | tf_op jit(solution)/shard_map/ppermute | solution.py:50
  115.7 21.6 %collective-permute-start.23 = (f32[4,32,2048]{2,1,0:T(8,128)S(1)}, f32[4,32,2048]{2,1,0:T(8,128)S(1)}, u32[]{:S(2)}, u32[]{:S(2)}) collective-permute-start(f32[4,32,2048]{2,1,0:T(8,128)S(1)} %shard_map.36), channel_id=1, source_target_pairs={{0,2},{2,0},{4,6},{6,4},{8,10},{10,8},{12,14},{14,12},{1,3},{3,1},... | collective-permute-start | bytes 3145736 | tf_op jit(solution)/shard_map/ppermute | solution.py:50

commit v5 on v4

--- a/solution.py
+++ b/solution.py
@@ -20,8 +20,8 @@
 HIGH = 2 * ITERS + REACH + 1
 FAR = 3
 EDGE = 2 * ITERS
-CHUNKS = (0, 1, 3)
-VMEM_LIMIT = 12 * 1024 * 1024
+CHUNKS = (0, 2)
+VMEM_LIMIT = 4 * 1024 * 1024
 
 F32 = jnp.float32
 
@@ -181,27 +181,27 @@
     speeds[...] = jnp.broadcast_to(value, speeds.shape)
 
 
-def theta_pass(phi, drift, speeds, theta, low, high, first, count):
+def theta_pass(phi, speeds, theta, low, high, first, count, shift=0):
     tiles = phi.shape[2] // LANES
 
     def body(k, carry):
         before, after, stretch = neighbours_of(k, first, count)
-        scale = speeds[pl.ds(k, 1), :] * stretch
+        scale = speeds[pl.ds(k - shift, 1), :] * stretch
         for t in range(tiles):
             cols = tile_of(t)
-            theta[k, :, cols] = scale * (phi[after, :, cols] - phi[before, :, cols]) - drift[k, :, cols]
+            theta[k, :, cols] = scale * (phi[after, :, cols] - phi[before, :, cols]) - theta[k, :, cols]
         return carry
 
     lax.fori_loop(low, high, body, 0)
 
 
-def update_pass(phi, speeds, theta, low, high, first, count, store):
+def update_pass(phi, speeds, theta, low, high, first, count, store, shift=0):
     rows = phi.shape[1]
     tiles = phi.shape[2] // LANES
 
     def body(k, carry):
         before, after, stretch = neighbours_of(k, first, count)
-        scale = speeds[pl.ds(k, 1), :] * stretch
+        scale = speeds[pl.ds(k - shift, 1), :] * stretch
         gid = k + first
         inside = (gid > 0) & (gid < count - 1)
 
@@ -247,80 +247,79 @@
     for q in range(local):
         place(phi, own_at(lo, q), keep[q], edge_rows[q])
         place(phi, own_at(1 - lo, q), recv[chunk_of(q)][q - CHUNKS[chunk_of(q)]], edge_rows[local + q])
-    phi[jnp.where(lo == 1, LOW - 1, top), 0:rows, :] = near_early[0]
-    phi[jnp.where(lo == 1, top, LOW - 1), 0:rows, :] = near_late[0]
-    drift_pass(phi, drift, norms, LOW, top, first, count, rows, LOW)
-
-
-def outer_kernel(*refs, count):
-    refs = list(refs)
-    pick = lambda n: [refs.pop(0) for _ in range(n)]
-    _, _, near_early, far_early = pick(4)
-    near_late, far_late = pick(len(CHUNKS)), pick(len([c for c in range(len(CHUNKS)) if far_count(c)]))
-    rows_early, rows_late, phi, drift = pick(4)
-    local, rows, _ = near_early.shape
+        low_at, high_at = LOW - 1 - q, top + q
+        place(phi, jnp.where(lo == 1, low_at, high_at), near_early[q], edge_rows[2 * local + q])
+        if q < near_late.shape[0]:
+            place(phi, jnp.where(lo == 1, high_at, low_at), near_late[q], edge_rows[3 * local + q])
+    drift_pass(phi, drift, norms, LOW - 1, top + 1, first, count, rows, LOW - 1)
+
+
+def middle_inner_kernel(_, __, norms, phi, theta, new_phi, new_drift, new_norms, speeds, *, count, local, rows):
+    hi, _ = pair_position()
+    first = hi * (PAIR * local) - LOW
+    top = LOW + PAIR * local
+    speeds_of(norms, speeds)
+    theta_pass(phi, speeds, theta, LOW - 1, top + 1, first, count, LOW - 1)
+
+    def store(k, t, value):
+        new_phi[k, :, tile_of(t)] = value
+
+    update_pass(phi, speeds, theta, LOW, top, first, count, store, LOW - 1)
+    new_norms[...] = jnp.zeros(new_norms.shape, F32)
+    drift_pass(new_phi, new_drift, new_norms, LOW + 1, top - 1, first, count, rows)
+
+
+def middle_outer_kernel(norms, near_late, far_early, far_late, rows_early, rows_late, *refs, count, local):
+    phi, theta, new_phi, new_drift, new_norms, speeds = refs[5:]
+    rows = near_late.shape[1]
     hi, lo = pair_position()
     first = hi * (PAIR * local) - LOW
     top = LOW + PAIR * local
-    skipped = len(CHUNKS) - len(far_late)
-    for q in range(local):
-        low_at, high_at = LOW - 1 - q, top + q
-        place(phi, jnp.where(lo == 1, low_at, high_at), near_early[q], rows_early[PAIR * local + q])
-        late = near_late[chunk_of(q)][q - CHUNKS[chunk_of(q)]]
-        place(phi, jnp.where(lo == 1, high_at, low_at), late, rows_late[q])
+    window = phi.shape[0]
+    done = CHUNKS[-1]
+    for q in range(done, local):
+        place(phi, jnp.where(lo == 1, top + q, LOW - 1 - q), near_late[q - done], rows_late[q - done])
     for i in range(FAR):
         low_at, high_at = LOW - 1 - local - i, top + local + i
-        q = local - 1 - i
-        late = far_late[chunk_of(q) - skipped].at[q - max(CHUNKS[chunk_of(q)], local - FAR)]
-        late_rows = rows_late.at[local + FAR - 1 - i]
-        early, early_rows = far_early.at[FAR - 1 - i], rows_early.at[(PAIR + 1) * local + FAR - 1 - i]
+        at = FAR - 1 - i
+        late, late_rows = far_late.at[at], rows_late.at[local - done + at]
+        early, early_rows = far_early.at[at], rows_early.at[3 * local + done + at]
 
         @pl.when(lo == 1)
         def _():
-            if high_at < phi.shape[0]:
+            if high_at < window:
                 place(phi, high_at, early[...], early_rows[...])
             if low_at >= 0:
                 place(phi, low_at, late[...], late_rows[...])
 
         @pl.when(lo == 0)
         def _():
-            if high_at < phi.shape[0]:
+            if high_at < window:
                 place(phi, high_at, late[...], late_rows[...])
             if low_at >= 0:
                 place(phi, low_at, early[...], early_rows[...])
 
-    drift_pass(phi, drift, None, 1, LOW, first, count, rows)
-    drift_pass(phi, drift, None, top, phi.shape[0] - 1, first, count, rows)
-
-
-def far_count(chunk):
-    ends = CHUNKS[1:] + (CHUNKS[-1] + FAR,)
-    return max(0, ends[chunk] - max(CHUNKS[chunk], 2 * ITERS - FAR))
-
-
-def middle_kernel(phi, drift, norms, new_phi, new_drift, new_norms, theta, speeds, *, count, local, rows, done):
-    hi, _ = pair_position()
-    first = hi * (PAIR * local) - LOW
-    window = phi.shape[0]
-    speeds_of(norms, speeds)
-    theta_pass(phi, drift, speeds, theta, done + 1, window - done - 1, first, count)
-
     def store(k, t, value):
         new_phi[k, :, tile_of(t)] = value
 
-    update_pass(phi, speeds, theta, done + 2, window - done - 2, first, count, store)
-    new_norms[...] = jnp.zeros(new_norms.shape, F32)
-    drift_pass(new_phi, new_drift, new_norms, done + 3, window - done - 3, first, count, rows)
-
-
-def last_kernel(phi, drift, norms, final, squares, theta, speeds, *, count, local, rows, done):
+    speeds_of(norms, speeds)
+    for low, high in ((1, LOW - 1), (top + 1, window - 1)):
+        drift_pass(phi, theta, None, low, high, first, count, rows)
+        theta_pass(phi, speeds, theta, low, high, first, count)
+    for low, high in ((2, LOW), (top, window - 2)):
+        update_pass(phi, speeds, theta, low, high, first, count, store)
+    for low, high in ((3, LOW + 1), (top - 1, window - 3)):
+        drift_pass(new_phi, new_drift, new_norms, low, high, first, count, rows)
+
+
+def last_kernel(phi, _, norms, final, squares, theta, speeds, *, count, local, rows, done):
     hi, _ = pair_position()
     first = hi * (PAIR * local) - LOW
     window = phi.shape[0]
     tiles = final.shape[2] // LANES
     shift = LOW - REACH
     speeds_of(norms, speeds)
-    theta_pass(phi, drift, speeds, theta, done + 1, window - done - 1, first, count)
+    theta_pass(phi, speeds, theta, done + 1, window - done - 1, first, count)
 
     def store(k, t, value):
         if t < tiles:
@@ -398,7 +397,7 @@
     half = columns // PAIR
     wide = half + LANES
     window = LOW + PAIR * local + HIGH
-    if devices & (devices - 1) or local != 2 * ITERS or count > SUBLANES * LANES or rows % SUBLANES:
+    if devices & (devices - 1) or ITERS != 2 or local != 2 * ITERS or count > SUBLANES * LANES or rows % SUBLANES:
         raise ValueError("unsupported sizes")
     shape = functools.partial(jax.ShapeDtypeStruct, dtype=F32)
     block = shape((local, rows, wide))
@@ -415,42 +414,42 @@
     near_early = move(keep, (1,), (0,))
     far_early = move(keep[local - FAR :], (0,), (1,))
     near_late = [move(value, (0,), (1,)) for value in recv]
-    far_late = [
-        move(value[max(0, local - FAR - a) :], (1,), (0,))
-        for i, (a, value) in enumerate(zip(CHUNKS, recv)) if far_count(i)
-    ]
-    rows_early = neighbour_rows([keep] + recv + [near_early, far_early])
-    rows_late = neighbour_rows(near_late + far_late)
+    far_late = move(jnp.concatenate(recv, axis=0)[local - FAR :], (1,), (0,))
+    rows_early = neighbour_rows([keep] + recv + [near_early, near_late[0], far_early])
+    rows_late = neighbour_rows([near_late[1], far_late])
     held = shape((window, rows + 2 * EDGE, wide))
     lines = -(-window // SUBLANES) * SUBLANES
     norm_shape = shape((2, lines, LANES))
     operands = [keep] + recv + [near_early, near_late[0], rows_early]
+    inside = PAIR * local + 2
+    inside_lines = -(-inside // SUBLANES) * SUBLANES
     phi, drift, norms = call(
-        functools.partial(inner_kernel, count=count), (held, held, shape((2, PAIR * local, LANES))),
+        functools.partial(inner_kernel, count=count), (held, held, shape((2, inside_lines, LANES))),
         operands=len(operands),
     )(*operands)
     norms = small_sum(norms, (1,))
-    low_norms = lax.ppermute(norms, "img", ahead)
-    high_norms = lax.ppermute(norms, "img", back)
-    operands = [phi, drift, near_early, far_early] + near_late + far_late + [rows_early, rows_late]
-    phi, drift = call(
-        functools.partial(outer_kernel, count=count), (held, held), operands=len(operands), aliases={0: 0, 1: 1}
-    )(*operands)
+    own_norms = norms[:, 1 : inside - 1]
+    low_norms = lax.ppermute(own_norms, "img", ahead)
+    high_norms = lax.ppermute(own_norms, "img", back)
+    state = call(
+        functools.partial(middle_inner_kernel, count=count, local=local, rows=rows),
+        (held, held, held, held, norm_shape), scratch=[pltpu.VMEM((inside_lines, LANES), F32)],
+        operands=3, aliases={0: 0, 1: 1},
+    )(phi, drift, norms)
     pad = jnp.zeros((2, lines - window, LANES), F32)
-    norms = jnp.concatenate([low_norms[:, PAIR * local - LOW :], norms, high_norms[:, :HIGH], pad], axis=1)
-    scratch = [pltpu.VMEM(held.shape, F32), pltpu.VMEM((lines, LANES), F32)]
-    for iteration in range(ITERS - 1):
-        if iteration:
-            norms = small_sum(norms, (1,))
-        phi, drift, norms = call(
-            functools.partial(middle_kernel, count=count, local=local, rows=rows, done=2 * iteration),
-            (held, held, norm_shape), scratch=scratch, operands=3,
-        )(phi, drift, norms)
+    norms = jnp.concatenate([low_norms[:, PAIR * local - LOW :], own_norms, high_norms[:, :HIGH], pad], axis=1)
+    operands = [norms, near_late[1], far_early, far_late, rows_early, rows_late]
+    _, _, phi, drift, norms = call(
+        functools.partial(middle_outer_kernel, count=count, local=local),
+        (held, held, held, held, norm_shape), scratch=[pltpu.VMEM((lines, LANES), F32)],
+        operands=len(operands) + len(state), aliases={len(operands) + i: i for i in range(len(state))},
+    )(*operands, *state)
+    scratch = [pltpu.VMEM((lines, LANES), F32)]
     norms = small_sum(norms, (1,))
-    final, squares = call(
+    final, squares, _ = call(
         functools.partial(last_kernel, count=count, local=local, rows=rows, done=2 * (ITERS - 1)),
-        (shape((PAIR * local + 2 * REACH + 1, rows, half)), shape((SUBLANES, LANES))),
-        scratch=scratch, operands=3,
+        (shape((PAIR * local + 2 * REACH + 1, rows, half)), shape((SUBLANES, LANES)), held),
+        scratch=scratch, operands=3, aliases={1: 2},
     )(phi, drift, norms)
     steps = []
     step = 1

time: 139 us -> 141 us (1.014)
  waiting for transfers between devices: 65.8 us -> 74.2 us
  starting transfers between devices: 44.1 us -> 38.2 us
    ppermute x7 -> x5, waiting for transfers between devices: 15.1 us -> 27.8 us  [per_device(): lax.ppermute(value, 'img', [p for p in ahead if p[0] % PAIR in up] + [p f...]
    ppermute x5 -> x4, starting transfers between devices: 11 us -> 6.47 us  [swap_pairs(): return lax.ppermute(value, 'img', [(i, i ^ 1) for i in range(count)])]
    ppermute x5 -> x4, waiting for transfers between devices: 38.4 us -> 34.5 us  [swap_pairs(): return lax.ppermute(value, 'img', [(i, i ^ 1) for i in range(count)])]
    ppermute x7 -> x5, starting transfers between devices: 18.8 us -> 16.2 us  [per_device(): lax.ppermute(value, 'img', [p for p in ahead if p[0] % PAIR in up] + [p f...]
  transfers between devices with their start and end apart: 24 -> 21, of which waited for: 14 -> 15; matrix products, arithmetic and copies ran while one was open for 0% -> 0% of each run, Pallas kernels for 5% -> 7%
where the time goes in v5:
time: 141 us
  waiting for transfers between devices  74.2 us (53%)
  starting transfers between devices  38.2 us (27%)
  Pallas kernels  26.3 us (19%)
  local copies, waits for them, and re-layouts  1.81 us (1%)
    ppermute x4, waiting for transfers between devices, swap_pairs(): return lax.ppermute(value, 'img', [(i, i ^ 1) for i in range(count)])  34.5 us
    ppermute x5, waiting for transfers between devices, per_device(): lax.ppermute(value, 'img', [p for p in ahead if p[0] % PAIR in up] + [p f...  27.8 us
    ppermute x5, starting transfers between devices, per_device(): lax.ppermute(value, 'img', [p for p in ahead if p[0] % PAIR in up] + [p f...  16.2 us
    ppermute x5, starting transfers between devices, small_sum(): lax.ppermute(value, 'img', [(i, i ^ step) for i in range(count)])  9.85 us
    ppermute x5, waiting for transfers between devices, small_sum(): lax.ppermute(value, 'img', [(i, i ^ step) for i in range(count)])  8.6 us
    pallas_call x1, Pallas kernels, per_device(): call(functools.partial(middle_outer_kernel, count=count, local=local), (h...  8.6 us
    ppermute x4, starting transfers between devices, swap_pairs(): return lax.ppermute(value, 'img', [(i, i ^ 1) for i in range(count)])  6.47 us
    pallas_call x1, Pallas kernels, per_device(): call(functools.partial(last_kernel, count=count, local=local, rows=rows,...  5.54 us
  transfers between devices with their start and end apart: 21, of which 15 were waited for; matrix products, arithmetic and copies ran while one was open for 0% of the time, Pallas kernels for 7%

profile of v5, /device:TPU:0, one launch (start us, length us, event | category | flops | bytes accessed | tf_op | source)
XLA Modules:
  0.0 140.9 jit_solution(6246135581764318778)
XLA Ops:
  0.0 1.6 %copy-done = f32[4,32,4096]{2,1,0:T(8,128)S(1)} copy-done((f32[4,32,4096]{2,1,0:T(8,128)S(1)}, f32[4,32,4096]{2,1,0:T(8,128)}, u32[]{:S(2)}) %copy-start) | copy-done | bytes 2097176
  1.8 3.1 %collective-permute-start = (f32[2,32,2176]{2,1,0:T(8,128)S(1)}, f32[2,32,2176]{2,1,0:T(8,128)S(1)}, u32[]{:S(2)}, u32[]{:S(2)}) collective-permute-start(f32[2,32,2176]{2,1,0:T(8,128)S(1)} %get-tuple-element.36), channel_id=1, source_target_pairs={{0,2},{2,0},{4,6},{6,4},{8,10},{10,8},{12,14},{14,12},{1,3},{3,1},... | collective-permute-start | bytes 1671176 | tf_op jit(solution)/shard_map/ppermute | solution.py:50
  4.9 1.3 collective-permute-start.2
  6.3 4.6 %collective-permute-start.4 = (f32[3,32,2176]{2,1,0:T(8,128)S(1)}, f32[3,32,2176]{2,1,0:T(8,128)S(1)}, u32[]{:S(2)}, u32[]{:S(2)}) collective-permute-start(f32[3,32,2176]{2,1,0:T(8,128)S(1)} %slice.23), channel_id=1, source_target_pairs={{0,4},{4,8},{8,12},{6,2},{10,6},{14,10},{1,5},{5,9},{9,13},{7,3},{... | collective-permute-start | bytes 2506760 | tf_op jit(solution)/shard_map/ppermute | solution.py:406
  10.9 7.4 %collective-permute-done.refs_1_ = f32[2,32,2176]{2,1,0:T(8,128)S(1)} collective-permute-done((f32[2,32,2176]{2,1,0:T(8,128)S(1)}, f32[2,32,2176]{2,1,0:T(8,128)S(1)}, u32[]{:S(2)}, u32[]{:S(2)}) %collective-permute-start) | collective-permute-done | bytes 557088 | tf_op jit(solution)/shard_map/ppermute | solution.py:50
  18.4 4.0 %collective-permute-start.3 = (f32[2,32,2176]{2,1,0:T(8,128)S(1)}, f32[2,32,2176]{2,1,0:T(8,128)S(1)}, u32[]{:S(2)}, u32[]{:S(2)}) collective-permute-start(f32[2,32,2176]{2,1,0:T(8,128)S(1)} %collective-permute-done.refs_1_), channel_id=1, source_target_pairs={{0,4},{4,8},{8,12},{6,2},{10,6},{14,10},{1,5},{5,9},{9,13},{7,3},{... | collective-permute-start | bytes 1671176 | tf_op jit(solution)/shard_map/ppermute | solution.py:406
  22.4 7.1 %collective-permute-done.1.refs_2_ = f32[2,32,2176]{2,1,0:T(8,128)S(1)} collective-permute-done((f32[2,32,2176]{2,1,0:T(8,128)S(1)}, f32[2,32,2176]{2,1,0:T(8,128)S(1)}, u32[]{:S(2)}, u32[]{:S(2)}) %collective-permute-start.1) | collective-permute-done | bytes 557088 | tf_op jit(solution)/shard_map/ppermute | solution.py:50
  29.8 10.2 %collective-permute-done.3.refs_4_ = f32[2,32,2176]{2,1,0:T(8,128)S(1)} collective-permute-done((f32[2,32,2176]{2,1,0:T(8,128)S(1)}, f32[2,32,2176]{2,1,0:T(8,128)S(1)}, u32[]{:S(2)}, u32[]{:S(2)}) %collective-permute-start.3) | collective-permute-done | bytes 557088 | tf_op jit(solution)/shard_map/ppermute | solution.py:406
  40.4 1.3 collective-permute-start.11
  41.7 5.0 %collective-permute-start.10 = (f32[2,32,2176]{2,1,0:T(8,128)S(1)}, f32[2,32,2176]{2,1,0:T(8,128)S(1)}, u32[]{:S(2)}, u32[]{:S(2)}) collective-permute-start(f32[2,32,2176]{2,1,0:T(8,128)S(1)} %collective-permute-done.1.refs_2_), channel_id=1, source_target_pairs={{0,4},{4,8},{8,12},{6,2},{10,6},{14,10},{1,5},{5,9},{9,13},{7,3},{... | collective-permute-start | bytes 1671176 | tf_op jit(solution)/shard_map/ppermute | solution.py:406
  46.7 12.5 %collective-permute-done.10.refs_0_.near_late = f32[2,32,2176]{2,1,0:T(8,128)S(1)} collective-permute-done((f32[2,32,2176]{2,1,0:T(8,128)S(1)}, f32[2,32,2176]{2,1,0:T(8,128)S(1)}, u32[]{:S(2)}, u32[]{:S(2)}) %collective-permute-start.10) | collective-permute-done | bytes 557088 | tf_op jit(solution)/shard_map/ppermute | solution.py:406
  59.2 4.8 %collective-permute-done.11.refs_1_.far_late = f32[3,32,2176]{2,1,0:T(8,128)S(1)} collective-permute-done((f32[3,32,2176]{2,1,0:T(8,128)S(1)}, f32[3,32,2176]{2,1,0:T(8,128)S(1)}, u32[]{:S(2)}, u32[]{:S(2)}) %collective-permute-start.11) | collective-permute-done | bytes 835616 | tf_op jit(solution)/shard_map/ppermute | solution.py:406
  64.2 3.1 %shard_map.30 = (f32[21,40,2176]{2,1,0:T(8,128)S(1)}, f32[21,40,2176]{2,1,0:T(8,128)S(1)}, f32[2,16,128]{2,1,0:T(8,128)S(1)}) custom-call(f32[4,32,2176]{2,1,0:T(8,128)S(1)} %get-tuple-element.20.refs_0_, f32[2,32,2176]{2,1,0:T(8,128)S(1)} %collective-permute-done.refs_1_, f32[2,32,2176]{2,1,0:T(8,128)S(1)} %collective-permute-done.1.refs_2_, ...), custom_call_target="tpu_custom_call" | custom-call | tf_op jit(solution)/shard_map/pallas_call | solution.py:426
  69.6 2.9 %collective-permute-done.7 = f32[2,16,128]{2,1,0:T(8,128)S(1)} collective-permute-done((f32[2,16,128]{2,1,0:T(8,128)S(1)}, f32[2,16,128]{2,1,0:T(8,128)S(1)}, u32[]{:S(2)}, u32[]{:S(2)}) %collective-permute-start.7) | collective-permute-done | bytes 16416 | tf_op jit(solution)/shard_map/ppermute | solution.py:64
  72.5 3.6 %collective-permute-start.8 = (f32[2,8,128]{2,1,0:T(8,128)S(1)}, f32[2,8,128]{2,1,0:T(8,128)S(1)}, u32[]{:S(2)}, u32[]{:S(2)}) collective-permute-start(f32[2,8,128]{2,1,0:T(8,128)S(1)} %slice.28), channel_id=1, source_target_pairs={{0,4},{2,6},{4,8},{6,10},{8,12},{10,14},{1,5},{3,7},{5,9},{7,11},{... | collective-permute-start | bytes 24584 | tf_op jit(solution)/shard_map/ppermute | solution.py:432
  76.1 1.3 collective-permute-start.9
  77.5 5.1 %shard_map.32 = (f32[21,40,2176]{2,1,0:T(8,128)S(1)}, f32[21,40,2176]{2,1,0:T(8,128)S(1)}, f32[21,40,2176]{2,1,0:T(8,128)S(1)}, f32[21,40,2176]{2,1,0:T(8,128)S(1)}, f32[2,24,128]{2,1,0:T(8,128)S(1)}) custom-call(f32[21,40,2176]{2,1,0:T(8,128)S(1)} %get-tuple-element.23._, ...), custom_call_target="tpu_custom_call", output_to_operand_aliasing={{0}: (0, {}), {1}: (1, {})} | custom-call | tf_op jit(solution)/shard_map/pallas_call | solution.py:434
  82.7 8.6 %shard_map.33 = (f32[21,40,2176]{2,1,0:T(8,128)S(1)}, f32[21,40,2176]{2,1,0:T(8,128)S(1)}, f32[21,40,2176]{2,1,0:T(8,128)S(1)}, f32[21,40,2176]{2,1,0:T(8,128)S(1)}, f32[2,24,128]{2,1,0:T(8,128)S(1)}) custom-call(f32[2,24,128]{2,1,0:T(8,128)S(1)} %maximum_maximum_fusion.norms, ...), custom_call_target="tpu_custom_call", output_to_operand_aliasing={{0}: (6, {}), {1}: (7, {}), {2}: (8, {}), {3}: (9, {}), {4}... | custom-call | tf_op jit(solution)/shard_map/pallas_call | solution.py:442
  91.4 1.2 collective-permute-done.13
  92.5 1.6 %collective-permute-start.14 = (f32[2,24,128]{2,1,0:T(8,128)S(1)}, f32[2,24,128]{2,1,0:T(8,128)S(1)}, u32[]{:S(2)}, u32[]{:S(2)}) collective-permute-start(f32[2,24,128]{2,1,0:T(8,128)S(1)} %add.26), channel_id=1, source_target_pairs={{0,2},{2,0},{4,6},{6,4},{8,10},{10,8},{12,14},{14,12},{1,3},{3,1},... | collective-permute-start | bytes 73736 | tf_op jit(solution)/shard_map/ppermute | solution.py:64
  94.2 2.2 %collective-permute-done.14 = f32[2,24,128]{2,1,0:T(8,128)S(1)} collective-permute-done((f32[2,24,128]{2,1,0:T(8,128)S(1)}, f32[2,24,128]{2,1,0:T(8,128)S(1)}, u32[]{:S(2)}, u32[]{:S(2)}) %collective-permute-start.14) | collective-permute-done | bytes 24608 | tf_op jit(solution)/shard_map/ppermute | solution.py:64
  96.4 5.5 %shard_map.34 = (f32[13,32,2048]{2,1,0:T(8,128)S(1)}, f32[8,128]{1,0:T(8,128)S(1)}, f32[21,40,2176]{2,1,0:T(8,128)S(1)}) custom-call(f32[21,40,2176]{2,1,0:T(8,128)S(1)} %get-tuple-element.30.phi, f32[21,40,2176]{2,1,0:T(8,128)S(1)} %get-tuple-element.31._, f32[2,24,128]{2,1,0:T(8,128)S(1)} %add.27.norms), custom_call_target="tpu_custom_call", output_to_operand_aliasing={{2}: (1, {})} | custom-call | tf_op jit(solution)/shard_map/pallas_call | solution.py:449
  103.1 1.6 %collective-permute-start.16 = (f32[8,128]{1,0:T(8,128)S(1)}, f32[8,128]{1,0:T(8,128)S(1)}, u32[]{:S(2)}, u32[]{:S(2)}) collective-permute-start(f32[8,128]{1,0:T(8,128)S(1)} %add.28), channel_id=1, source_target_pairs={{0,2},{2,0},{4,6},{6,4},{8,10},{10,8},{12,14},{14,12},{1,3},{3,1},... | collective-permute-start | bytes 12296 | tf_op jit(solution)/shard_map/ppermute | solution.py:64
  104.7 2.0 %collective-permute-done.16 = f32[8,128]{1,0:T(8,128)S(1)} collective-permute-done((f32[8,128]{1,0:T(8,128)S(1)}, f32[8,128]{1,0:T(8,128)S(1)}, u32[]{:S(2)}, u32[]{:S(2)}) %collective-permute-start.16) | collective-permute-done | bytes 4128 | tf_op jit(solution)/shard_map/ppermute | solution.py:64
  106.7 2.7 %collective-permute-start.17 = (f32[8,128]{1,0:T(8,128)S(1)}, f32[8,128]{1,0:T(8,128)S(1)}, u32[]{:S(2)}, u32[]{:S(2)}) collective-permute-start(f32[8,128]{1,0:T(8,128)S(1)} %add.29), channel_id=1, source_target_pairs={{0,4},{2,6},{4,0},{6,2},{8,12},{10,14},{12,8},{14,10},{1,5},{3,7},... | collective-permute-start | bytes 12296 | tf_op jit(solution)/shard_map/ppermute | solution.py:64
  109.4 1.6 %collective-permute-done.17 = f32[8,128]{1,0:T(8,128)S(1)} collective-permute-done((f32[8,128]{1,0:T(8,128)S(1)}, f32[8,128]{1,0:T(8,128)S(1)}, u32[]{:S(2)}, u32[]{:S(2)}) %collective-permute-start.17) | collective-permute-done | bytes 4128 | tf_op jit(solution)/shard_map/ppermute | solution.py:64
  111.0 3.0 %collective-permute-start.18 = (f32[8,128]{1,0:T(8,128)S(1)}, f32[8,128]{1,0:T(8,128)S(1)}, u32[]{:S(2)}, u32[]{:S(2)}) collective-permute-start(f32[8,128]{1,0:T(8,128)S(1)} %add.30), channel_id=1, source_target_pairs={{0,8},{2,10},{4,12},{6,14},{8,0},{10,2},{12,4},{14,6},{1,9},{3,11}... | collective-permute-start | bytes 12296 | tf_op jit(solution)/shard_map/ppermute | solution.py:64
  114.0 1.6 %collective-permute-start.19 = (s32[4]{0:T(128)S(1)}, s32[4]{0:T(128)S(1)}, u32[]{:S(2)}, u32[]{:S(2)}) collective-permute-start(s32[4]{0:T(128)S(1)} %copy-done.1), channel_id=1, source_target_pairs={{0,2},{2,0},{4,6},{6,4},{8,10},{10,8},{12,14},{14,12},{1,3},{3,1},... | collective-permute-start | bytes 56 | tf_op jit(solution)/shard_map/ppermute | solution.py:50
  115.6 1.9 %collective-permute-done.19.bracket = s32[4]{0:T(128)S(1)} collective-permute-done((s32[4]{0:T(128)S(1)}, s32[4]{0:T(128)S(1)}, u32[]{:S(2)}, u32[]{:S(2)}) %collective-permute-start.19) | collective-permute-done | bytes 48 | tf_op jit(solution)/shard_map/ppermute | solution.py:50
  118.4 1.7 %collective-permute-start.20 = (f32[4,32,2048]{2,1,0:T(8,128)S(1)}, f32[4,32,2048]{2,1,0:T(8,128)S(1)}, u32[]{:S(2)}, u32[]{:S(2)}) collective-permute-start(f32[4,32,2048]{2,1,0:T(8,128)S(1)} %shard_map.36), channel_id=1, source_target_pairs={{0,2},{2,0},{4,6},{6,4},{8,10},{10,8},{12,14},{14,12},{1,3},{3,1},... | collective-permute-start | bytes 3145736 | tf_op jit(solution)/shard_map/ppermute | solution.py:50
  120.1 1.8 %shard_map.35.whole_in = f32[4,32,4096]{2,1,0:T(8,128)} custom-call(s32[4]{0:T(128)S(1)} %copy-done.1, f32[13,32,2048]{2,1,0:T(8,128)S(1)} %get-tuple-element.33.window, f32[8,128]{1,0:T(8,128)S(1)} %add.31.squares), custom_call_target="tpu_custom_call" | custom-call | tf_op jit(solution)/shard_map/pallas_call | solution.py:468
  121.8 18.1 %collective-permute-done.20.other = f32[4,32,2048]{2,1,0:T(8,128)S(1)} collective-permute-done((f32[4,32,2048]{2,1,0:T(8,128)S(1)}, f32[4,32,2048]{2,1,0:T(8,128)S(1)}, u32[]{:S(2)}, u32[]{:S(2)}) %collective-permute-start.20) | collective-permute-done | bytes 1048608 | tf_op jit(solution)/shard_map/ppermute | solution.py:50
  (40 shorter events, 6.6 us)
Async XLA Ops:
  0.0 1.6 %copy-start = (f32[4,32,4096]{2,1,0:T(8,128)S(1)}, f32[4,32,4096]{2,1,0:T(8,128)}, u32[]{:S(2)}) copy-start(f32[4,32,4096]{2,1,0:T(8,128)} %x_ref.1) | copy-start | bytes 6291460
  1.8 16.5 %collective-permute-start = (f32[2,32,2176]{2,1,0:T(8,128)S(1)}, f32[2,32,2176]{2,1,0:T(8,128)S(1)}, u32[]{:S(2)}, u32[]{:S(2)}) collective-permute-start(f32[2,32,2176]{2,1,0:T(8,128)S(1)} %get-tuple-element.36), channel_id=1, source_target_pairs={{0,2},{2,0},{4,6},{6,4},{8,10},{10,8},{12,14},{14,12},{1,3},{3,1},... | collective-permute-start | bytes 1671176 | tf_op jit(solution)/shard_map/ppermute | solution.py:50
  4.9 35.1 %collective-permute-start.2 = (f32[4,32,2176]{2,1,0:T(8,128)S(1)}, f32[4,32,2176]{2,1,0:T(8,128)S(1)}, u32[]{:S(2)}, u32[]{:S(2)}) collective-permute-start(f32[4,32,2176]{2,1,0:T(8,128)S(1)} %get-tuple-element.20.refs_0_), channel_id=1, source_target_pairs={{2,6},{6,10},{10,14},{4,0},{8,4},{12,8},{3,7},{7,11},{11,15},{5,1}... | collective-permute-start | bytes 3342344 | tf_op jit(solution)/shard_map/ppermute | solution.py:406
  6.3 23.5 %collective-permute-start.4 = (f32[3,32,2176]{2,1,0:T(8,128)S(1)}, f32[3,32,2176]{2,1,0:T(8,128)S(1)}, u32[]{:S(2)}, u32[]{:S(2)}) collective-permute-start(f32[3,32,2176]{2,1,0:T(8,128)S(1)} %slice.23), channel_id=1, source_target_pairs={{0,4},{4,8},{8,12},{6,2},{10,6},{14,10},{1,5},{5,9},{9,13},{7,3},{... | collective-permute-start | bytes 2506760 | tf_op jit(solution)/shard_map/ppermute | solution.py:406
  10.9 18.6 %collective-permute-start.1 = (f32[2,32,2176]{2,1,0:T(8,128)S(1)}, f32[2,32,2176]{2,1,0:T(8,128)S(1)}, u32[]{:S(2)}, u32[]{:S(2)}) collective-permute-start(f32[2,32,2176]{2,1,0:T(8,128)S(1)} %get-tuple-element.35), channel_id=1, source_target_pairs={{0,2},{2,0},{4,6},{6,4},{8,10},{10,8},{12,14},{14,12},{1,3},{3,1},... | collective-permute-start | bytes 1671176 | tf_op jit(solution)/shard_map/ppermute | solution.py:50
  18.4 21.6 %collective-permute-start.3 = (f32[2,32,2176]{2,1,0:T(8,128)S(1)}, f32[2,32,2176]{2,1,0:T(8,128)S(1)}, u32[]{:S(2)}, u32[]{:S(2)}) collective-permute-start(f32[2,32,2176]{2,1,0:T(8,128)S(1)} %collective-permute-done.refs_1_), channel_id=1, source_target_pairs={{0,4},{4,8},{8,12},{6,2},{10,6},{14,10},{1,5},{5,9},{9,13},{7,3},{... | collective-permute-start | bytes 1671176 | tf_op jit(solution)/shard_map/ppermute | solution.py:406
  40.2 23.9 %collective-permute-start.5 = (f32[17,8,2176]{2,1,0:T(8,128)S(1)}, f32[17,8,2176]{2,1,0:T(8,128)S(1)}, u32[]{:S(2)}, u32[]{:S(2)}) collective-permute-start(f32[17,8,2176]{2,1,0:T(8,128)S(1)} %shard_map.29), channel_id=1, source_target_pairs={{0,1},{1,0},{2,3},{3,2},{4,5},{5,4},{6,7},{7,6},{8,9},{9,8},{10,11... | collective-permute-start | bytes 3551240 | tf_op jit(solution)/shard_map/ppermute | solution.py:87
  40.4 23.6 %collective-permute-start.11 = (f32[3,32,2176]{2,1,0:T(8,128)S(1)}, f32[3,32,2176]{2,1,0:T(8,128)S(1)}, u32[]{:S(2)}, u32[]{:S(2)}) collective-permute-start(f32[3,32,2176]{2,1,0:T(8,128)S(1)} %pad_maximum_fusion), channel_id=1, source_target_pairs={{2,6},{6,10},{10,14},{4,0},{8,4},{12,8},{3,7},{7,11},{11,15},{5,1}... | collective-permute-start | bytes 2506760 | tf_op jit(solution)/shard_map/ppermute | solution.py:406
  41.7 17.5 %collective-permute-start.10 = (f32[2,32,2176]{2,1,0:T(8,128)S(1)}, f32[2,32,2176]{2,1,0:T(8,128)S(1)}, u32[]{:S(2)}, u32[]{:S(2)}) collective-permute-start(f32[2,32,2176]{2,1,0:T(8,128)S(1)} %collective-permute-done.1.refs_2_), channel_id=1, source_target_pairs={{0,4},{4,8},{8,12},{6,2},{10,6},{14,10},{1,5},{5,9},{9,13},{7,3},{... | collective-permute-start | bytes 1671176 | tf_op jit(solution)/shard_map/ppermute | solution.py:406
  64.1 18.6 %collective-permute-start.12 = (f32[5,8,2176]{2,1,0:T(8,128)S(1)}, f32[5,8,2176]{2,1,0:T(8,128)S(1)}, u32[]{:S(2)}, u32[]{:S(2)}) collective-permute-start(f32[5,8,2176]{2,1,0:T(8,128)S(1)} %shard_map.31), channel_id=1, source_target_pairs={{0,1},{1,0},{2,3},{3,2},{4,5},{5,4},{6,7},{7,6},{8,9},{9,8},{10,11... | collective-permute-start | bytes 1044488 | tf_op jit(solution)/shard_map/ppermute | solution.py:87
  67.3 1.4 collective-permute-start.6
  68.7 3.7 %collective-permute-start.7 = (f32[2,16,128]{2,1,0:T(8,128)S(1)}, f32[2,16,128]{2,1,0:T(8,128)S(1)}, u32[]{:S(2)}, u32[]{:S(2)}) collective-permute-start(f32[2,16,128]{2,1,0:T(8,128)S(1)} %add.24), channel_id=1, source_target_pairs={{0,2},{2,0},{4,6},{6,4},{8,10},{10,8},{12,14},{14,12},{1,3},{3,1},... | collective-permute-start | bytes 49160 | tf_op jit(solution)/shard_map/ppermute | solution.py:64
  72.5 10.1 %collective-permute-start.8 = (f32[2,8,128]{2,1,0:T(8,128)S(1)}, f32[2,8,128]{2,1,0:T(8,128)S(1)}, u32[]{:S(2)}, u32[]{:S(2)}) collective-permute-start(f32[2,8,128]{2,1,0:T(8,128)S(1)} %slice.28), channel_id=1, source_target_pairs={{0,4},{2,6},{4,8},{6,10},{8,12},{10,14},{1,5},{3,7},{5,9},{7,11},{... | collective-permute-start | bytes 24584 | tf_op jit(solution)/shard_map/ppermute | solution.py:432
  76.1 6.5 %collective-permute-start.9 = (f32[2,8,128]{2,1,0:T(8,128)S(1)}, f32[2,8,128]{2,1,0:T(8,128)S(1)}, u32[]{:S(2)}, u32[]{:S(2)}) collective-permute-start(f32[2,8,128]{2,1,0:T(8,128)S(1)} %slice.28), channel_id=1, source_target_pairs={{4,0},{6,2},{8,4},{10,6},{12,8},{14,10},{5,1},{7,3},{9,5},{11,7},{... | collective-permute-start | bytes 24584 | tf_op jit(solution)/shard_map/ppermute | solution.py:433
  91.3 1.3 collective-permute-start.13
  92.5 3.8 %collective-permute-start.14 = (f32[2,24,128]{2,1,0:T(8,128)S(1)}, f32[2,24,128]{2,1,0:T(8,128)S(1)}, u32[]{:S(2)}, u32[]{:S(2)}) collective-permute-start(f32[2,24,128]{2,1,0:T(8,128)S(1)} %add.26), channel_id=1, source_target_pairs={{0,2},{2,0},{4,6},{6,4},{8,10},{10,8},{12,14},{14,12},{1,3},{3,1},... | collective-permute-start | bytes 73736 | tf_op jit(solution)/shard_map/ppermute | solution.py:64
  96.4 17.6 %copy-start.1 = (s32[4]{0:T(128)S(1)}, s32[4]{0:T(128)}, u32[]{:S(2)}) copy-start(s32[4]{0:T(128)} %bracket.1) | copy-start | bytes 52
  101.9 1.2 collective-permute-start.15
  103.1 3.6 %collective-permute-start.16 = (f32[8,128]{1,0:T(8,128)S(1)}, f32[8,128]{1,0:T(8,128)S(1)}, u32[]{:S(2)}, u32[]{:S(2)}) collective-permute-start(f32[8,128]{1,0:T(8,128)S(1)} %add.28), channel_id=1, source_target_pairs={{0,2},{2,0},{4,6},{6,4},{8,10},{10,8},{12,14},{14,12},{1,3},{3,1},... | collective-permute-start | bytes 12296 | tf_op jit(solution)/shard_map/ppermute | solution.py:64
  106.7 4.2 %collective-permute-start.17 = (f32[8,128]{1,0:T(8,128)S(1)}, f32[8,128]{1,0:T(8,128)S(1)}, u32[]{:S(2)}, u32[]{:S(2)}) collective-permute-start(f32[8,128]{1,0:T(8,128)S(1)} %add.29), channel_id=1, source_target_pairs={{0,4},{2,6},{4,0},{6,2},{8,12},{10,14},{12,8},{14,10},{1,5},{3,7},... | collective-permute-start | bytes 12296 | tf_op jit(solution)/shard_map/ppermute | solution.py:64
  111.0 4.7 %collective-permute-start.18 = (f32[8,128]{1,0:T(8,128)S(1)}, f32[8,128]{1,0:T(8,128)S(1)}, u32[]{:S(2)}, u32[]{:S(2)}) collective-permute-start(f32[8,128]{1,0:T(8,128)S(1)} %add.30), channel_id=1, source_target_pairs={{0,8},{2,10},{4,12},{6,14},{8,0},{10,2},{12,4},{14,6},{1,9},{3,11}... | collective-permute-start | bytes 12296 | tf_op jit(solution)/shard_map/ppermute | solution.py:64
  114.0 3.6 %collective-permute-start.19 = (s32[4]{0:T(128)S(1)}, s32[4]{0:T(128)S(1)}, u32[]{:S(2)}, u32[]{:S(2)}) collective-permute-start(s32[4]{0:T(128)S(1)} %copy-done.1), channel_id=1, source_target_pairs={{0,2},{2,0},{4,6},{6,4},{8,10},{10,8},{12,14},{14,12},{1,3},{3,1},... | collective-permute-start | bytes 56 | tf_op jit(solution)/shard_map/ppermute | solution.py:50
  118.4 21.6 %collective-permute-start.20 = (f32[4,32,2048]{2,1,0:T(8,128)S(1)}, f32[4,32,2048]{2,1,0:T(8,128)S(1)}, u32[]{:S(2)}, u32[]{:S(2)}) collective-permute-start(f32[4,32,2048]{2,1,0:T(8,128)S(1)} %shard_map.36), channel_id=1, source_target_pairs={{0,2},{2,0},{4,6},{6,4},{8,10},{10,8},{12,14},{14,12},{1,3},{3,1},... | collective-permute-start | bytes 3145736 | tf_op jit(solution)/shard_map/ppermute | solution.py:50

commit v6 on v5

--- a/solution.py
+++ b/solution.py
@@ -19,6 +19,7 @@
 LOW = 2 * ITERS + REACH
 HIGH = 2 * ITERS + REACH + 1
 FAR = 3
+SHARED = 2
 EDGE = 2 * ITERS
 CHUNKS = (0, 2)
 VMEM_LIMIT = 4 * 1024 * 1024
@@ -269,7 +270,7 @@
     drift_pass(new_phi, new_drift, new_norms, LOW + 1, top - 1, first, count, rows)
 
 
-def middle_outer_kernel(norms, near_late, far_early, far_late, rows_early, rows_late, *refs, count, local):
+def middle_outer_kernel(norms, near_late, far_early, far_extra, far_late, rows_late, *refs, count, local):
     phi, theta, new_phi, new_drift, new_norms, speeds = refs[5:]
     rows = near_late.shape[1]
     hi, lo = pair_position()
@@ -283,7 +284,8 @@
         low_at, high_at = LOW - 1 - local - i, top + local + i
         at = FAR - 1 - i
         late, late_rows = far_late.at[at], rows_late.at[local - done + at]
-        early, early_rows = far_early.at[at], rows_early.at[3 * local + done + at]
+        early = far_early.at[SHARED - 1 - i] if i < SHARED else far_extra.at[FAR - 1 - i]
+        early_rows = rows_late.at[local - done + FAR + (SHARED - 1 - i if i < SHARED else FAR - 1 - i + SHARED)]
 
         @pl.when(lo == 1)
         def _():
@@ -412,11 +414,12 @@
     recv = [swap_pairs(send[a:b]) for a, b in zip(CHUNKS, ends)]
     other_bracket = swap_pairs(bracket)
     near_early = move(keep, (1,), (0,))
-    far_early = move(keep[local - FAR :], (0,), (1,))
+    far_early = move(keep[local - SHARED :], (0,), (1,))
     near_late = [move(value, (0,), (1,)) for value in recv]
     far_late = move(jnp.concatenate(recv, axis=0)[local - FAR :], (1,), (0,))
-    rows_early = neighbour_rows([keep] + recv + [near_early, near_late[0], far_early])
-    rows_late = neighbour_rows([near_late[1], far_late])
+    far_extra = move(keep[local - FAR : local - SHARED], (), (1,))
+    rows_early = neighbour_rows([keep] + recv + [near_early, near_late[0]])
+    rows_late = neighbour_rows([near_late[1], far_late, far_early, far_extra])
     held = shape((window, rows + 2 * EDGE, wide))
     lines = -(-window // SUBLANES) * SUBLANES
     norm_shape = shape((2, lines, LANES))
@@ -438,7 +441,7 @@
     )(phi, drift, norms)
     pad = jnp.zeros((2, lines - window, LANES), F32)
     norms = jnp.concatenate([low_norms[:, PAIR * local - LOW :], own_norms, high_norms[:, :HIGH], pad], axis=1)
-    operands = [norms, near_late[1], far_early, far_late, rows_early, rows_late]
+    operands = [norms, near_late[1], far_early, far_extra, far_late, rows_late]
     _, _, phi, drift, norms = call(
         functools.partial(middle_outer_kernel, count=count, local=local),
         (held, held, held, held, norm_shape), scratch=[pltpu.VMEM((lines, LANES), F32)],

time: 141 us -> 145 us (1.028)
  starting transfers between devices: 38.2 us -> 48.4 us
  waiting for transfers between devices: 74.2 us -> 68 us
    ppermute x5, starting transfers between devices: 9.85 us -> 18.3 us  [small_sum(): lax.ppermute(value, 'img', [(i, i ^ step) for i in range(count)])]
    ppermute x5 -> x6, waiting for transfers between devices: 27.8 us -> 22.2 us  [per_device(): lax.ppermute(value, 'img', [p for p in ahead if p[0] % PAIR in up] + [p f...]
    ppermute x4, starting transfers between devices: 6.47 us -> 10 us  [swap_pairs(): return lax.ppermute(value, 'img', [(i, i ^ 1) for i in range(count)])]
    ppermute x5, waiting for transfers between devices: 8.6 us -> 6.69 us  [small_sum(): lax.ppermute(value, 'img', [(i, i ^ step) for i in range(count)])]
    ppermute x5 -> x6, starting transfers between devices: 16.2 us -> 14.6 us  [per_device(): lax.ppermute(value, 'img', [p for p in ahead if p[0] % PAIR in up] + [p f...]
  transfers between devices with their start and end apart: 21 -> 22, of which waited for: 15 -> 15; matrix products, arithmetic and copies ran while one was open for 0% -> 0% of each run, Pallas kernels for 7% -> 7%
where the time goes in v6:
time: 145 us
  waiting for transfers between devices  68 us (47%)
  starting transfers between devices  48.4 us (33%)
  Pallas kernels  26.1 us (18%)
  local copies, waits for them, and re-layouts  1.81 us (1%)
    ppermute x4, waiting for transfers between devices, swap_pairs(): return lax.ppermute(value, 'img', [(i, i ^ 1) for i in range(count)])  36 us
    ppermute x6, waiting for transfers between devices, per_device(): lax.ppermute(value, 'img', [p for p in ahead if p[0] % PAIR in up] + [p f...  22.2 us
    ppermute x5, starting transfers between devices, small_sum(): lax.ppermute(value, 'img', [(i, i ^ step) for i in range(count)])  18.3 us
    ppermute x6, starting transfers between devices, per_device(): lax.ppermute(value, 'img', [p for p in ahead if p[0] % PAIR in up] + [p f...  14.6 us
    ppermute x4, starting transfers between devices, swap_pairs(): return lax.ppermute(value, 'img', [(i, i ^ 1) for i in range(count)])  10 us
    pallas_call x1, Pallas kernels, per_device(): call(functools.partial(middle_outer_kernel, count=count, local=local), (h...  8.59 us
    ppermute x5, waiting for transfers between devices, small_sum(): lax.ppermute(value, 'img', [(i, i ^ step) for i in range(count)])  6.69 us
    pallas_call x1, Pallas kernels, per_device(): call(functools.partial(last_kernel, count=count, local=local, rows=rows,...  5.38 us
  transfers between devices with their start and end apart: 22, of which 15 were waited for; matrix products, arithmetic and copies ran while one was open for 0% of the time, Pallas kernels for 7%

profile of v6, /device:TPU:0, one launch (start us, length us, event | category | flops | bytes accessed | tf_op | source)
XLA Modules:
  0.0 144.8 jit_solution(3016680464503536145)
XLA Ops:
  0.0 1.6 %copy-done = f32[4,32,4096]{2,1,0:T(8,128)S(1)} copy-done((f32[4,32,4096]{2,1,0:T(8,128)S(1)}, f32[4,32,4096]{2,1,0:T(8,128)}, u32[]{:S(2)}) %copy-start) | copy-done | bytes 2097176
  1.8 3.1 %collective-permute-start = (f32[2,32,2176]{2,1,0:T(8,128)S(1)}, f32[2,32,2176]{2,1,0:T(8,128)S(1)}, u32[]{:S(2)}, u32[]{:S(2)}) collective-permute-start(f32[2,32,2176]{2,1,0:T(8,128)S(1)} %get-tuple-element.36), channel_id=1, source_target_pairs={{0,2},{2,0},{4,6},{6,4},{8,10},{10,8},{12,14},{14,12},{1,3},{3,1},... | collective-permute-start | bytes 1671176 | tf_op jit(solution)/shard_map/ppermute | solution.py:51
  6.2 2.8 %collective-permute-start.1 = (f32[2,32,2176]{2,1,0:T(8,128)S(1)}, f32[2,32,2176]{2,1,0:T(8,128)S(1)}, u32[]{:S(2)}, u32[]{:S(2)}) collective-permute-start(f32[2,32,2176]{2,1,0:T(8,128)S(1)} %get-tuple-element.35), channel_id=1, source_target_pairs={{0,2},{2,0},{4,6},{6,4},{8,10},{10,8},{12,14},{14,12},{1,3},{3,1},... | collective-permute-start | bytes 1671176 | tf_op jit(solution)/shard_map/ppermute | solution.py:51
  9.0 9.4 %collective-permute-done.refs_1_ = f32[2,32,2176]{2,1,0:T(8,128)S(1)} collective-permute-done((f32[2,32,2176]{2,1,0:T(8,128)S(1)}, f32[2,32,2176]{2,1,0:T(8,128)S(1)}, u32[]{:S(2)}, u32[]{:S(2)}) %collective-permute-start) | collective-permute-done | bytes 557088 | tf_op jit(solution)/shard_map/ppermute | solution.py:51
  18.4 4.0 %collective-permute-start.3 = (f32[2,32,2176]{2,1,0:T(8,128)S(1)}, f32[2,32,2176]{2,1,0:T(8,128)S(1)}, u32[]{:S(2)}, u32[]{:S(2)}) collective-permute-start(f32[2,32,2176]{2,1,0:T(8,128)S(1)} %collective-permute-done.refs_1_), channel_id=1, source_target_pairs={{0,4},{4,8},{8,12},{6,2},{10,6},{14,10},{1,5},{5,9},{9,13},{7,3},{... | collective-permute-start | bytes 1671176 | tf_op jit(solution)/shard_map/ppermute | solution.py:408
  22.4 7.1 %collective-permute-done.1.refs_2_ = f32[2,32,2176]{2,1,0:T(8,128)S(1)} collective-permute-done((f32[2,32,2176]{2,1,0:T(8,128)S(1)}, f32[2,32,2176]{2,1,0:T(8,128)S(1)}, u32[]{:S(2)}, u32[]{:S(2)}) %collective-permute-start.1) | collective-permute-done | bytes 557088 | tf_op jit(solution)/shard_map/ppermute | solution.py:51
  29.5 1.3 collective-permute-start.12
  30.8 1.4 collective-permute-done.3.refs_4_
  33.1 3.9 %collective-permute-start.10 = (f32[2,32,2176]{2,1,0:T(8,128)S(1)}, f32[2,32,2176]{2,1,0:T(8,128)S(1)}, u32[]{:S(2)}, u32[]{:S(2)}) collective-permute-start(f32[2,32,2176]{2,1,0:T(8,128)S(1)} %slice.29), channel_id=1, source_target_pairs={{0,4},{4,8},{8,12},{6,2},{10,6},{14,10},{1,5},{5,9},{9,13},{7,3},{... | collective-permute-start | bytes 1671176 | tf_op jit(solution)/shard_map/ppermute | solution.py:408
  37.0 3.5 %collective-permute-start.9 = (f32[2,32,2176]{2,1,0:T(8,128)S(1)}, f32[2,32,2176]{2,1,0:T(8,128)S(1)}, u32[]{:S(2)}, u32[]{:S(2)}) collective-permute-start(f32[2,32,2176]{2,1,0:T(8,128)S(1)} %collective-permute-done.1.refs_2_), channel_id=1, source_target_pairs={{0,4},{4,8},{8,12},{6,2},{10,6},{14,10},{1,5},{5,9},{9,13},{7,3},{... | collective-permute-start | bytes 1671176 | tf_op jit(solution)/shard_map/ppermute | solution.py:408
  41.2 8.7 %collective-permute-done.10.refs_2_.far_early = f32[2,32,2176]{2,1,0:T(8,128)S(1)} collective-permute-done((f32[2,32,2176]{2,1,0:T(8,128)S(1)}, f32[2,32,2176]{2,1,0:T(8,128)S(1)}, u32[]{:S(2)}, u32[]{:S(2)}) %collective-permute-start.10) | collective-permute-done | bytes 557088 | tf_op jit(solution)/shard_map/ppermute | solution.py:408
  49.9 11.5 %collective-permute-done.9.refs_0_.near_late = f32[2,32,2176]{2,1,0:T(8,128)S(1)} collective-permute-done((f32[2,32,2176]{2,1,0:T(8,128)S(1)}, f32[2,32,2176]{2,1,0:T(8,128)S(1)}, u32[]{:S(2)}, u32[]{:S(2)}) %collective-permute-start.9) | collective-permute-done | bytes 557088 | tf_op jit(solution)/shard_map/ppermute | solution.py:408
  61.6 3.1 %shard_map.30 = (f32[21,40,2176]{2,1,0:T(8,128)S(1)}, f32[21,40,2176]{2,1,0:T(8,128)S(1)}, f32[2,16,128]{2,1,0:T(8,128)S(1)}) custom-call(f32[4,32,2176]{2,1,0:T(8,128)S(1)} %get-tuple-element.20.refs_0_, f32[2,32,2176]{2,1,0:T(8,128)S(1)} %collective-permute-done.refs_1_, f32[2,32,2176]{2,1,0:T(8,128)S(1)} %collective-permute-done.1.refs_2_, ...), custom_call_target="tpu_custom_call" | custom-call | tf_op jit(solution)/shard_map/pallas_call | solution.py:429
  66.1 8.6 %collective-permute-start.6 = (f32[2,16,128]{2,1,0:T(8,128)S(1)}, f32[2,16,128]{2,1,0:T(8,128)S(1)}, u32[]{:S(2)}, u32[]{:S(2)}) collective-permute-start(f32[2,16,128]{2,1,0:T(8,128)S(1)} %add.24), channel_id=1, source_target_pairs={{0,2},{2,0},{4,6},{6,4},{8,10},{10,8},{12,14},{14,12},{1,3},{3,1},... | collective-permute-start | bytes 49160 | tf_op jit(solution)/shard_map/ppermute | solution.py:65
  74.7 1.7 %collective-permute-done.6 = f32[2,16,128]{2,1,0:T(8,128)S(1)} collective-permute-done((f32[2,16,128]{2,1,0:T(8,128)S(1)}, f32[2,16,128]{2,1,0:T(8,128)S(1)}, u32[]{:S(2)}, u32[]{:S(2)}) %collective-permute-start.6) | collective-permute-done | bytes 16416 | tf_op jit(solution)/shard_map/ppermute | solution.py:65
  76.4 3.4 %collective-permute-start.7 = (f32[2,8,128]{2,1,0:T(8,128)S(1)}, f32[2,8,128]{2,1,0:T(8,128)S(1)}, u32[]{:S(2)}, u32[]{:S(2)}) collective-permute-start(f32[2,8,128]{2,1,0:T(8,128)S(1)} %slice.32), channel_id=1, source_target_pairs={{0,4},{2,6},{4,8},{6,10},{8,12},{10,14},{1,5},{3,7},{5,9},{7,11},{... | collective-permute-start | bytes 24584 | tf_op jit(solution)/shard_map/ppermute | solution.py:435
  79.9 1.3 collective-permute-start.8
  81.3 5.0 %shard_map.32 = (f32[21,40,2176]{2,1,0:T(8,128)S(1)}, f32[21,40,2176]{2,1,0:T(8,128)S(1)}, f32[21,40,2176]{2,1,0:T(8,128)S(1)}, f32[21,40,2176]{2,1,0:T(8,128)S(1)}, f32[2,24,128]{2,1,0:T(8,128)S(1)}) custom-call(f32[21,40,2176]{2,1,0:T(8,128)S(1)} %get-tuple-element.23._, ...), custom_call_target="tpu_custom_call", output_to_operand_aliasing={{0}: (0, {}), {1}: (1, {})} | custom-call | tf_op jit(solution)/shard_map/pallas_call | solution.py:437
  86.4 8.6 %shard_map.33 = (f32[21,40,2176]{2,1,0:T(8,128)S(1)}, f32[21,40,2176]{2,1,0:T(8,128)S(1)}, f32[21,40,2176]{2,1,0:T(8,128)S(1)}, f32[21,40,2176]{2,1,0:T(8,128)S(1)}, f32[2,24,128]{2,1,0:T(8,128)S(1)}) custom-call(f32[2,24,128]{2,1,0:T(8,128)S(1)} %maximum_maximum_fusion.norms, ...), custom_call_target="tpu_custom_call", output_to_operand_aliasing={{0}: (6, {}), {1}: (7, {}), {2}: (8, {}), {3}: (9, {}), {4}... | custom-call | tf_op jit(solution)/shard_map/pallas_call | solution.py:445
  96.3 2.0 %collective-permute-start.15 = (f32[2,24,128]{2,1,0:T(8,128)S(1)}, f32[2,24,128]{2,1,0:T(8,128)S(1)}, u32[]{:S(2)}, u32[]{:S(2)}) collective-permute-start(f32[2,24,128]{2,1,0:T(8,128)S(1)} %add.26), channel_id=1, source_target_pairs={{0,2},{2,0},{4,6},{6,4},{8,10},{10,8},{12,14},{14,12},{1,3},{3,1},... | collective-permute-start | bytes 73736 | tf_op jit(solution)/shard_map/ppermute | solution.py:65
  98.3 1.8 %collective-permute-done.15 = f32[2,24,128]{2,1,0:T(8,128)S(1)} collective-permute-done((f32[2,24,128]{2,1,0:T(8,128)S(1)}, f32[2,24,128]{2,1,0:T(8,128)S(1)}, u32[]{:S(2)}, u32[]{:S(2)}) %collective-permute-start.15) | collective-permute-done | bytes 24608 | tf_op jit(solution)/shard_map/ppermute | solution.py:65
  100.1 5.4 %shard_map.34 = (f32[13,32,2048]{2,1,0:T(8,128)S(1)}, f32[8,128]{1,0:T(8,128)S(1)}, f32[21,40,2176]{2,1,0:T(8,128)S(1)}) custom-call(f32[21,40,2176]{2,1,0:T(8,128)S(1)} %get-tuple-element.30.phi, f32[21,40,2176]{2,1,0:T(8,128)S(1)} %get-tuple-element.31._, f32[2,24,128]{2,1,0:T(8,128)S(1)} %add.27.norms), custom_call_target="tpu_custom_call", output_to_operand_aliasing={{2}: (1, {})} | custom-call | tf_op jit(solution)/shard_map/pallas_call | solution.py:452
  106.7 2.0 %collective-permute-start.17 = (f32[8,128]{1,0:T(8,128)S(1)}, f32[8,128]{1,0:T(8,128)S(1)}, u32[]{:S(2)}, u32[]{:S(2)}) collective-permute-start(f32[8,128]{1,0:T(8,128)S(1)} %add.28), channel_id=1, source_target_pairs={{0,2},{2,0},{4,6},{6,4},{8,10},{10,8},{12,14},{14,12},{1,3},{3,1},... | collective-permute-start | bytes 12296 | tf_op jit(solution)/shard_map/ppermute | solution.py:65
  108.7 1.6 %collective-permute-done.17 = f32[8,128]{1,0:T(8,128)S(1)} collective-permute-done((f32[8,128]{1,0:T(8,128)S(1)}, f32[8,128]{1,0:T(8,128)S(1)}, u32[]{:S(2)}, u32[]{:S(2)}) %collective-permute-start.17) | collective-permute-done | bytes 4128 | tf_op jit(solution)/shard_map/ppermute | solution.py:65
  110.3 2.6 %collective-permute-start.18 = (f32[8,128]{1,0:T(8,128)S(1)}, f32[8,128]{1,0:T(8,128)S(1)}, u32[]{:S(2)}, u32[]{:S(2)}) collective-permute-start(f32[8,128]{1,0:T(8,128)S(1)} %add.29), channel_id=1, source_target_pairs={{0,4},{2,6},{4,0},{6,2},{8,12},{10,14},{12,8},{14,10},{1,5},{3,7},... | collective-permute-start | bytes 12296 | tf_op jit(solution)/shard_map/ppermute | solution.py:65
  113.0 1.6 %collective-permute-done.18 = f32[8,128]{1,0:T(8,128)S(1)} collective-permute-done((f32[8,128]{1,0:T(8,128)S(1)}, f32[8,128]{1,0:T(8,128)S(1)}, u32[]{:S(2)}, u32[]{:S(2)}) %collective-permute-start.18) | collective-permute-done | bytes 4128 | tf_op jit(solution)/shard_map/ppermute | solution.py:65
  114.5 3.0 %collective-permute-start.19 = (f32[8,128]{1,0:T(8,128)S(1)}, f32[8,128]{1,0:T(8,128)S(1)}, u32[]{:S(2)}, u32[]{:S(2)}) collective-permute-start(f32[8,128]{1,0:T(8,128)S(1)} %add.30), channel_id=1, source_target_pairs={{0,8},{2,10},{4,12},{6,14},{8,0},{10,2},{12,4},{14,6},{1,9},{3,11}... | collective-permute-start | bytes 12296 | tf_op jit(solution)/shard_map/ppermute | solution.py:65
  117.6 2.0 %collective-permute-start.20 = (s32[4]{0:T(128)S(1)}, s32[4]{0:T(128)S(1)}, u32[]{:S(2)}, u32[]{:S(2)}) collective-permute-start(s32[4]{0:T(128)S(1)} %copy-done.1), channel_id=1, source_target_pairs={{0,2},{2,0},{4,6},{6,4},{8,10},{10,8},{12,14},{14,12},{1,3},{3,1},... | collective-permute-start | bytes 56 | tf_op jit(solution)/shard_map/ppermute | solution.py:51
  119.6 1.5 %collective-permute-done.20.bracket = s32[4]{0:T(128)S(1)} collective-permute-done((s32[4]{0:T(128)S(1)}, s32[4]{0:T(128)S(1)}, u32[]{:S(2)}, u32[]{:S(2)}) %collective-permute-start.20) | collective-permute-done | bytes 48 | tf_op jit(solution)/shard_map/ppermute | solution.py:51
  122.0 2.1 %collective-permute-start.21 = (f32[4,32,2048]{2,1,0:T(8,128)S(1)}, f32[4,32,2048]{2,1,0:T(8,128)S(1)}, u32[]{:S(2)}, u32[]{:S(2)}) collective-permute-start(f32[4,32,2048]{2,1,0:T(8,128)S(1)} %shard_map.36), channel_id=1, source_target_pairs={{0,2},{2,0},{4,6},{6,4},{8,10},{10,8},{12,14},{14,12},{1,3},{3,1},... | collective-permute-start | bytes 3145736 | tf_op jit(solution)/shard_map/ppermute | solution.py:51
  124.0 1.8 %shard_map.35.whole_in = f32[4,32,4096]{2,1,0:T(8,128)} custom-call(s32[4]{0:T(128)S(1)} %copy-done.1, f32[13,32,2048]{2,1,0:T(8,128)S(1)} %get-tuple-element.33.window, f32[8,128]{1,0:T(8,128)S(1)} %add.31.squares), custom_call_target="tpu_custom_call" | custom-call | tf_op jit(solution)/shard_map/pallas_call | solution.py:471
  125.8 18.0 %collective-permute-done.21.other = f32[4,32,2048]{2,1,0:T(8,128)S(1)} collective-permute-done((f32[4,32,2048]{2,1,0:T(8,128)S(1)}, f32[4,32,2048]{2,1,0:T(8,128)S(1)}, u32[]{:S(2)}, u32[]{:S(2)}) %collective-permute-start.21) | collective-permute-done | bytes 1048608 | tf_op jit(solution)/shard_map/ppermute | solution.py:51
  (43 shorter events, 9.1 us)
Async XLA Ops:
  0.0 1.6 %copy-start = (f32[4,32,4096]{2,1,0:T(8,128)S(1)}, f32[4,32,4096]{2,1,0:T(8,128)}, u32[]{:S(2)}) copy-start(f32[4,32,4096]{2,1,0:T(8,128)} %x_ref.1) | copy-start | bytes 6291460
  1.8 16.5 %collective-permute-start = (f32[2,32,2176]{2,1,0:T(8,128)S(1)}, f32[2,32,2176]{2,1,0:T(8,128)S(1)}, u32[]{:S(2)}, u32[]{:S(2)}) collective-permute-start(f32[2,32,2176]{2,1,0:T(8,128)S(1)} %get-tuple-element.36), channel_id=1, source_target_pairs={{0,2},{2,0},{4,6},{6,4},{8,10},{10,8},{12,14},{14,12},{1,3},{3,1},... | collective-permute-start | bytes 1671176 | tf_op jit(solution)/shard_map/ppermute | solution.py:51
  4.9 27.9 %collective-permute-start.2 = (f32[4,32,2176]{2,1,0:T(8,128)S(1)}, f32[4,32,2176]{2,1,0:T(8,128)S(1)}, u32[]{:S(2)}, u32[]{:S(2)}) collective-permute-start(f32[4,32,2176]{2,1,0:T(8,128)S(1)} %get-tuple-element.20.refs_0_), channel_id=1, source_target_pairs={{2,6},{6,10},{10,14},{4,0},{8,4},{12,8},{3,7},{7,11},{11,15},{5,1}... | collective-permute-start | bytes 3342344 | tf_op jit(solution)/shard_map/ppermute | solution.py:408
  6.2 23.3 %collective-permute-start.1 = (f32[2,32,2176]{2,1,0:T(8,128)S(1)}, f32[2,32,2176]{2,1,0:T(8,128)S(1)}, u32[]{:S(2)}, u32[]{:S(2)}) collective-permute-start(f32[2,32,2176]{2,1,0:T(8,128)S(1)} %get-tuple-element.35), channel_id=1, source_target_pairs={{0,2},{2,0},{4,6},{6,4},{8,10},{10,8},{12,14},{14,12},{1,3},{3,1},... | collective-permute-start | bytes 1671176 | tf_op jit(solution)/shard_map/ppermute | solution.py:51
  18.4 13.9 %collective-permute-start.3 = (f32[2,32,2176]{2,1,0:T(8,128)S(1)}, f32[2,32,2176]{2,1,0:T(8,128)S(1)}, u32[]{:S(2)}, u32[]{:S(2)}) collective-permute-start(f32[2,32,2176]{2,1,0:T(8,128)S(1)} %collective-permute-done.refs_1_), channel_id=1, source_target_pairs={{0,4},{4,8},{8,12},{6,2},{10,6},{14,10},{1,5},{5,9},{9,13},{7,3},{... | collective-permute-start | bytes 1671176 | tf_op jit(solution)/shard_map/ppermute | solution.py:408
  29.5 31.9 %collective-permute-start.12 = (f32[3,32,2176]{2,1,0:T(8,128)S(1)}, f32[3,32,2176]{2,1,0:T(8,128)S(1)}, u32[]{:S(2)}, u32[]{:S(2)}) collective-permute-start(f32[3,32,2176]{2,1,0:T(8,128)S(1)} %pad_maximum_fusion), channel_id=1, source_target_pairs={{2,6},{6,10},{10,14},{4,0},{8,4},{12,8},{3,7},{7,11},{11,15},{5,1}... | collective-permute-start | bytes 2506760 | tf_op jit(solution)/shard_map/ppermute | solution.py:408
  33.0 28.6 %collective-permute-start.4 = (f32[14,8,2176]{2,1,0:T(8,128)S(1)}, f32[14,8,2176]{2,1,0:T(8,128)S(1)}, u32[]{:S(2)}, u32[]{:S(2)}) collective-permute-start(f32[14,8,2176]{2,1,0:T(8,128)S(1)} %shard_map.29), channel_id=1, source_target_pairs={{0,1},{1,0},{2,3},{3,2},{4,5},{5,4},{6,7},{7,6},{8,9},{9,8},{10,11... | collective-permute-start | bytes 2924552 | tf_op jit(solution)/shard_map/ppermute | solution.py:88
  33.1 16.8 %collective-permute-start.10 = (f32[2,32,2176]{2,1,0:T(8,128)S(1)}, f32[2,32,2176]{2,1,0:T(8,128)S(1)}, u32[]{:S(2)}, u32[]{:S(2)}) collective-permute-start(f32[2,32,2176]{2,1,0:T(8,128)S(1)} %slice.29), channel_id=1, source_target_pairs={{0,4},{4,8},{8,12},{6,2},{10,6},{14,10},{1,5},{5,9},{9,13},{7,3},{... | collective-permute-start | bytes 1671176 | tf_op jit(solution)/shard_map/ppermute | solution.py:408
  37.0 24.4 %collective-permute-start.9 = (f32[2,32,2176]{2,1,0:T(8,128)S(1)}, f32[2,32,2176]{2,1,0:T(8,128)S(1)}, u32[]{:S(2)}, u32[]{:S(2)}) collective-permute-start(f32[2,32,2176]{2,1,0:T(8,128)S(1)} %collective-permute-done.1.refs_2_), channel_id=1, source_target_pairs={{0,4},{4,8},{8,12},{6,2},{10,6},{14,10},{1,5},{5,9},{9,13},{7,3},{... | collective-permute-start | bytes 1671176 | tf_op jit(solution)/shard_map/ppermute | solution.py:408
  40.5 0.7 collective-permute-start.11
  61.5 24.9 %collective-permute-start.13 = (f32[8,8,2176]{2,1,0:T(8,128)S(1)}, f32[8,8,2176]{2,1,0:T(8,128)S(1)}, u32[]{:S(2)}, u32[]{:S(2)}) collective-permute-start(f32[8,8,2176]{2,1,0:T(8,128)S(1)} %shard_map.31), channel_id=1, source_target_pairs={{0,1},{1,0},{2,3},{3,2},{4,5},{5,4},{6,7},{7,6},{8,9},{9,8},{10,11... | collective-permute-start | bytes 1671176 | tf_op jit(solution)/shard_map/ppermute | solution.py:88
  64.7 1.4 collective-permute-start.5
  66.1 10.3 %collective-permute-start.6 = (f32[2,16,128]{2,1,0:T(8,128)S(1)}, f32[2,16,128]{2,1,0:T(8,128)S(1)}, u32[]{:S(2)}, u32[]{:S(2)}) collective-permute-start(f32[2,16,128]{2,1,0:T(8,128)S(1)} %add.24), channel_id=1, source_target_pairs={{0,2},{2,0},{4,6},{6,4},{8,10},{10,8},{12,14},{14,12},{1,3},{3,1},... | collective-permute-start | bytes 49160 | tf_op jit(solution)/shard_map/ppermute | solution.py:65
  76.4 9.9 %collective-permute-start.7 = (f32[2,8,128]{2,1,0:T(8,128)S(1)}, f32[2,8,128]{2,1,0:T(8,128)S(1)}, u32[]{:S(2)}, u32[]{:S(2)}) collective-permute-start(f32[2,8,128]{2,1,0:T(8,128)S(1)} %slice.32), channel_id=1, source_target_pairs={{0,4},{2,6},{4,8},{6,10},{8,12},{10,14},{1,5},{3,7},{5,9},{7,11},{... | collective-permute-start | bytes 24584 | tf_op jit(solution)/shard_map/ppermute | solution.py:435
  79.9 6.5 %collective-permute-start.8 = (f32[2,8,128]{2,1,0:T(8,128)S(1)}, f32[2,8,128]{2,1,0:T(8,128)S(1)}, u32[]{:S(2)}, u32[]{:S(2)}) collective-permute-start(f32[2,8,128]{2,1,0:T(8,128)S(1)} %slice.32), channel_id=1, source_target_pairs={{4,0},{6,2},{8,4},{10,6},{12,8},{14,10},{5,1},{7,3},{9,5},{11,7},{... | collective-permute-start | bytes 24584 | tf_op jit(solution)/shard_map/ppermute | solution.py:436
  95.0 1.3 collective-permute-start.14
  96.3 3.8 %collective-permute-start.15 = (f32[2,24,128]{2,1,0:T(8,128)S(1)}, f32[2,24,128]{2,1,0:T(8,128)S(1)}, u32[]{:S(2)}, u32[]{:S(2)}) collective-permute-start(f32[2,24,128]{2,1,0:T(8,128)S(1)} %add.26), channel_id=1, source_target_pairs={{0,2},{2,0},{4,6},{6,4},{8,10},{10,8},{12,14},{14,12},{1,3},{3,1},... | collective-permute-start | bytes 73736 | tf_op jit(solution)/shard_map/ppermute | solution.py:65
  100.1 17.4 %copy-start.1 = (s32[4]{0:T(128)S(1)}, s32[4]{0:T(128)}, u32[]{:S(2)}) copy-start(s32[4]{0:T(128)} %bracket.1) | copy-start | bytes 52
  105.5 1.2 collective-permute-start.16
  106.7 3.6 %collective-permute-start.17 = (f32[8,128]{1,0:T(8,128)S(1)}, f32[8,128]{1,0:T(8,128)S(1)}, u32[]{:S(2)}, u32[]{:S(2)}) collective-permute-start(f32[8,128]{1,0:T(8,128)S(1)} %add.28), channel_id=1, source_target_pairs={{0,2},{2,0},{4,6},{6,4},{8,10},{10,8},{12,14},{14,12},{1,3},{3,1},... | collective-permute-start | bytes 12296 | tf_op jit(solution)/shard_map/ppermute | solution.py:65
  110.3 4.2 %collective-permute-start.18 = (f32[8,128]{1,0:T(8,128)S(1)}, f32[8,128]{1,0:T(8,128)S(1)}, u32[]{:S(2)}, u32[]{:S(2)}) collective-permute-start(f32[8,128]{1,0:T(8,128)S(1)} %add.29), channel_id=1, source_target_pairs={{0,4},{2,6},{4,0},{6,2},{8,12},{10,14},{12,8},{14,10},{1,5},{3,7},... | collective-permute-start | bytes 12296 | tf_op jit(solution)/shard_map/ppermute | solution.py:65
  114.5 5.1 %collective-permute-start.19 = (f32[8,128]{1,0:T(8,128)S(1)}, f32[8,128]{1,0:T(8,128)S(1)}, u32[]{:S(2)}, u32[]{:S(2)}) collective-permute-start(f32[8,128]{1,0:T(8,128)S(1)} %add.30), channel_id=1, source_target_pairs={{0,8},{2,10},{4,12},{6,14},{8,0},{10,2},{12,4},{14,6},{1,9},{3,11}... | collective-permute-start | bytes 12296 | tf_op jit(solution)/shard_map/ppermute | solution.py:65
  117.6 3.6 %collective-permute-start.20 = (s32[4]{0:T(128)S(1)}, s32[4]{0:T(128)S(1)}, u32[]{:S(2)}, u32[]{:S(2)}) collective-permute-start(s32[4]{0:T(128)S(1)} %copy-done.1), channel_id=1, source_target_pairs={{0,2},{2,0},{4,6},{6,4},{8,10},{10,8},{12,14},{14,12},{1,3},{3,1},... | collective-permute-start | bytes 56 | tf_op jit(solution)/shard_map/ppermute | solution.py:51
  122.0 21.9 %collective-permute-start.21 = (f32[4,32,2048]{2,1,0:T(8,128)S(1)}, f32[4,32,2048]{2,1,0:T(8,128)S(1)}, u32[]{:S(2)}, u32[]{:S(2)}) collective-permute-start(f32[4,32,2048]{2,1,0:T(8,128)S(1)} %shard_map.36), channel_id=1, source_target_pairs={{0,2},{2,0},{4,6},{6,4},{8,10},{10,8},{12,14},{14,12},{1,3},{3,1},... | collective-permute-start | bytes 3145736 | tf_op jit(solution)/shard_map/ppermute | solution.py:51

commit v7 on v6

--- a/solution.py
+++ b/solution.py
@@ -66,21 +66,45 @@
     return value
 
 
+def tile_of(t):
+    return slice(t * LANES, (t + 1) * LANES)
+
+
+def images_of(message, tiles):
+    return (message.shape[0] - 1) // tiles
+
+
+def edge_tile(message, i):
+    return pltpu.roll(message[message.shape[0] - 1], LANES - EDGE - 2 * EDGE * i, 1)
+
+
+def pack_edges(tiles):
+    lane = lax.broadcasted_iota(jnp.int32, tiles[0].shape, 1)
+    packed = jnp.zeros(tiles[0].shape, F32)
+    for i, tile in enumerate(tiles):
+        mine = (lane >= 2 * EDGE * i) & (lane < 2 * EDGE * (i + 1))
+        packed = jnp.where(mine, pltpu.roll(tile, EDGE + 2 * EDGE * i, 1), packed)
+    return packed
+
+
 def pick_kernel(*refs):
-    *blocks, picked = refs
+    *messages, picked = refs
+    tiles = picked.shape[2] // LANES - 1
     at = 0
-    for block in blocks:
-        for i in range(block.shape[0]):
-            picked[at, 0:EDGE, :] = block[i, 0:EDGE, :]
-            picked[at, EDGE:, :] = block[i, block.shape[1] - EDGE :, :]
+    for message in messages:
+        for i in range(images_of(message, tiles)):
+            for t in range(tiles + 1):
+                tile = message[i * tiles + t] if t < tiles else edge_tile(message, i)
+                picked[at, 0:EDGE, tile_of(t)] = tile[0:EDGE]
+                picked[at, EDGE:, tile_of(t)] = tile[tile.shape[0] - EDGE :]
             at += 1
 
 
-def neighbour_rows(blocks):
+def neighbour_rows(tiles, blocks):
     size = lax.axis_size("space")
-    count = sum(block.shape[0] for block in blocks)
+    count = sum(images_of(block, tiles) for block in blocks)
     picked = call(
-        pick_kernel, jax.ShapeDtypeStruct((count, 2 * EDGE, blocks[0].shape[2]), F32), operands=len(blocks)
+        pick_kernel, jax.ShapeDtypeStruct((count, 2 * EDGE, (tiles + 1) * LANES), F32), operands=len(blocks)
     )(*blocks)
     if size == 1:
         return picked
@@ -91,27 +115,44 @@
     return jnp.concatenate([after, before], axis=1)
 
 
-def pack_kernel(x_ref, keep_ref, send_ref):
+def pack_kernel(x_ref, keep_ref, send_first, send_second, shared_ref, extra_ref):
     _, lo = pair_position()
-    columns = x_ref.shape[2]
+    local, rows, columns = x_ref.shape
     half = columns // PAIR
-    lane = lax.broadcasted_iota(jnp.int32, (x_ref.shape[1], LANES), 1)
-
-    local = x_ref.shape[0]
-
-    def body(q, carry):
-        k = jnp.where(lo == 0, q, local - 1 - q)
-        for ref, part in ((keep_ref, lo), (send_ref, 1 - lo)):
-            begin = pl.multiple_of(part * half, LANES)
-            right = pl.multiple_of((1 - part) * half, LANES)
-            left = pl.multiple_of((1 - part) * half + half - LANES, LANES)
-            ref[q, :, 0:half] = x_ref[k, :, pl.ds(begin, half)]
-            ref[q, :, half:] = jnp.where(
-                lane < LANES // 2, x_ref[k, :, pl.ds(right, LANES)], x_ref[k, :, pl.ds(left, LANES)]
+    tiles = half // LANES
+    lane = lax.broadcasted_iota(jnp.int32, (rows, LANES), 1)
+
+    def fill(ref, part, chosen):
+        begin = part * half
+        right = pl.multiple_of((1 - part) * half, LANES)
+        left = pl.multiple_of((1 - part) * half + half - LANES, LANES)
+        edges = []
+        for i, q in enumerate(chosen):
+            k = jnp.where(lo == 0, q, local - 1 - q)
+            for t in range(tiles):
+                ref[i * tiles + t] = x_ref[k, :, pl.ds(pl.multiple_of(begin + t * LANES, LANES), LANES)]
+            edges.append(
+                jnp.where(lane < LANES // 2, x_ref[k, :, pl.ds(right, LANES)], x_ref[k, :, pl.ds(left, LANES)])
             )
-        return carry
-
-    lax.fori_loop(0, local, body, 0)
+        ref[len(chosen) * tiles] = pack_edges(edges)
+
+    fill(send_first, 1 - lo, range(CHUNKS[1]))
+    fill(send_second, 1 - lo, range(CHUNKS[1], local))
+    fill(keep_ref, lo, range(local))
+    fill(shared_ref, lo, range(local - SHARED, local))
+    fill(extra_ref, lo, range(local - FAR, local - SHARED))
+
+
+def far_kernel(first, second, out):
+    tiles = (first.shape[0] - 1) // CHUNKS[1]
+    local = CHUNKS[1] + images_of(second, tiles)
+    edges = []
+    for i, q in enumerate(range(local - FAR, local)):
+        source, at = (first, q) if q < CHUNKS[1] else (second, q - CHUNKS[1])
+        for t in range(tiles):
+            out[i * tiles + t] = source[at * tiles + t]
+        edges.append(edge_tile(source, at))
+    out[FAR * tiles] = pack_edges(edges)
 
 
 def sum_of_neighbours(load, tiles, rows, use):
@@ -132,10 +173,6 @@
         center, from_left, to_left = following, shifted, next_to_left
 
 
-def tile_of(t):
-    return slice(t * LANES, (t + 1) * LANES)
-
-
 def neighbours_of(k, first, count):
     gid = k + first
     is_first, is_last = gid == 0, gid == count - 1
@@ -222,36 +259,34 @@
     lax.fori_loop(low, high, body, 0)
 
 
-def chunk_of(q):
-    return max(c for c in range(len(CHUNKS)) if CHUNKS[c] <= q)
-
-
-def place(phi, at, image, edge_rows):
-    rows = image.shape[0]
-    phi[at, 0:rows, :] = image
+def place(phi, at, message, i, edge_rows):
+    rows = message.shape[1]
+    tiles = phi.shape[2] // LANES - 1
+    for t in range(tiles):
+        phi[at, 0:rows, tile_of(t)] = message[i * tiles + t]
+    phi[at, 0:rows, tile_of(tiles)] = edge_tile(message, i)
     phi[at, rows:, :] = edge_rows
 
 
-def inner_kernel(*refs, count):
-    refs = list(refs)
-    pick = lambda n: [refs.pop(0) for _ in range(n)]
-    (keep,), recv = pick(1), pick(len(CHUNKS))
-    near_early, near_late, edge_rows, phi, drift, norms = pick(6)
-    local, rows, _ = keep.shape
+def inner_kernel(*refs, count, local):
+    keep, first_recv, second_recv, near_early, near_late, edge_rows, phi, drift, norms = refs
+    rows = keep.shape[1]
     hi, lo = pair_position()
     first = hi * (PAIR * local) - LOW
     top = LOW + PAIR * local
+    half = CHUNKS[1]
 
     def own_at(part, q):
         return LOW + part * local + jnp.where(part == 0, q, local - 1 - q)
 
     for q in range(local):
-        place(phi, own_at(lo, q), keep[q], edge_rows[q])
-        place(phi, own_at(1 - lo, q), recv[chunk_of(q)][q - CHUNKS[chunk_of(q)]], edge_rows[local + q])
+        place(phi, own_at(lo, q), keep, q, edge_rows[q])
+        source, at = (first_recv, q) if q < half else (second_recv, q - half)
+        place(phi, own_at(1 - lo, q), source, at, edge_rows[local + q])
         low_at, high_at = LOW - 1 - q, top + q
-        place(phi, jnp.where(lo == 1, low_at, high_at), near_early[q], edge_rows[2 * local + q])
-        if q < near_late.shape[0]:
-            place(phi, jnp.where(lo == 1, high_at, low_at), near_late[q], edge_rows[3 * local + q])
+        place(phi, jnp.where(lo == 1, low_at, high_at), near_early, q, edge_rows[2 * local + q])
+        if q < half:
+            place(phi, jnp.where(lo == 1, high_at, low_at), near_late, q, edge_rows[3 * local + q])
     drift_pass(phi, drift, norms, LOW - 1, top + 1, first, count, rows, LOW - 1)
 
 
@@ -279,27 +314,27 @@
     window = phi.shape[0]
     done = CHUNKS[-1]
     for q in range(done, local):
-        place(phi, jnp.where(lo == 1, top + q, LOW - 1 - q), near_late[q - done], rows_late[q - done])
+        place(phi, jnp.where(lo == 1, top + q, LOW - 1 - q), near_late, q - done, rows_late[q - done])
     for i in range(FAR):
         low_at, high_at = LOW - 1 - local - i, top + local + i
         at = FAR - 1 - i
-        late, late_rows = far_late.at[at], rows_late.at[local - done + at]
-        early = far_early.at[SHARED - 1 - i] if i < SHARED else far_extra.at[FAR - 1 - i]
-        early_rows = rows_late.at[local - done + FAR + (SHARED - 1 - i if i < SHARED else FAR - 1 - i + SHARED)]
+        late = (far_late, at, rows_late.at[local - done + at])
+        if i < SHARED:
+            early = (far_early, SHARED - 1 - i, rows_late.at[local - done + FAR + SHARED - 1 - i])
+        else:
+            early = (far_extra, FAR - 1 - i, rows_late.at[local - done + FAR + FAR - 1 - i + SHARED])
 
         @pl.when(lo == 1)
         def _():
-            if high_at < window:
-                place(phi, high_at, early[...], early_rows[...])
-            if low_at >= 0:
-                place(phi, low_at, late[...], late_rows[...])
+            for position, (message, index, edge) in ((high_at, early), (low_at, late)):
+                if 0 <= position < window:
+                    place(phi, position, message, index, edge[...])
 
         @pl.when(lo == 0)
         def _():
-            if high_at < window:
-                place(phi, high_at, late[...], late_rows[...])
-            if low_at >= 0:
-                place(phi, low_at, early[...], early_rows[...])
+            for position, (message, index, edge) in ((high_at, late), (low_at, early)):
+                if 0 <= position < window:
+                    place(phi, position, message, index, edge[...])
 
     def store(k, t, value):
         new_phi[k, :, tile_of(t)] = value
@@ -402,24 +437,29 @@
     if devices & (devices - 1) or ITERS != 2 or local != 2 * ITERS or count > SUBLANES * LANES or rows % SUBLANES:
         raise ValueError("unsupported sizes")
     shape = functools.partial(jax.ShapeDtypeStruct, dtype=F32)
-    block = shape((local, rows, wide))
     ahead = [(i, i + PAIR) for i in range(devices - PAIR)]
     back = [(target, source) for source, target in ahead]
     move = lambda value, up, down: lax.ppermute(
         value, "img",
         [p for p in ahead if p[0] % PAIR in up] + [p for p in back if p[0] % PAIR in down],
     )
-    keep, send = call(pack_kernel, (block, block), operands=1)(path)
-    ends = CHUNKS[1:] + (local,)
-    recv = [swap_pairs(send[a:b]) for a, b in zip(CHUNKS, ends)]
+    tiles = half // LANES
+    message = lambda n: shape((n * tiles + 1, rows, LANES))
+    first_chunk = CHUNKS[1]
+    keep, send_first, send_second, shared, extra = call(
+        pack_kernel,
+        (message(local), message(first_chunk), message(local - first_chunk), message(SHARED), message(FAR - SHARED)),
+        operands=1,
+    )(path)
+    recv = [swap_pairs(send_first), swap_pairs(send_second)]
     other_bracket = swap_pairs(bracket)
     near_early = move(keep, (1,), (0,))
-    far_early = move(keep[local - SHARED :], (0,), (1,))
+    far_early = move(shared, (0,), (1,))
     near_late = [move(value, (0,), (1,)) for value in recv]
-    far_late = move(jnp.concatenate(recv, axis=0)[local - FAR :], (1,), (0,))
-    far_extra = move(keep[local - FAR : local - SHARED], (), (1,))
-    rows_early = neighbour_rows([keep] + recv + [near_early, near_late[0]])
-    rows_late = neighbour_rows([near_late[1], far_late, far_early, far_extra])
+    far_late = move(call(far_kernel, message(FAR), operands=2)(*recv), (1,), (0,))
+    far_extra = move(extra, (), (1,))
+    rows_early = neighbour_rows(tiles, [keep] + recv + [near_early, near_late[0]])
+    rows_late = neighbour_rows(tiles, [near_late[1], far_late, far_early, far_extra])
     held = shape((window, rows + 2 * EDGE, wide))
     lines = -(-window // SUBLANES) * SUBLANES
     norm_shape = shape((2, lines, LANES))
@@ -427,7 +467,7 @@
     inside = PAIR * local + 2
     inside_lines = -(-inside // SUBLANES) * SUBLANES
     phi, drift, norms = call(
-        functools.partial(inner_kernel, count=count), (held, held, shape((2, inside_lines, LANES))),
+        functools.partial(inner_kernel, count=count, local=local), (held, held, shape((2, inside_lines, LANES))),
         operands=len(operands),
     )(*operands)
     norms = small_sum(norms, (1,))

time: 145 us -> 144 us (level)
  waiting for transfers between devices: 68 us -> 66.2 us
    pallas_call x4 -> x5, Pallas kernels: 3.57 us -> 4.08 us  [the longest x1 3.15 us: per_device(): call(functools.partial(inner_kernel, count=count, local=local), (held, he...]
  transfers between devices with their start and end apart: 22 -> 22, of which waited for: 15 -> 14; matrix products, arithmetic and copies ran while one was open for 0% -> 0% of each run, Pallas kernels for 7% -> 7%
where the time goes in v7:
time: 144 us
  waiting for transfers between devices  66.2 us (46%)
  starting transfers between devices  48.8 us (34%)
  Pallas kernels  26.7 us (19%)
  local copies, waits for them, and re-layouts  1.68 us (1%)
    ppermute x4, waiting for transfers between devices, swap_pairs(): return lax.ppermute(value, 'img', [(i, i ^ 1) for i in range(count)])  35.3 us
    ppermute x6, waiting for transfers between devices, per_device(): lax.ppermute(value, 'img', [p for p in ahead if p[0] % PAIR in up] + [p f...  21 us
    ppermute x5, starting transfers between devices, small_sum(): lax.ppermute(value, 'img', [(i, i ^ step) for i in range(count)])  18.4 us
    ppermute x6, starting transfers between devices, per_device(): lax.ppermute(value, 'img', [p for p in ahead if p[0] % PAIR in up] + [p f...  14.9 us
    ppermute x4, starting transfers between devices, swap_pairs(): return lax.ppermute(value, 'img', [(i, i ^ 1) for i in range(count)])  9.99 us
    pallas_call x1, Pallas kernels, per_device(): call(functools.partial(middle_outer_kernel, count=count, local=local), (h...  8.69 us
    ppermute x5, waiting for transfers between devices, small_sum(): lax.ppermute(value, 'img', [(i, i ^ step) for i in range(count)])  6.7 us
    pallas_call x1, Pallas kernels, per_device(): call(functools.partial(last_kernel, count=count, local=local, rows=rows,...  5.38 us
  transfers between devices with their start and end apart: 22, of which 14 were waited for; matrix products, arithmetic and copies ran while one was open for 0% of the time, Pallas kernels for 7%

profile of v7, /device:TPU:0, one launch (start us, length us, event | category | flops | bytes accessed | tf_op | source)
XLA Modules:
  0.0 143.7 jit_solution(11320516427537585353)
XLA Ops:
  0.0 1.6 %copy-done = f32[4,32,4096]{2,1,0:T(8,128)S(1)} copy-done((f32[4,32,4096]{2,1,0:T(8,128)S(1)}, f32[4,32,4096]{2,1,0:T(8,128)}, u32[]{:S(2)}) %copy-start) | copy-done | bytes 2097176
  2.0 3.1 %collective-permute-start = (f32[33,32,128]{2,1,0:T(8,128)S(1)}, f32[33,32,128]{2,1,0:T(8,128)S(1)}, u32[]{:S(2)}, u32[]{:S(2)}) collective-permute-start(f32[33,32,128]{2,1,0:T(8,128)S(1)} %get-tuple-element.24), channel_id=1, source_target_pairs={{0,2},{2,0},{4,6},{6,4},{8,10},{10,8},{12,14},{14,12},{1,3},{3,1},... | collective-permute-start | bytes 1622024 | tf_op jit(solution)/shard_map/ppermute | solution.py:51
  6.3 2.8 %collective-permute-start.1 = (f32[33,32,128]{2,1,0:T(8,128)S(1)}, f32[33,32,128]{2,1,0:T(8,128)S(1)}, u32[]{:S(2)}, u32[]{:S(2)}) collective-permute-start(f32[33,32,128]{2,1,0:T(8,128)S(1)} %get-tuple-element.25), channel_id=1, source_target_pairs={{0,2},{2,0},{4,6},{6,4},{8,10},{10,8},{12,14},{14,12},{1,3},{3,1},... | collective-permute-start | bytes 1622024 | tf_op jit(solution)/shard_map/ppermute | solution.py:51
  9.2 9.0 %collective-permute-done.refs_1_.first = f32[33,32,128]{2,1,0:T(8,128)S(1)} collective-permute-done((f32[33,32,128]{2,1,0:T(8,128)S(1)}, f32[33,32,128]{2,1,0:T(8,128)S(1)}, u32[]{:S(2)}, u32[]{:S(2)}) %collective-permute-start) | collective-permute-done | bytes 540704 | tf_op jit(solution)/shard_map/ppermute | solution.py:51
  18.2 4.0 %collective-permute-start.3 = (f32[33,32,128]{2,1,0:T(8,128)S(1)}, f32[33,32,128]{2,1,0:T(8,128)S(1)}, u32[]{:S(2)}, u32[]{:S(2)}) collective-permute-start(f32[33,32,128]{2,1,0:T(8,128)S(1)} %collective-permute-done.refs_1_.first), channel_id=1, source_target_pairs={{0,4},{4,8},{8,12},{6,2},{10,6},{14,10},{1,5},{5,9},{9,13},{7,3},{... | collective-permute-start | bytes 1622024 | tf_op jit(solution)/shard_map/ppermute | solution.py:442
  22.2 6.7 %collective-permute-done.1.refs_2_.second = f32[33,32,128]{2,1,0:T(8,128)S(1)} collective-permute-done((f32[33,32,128]{2,1,0:T(8,128)S(1)}, f32[33,32,128]{2,1,0:T(8,128)S(1)}, u32[]{:S(2)}, u32[]{:S(2)}) %collective-permute-start.1) | collective-permute-done | bytes 540704 | tf_op jit(solution)/shard_map/ppermute | solution.py:51
  29.1 1.3 collective-permute-start.12
  30.4 1.5 %collective-permute-done.2.refs_3_ = f32[65,32,128]{2,1,0:T(8,128)S(1)} collective-permute-done((f32[65,32,128]{2,1,0:T(8,128)S(1)}, f32[65,32,128]{2,1,0:T(8,128)S(1)}, u32[]{:S(2)}, u32[]{:S(2)}) %collective-permute-start.2) | collective-permute-done | bytes 1064992 | tf_op jit(solution)/shard_map/ppermute | solution.py:442
  32.2 4.2 %collective-permute-start.10 = (f32[33,32,128]{2,1,0:T(8,128)S(1)}, f32[33,32,128]{2,1,0:T(8,128)S(1)}, u32[]{:S(2)}, u32[]{:S(2)}) collective-permute-start(f32[33,32,128]{2,1,0:T(8,128)S(1)} %get-tuple-element.27), channel_id=1, source_target_pairs={{0,4},{4,8},{8,12},{6,2},{10,6},{14,10},{1,5},{5,9},{9,13},{7,3},{... | collective-permute-start | bytes 1622024 | tf_op jit(solution)/shard_map/ppermute | solution.py:442
  36.4 3.5 %collective-permute-start.9 = (f32[33,32,128]{2,1,0:T(8,128)S(1)}, f32[33,32,128]{2,1,0:T(8,128)S(1)}, u32[]{:S(2)}, u32[]{:S(2)}) collective-permute-start(f32[33,32,128]{2,1,0:T(8,128)S(1)} %collective-permute-done.1.refs_2_.second), channel_id=1, source_target_pairs={{0,4},{4,8},{8,12},{6,2},{10,6},{14,10},{1,5},{5,9},{9,13},{7,3},{... | collective-permute-start | bytes 1622024 | tf_op jit(solution)/shard_map/ppermute | solution.py:442
  40.6 8.4 %collective-permute-done.10.refs_2_.far_early = f32[33,32,128]{2,1,0:T(8,128)S(1)} collective-permute-done((f32[33,32,128]{2,1,0:T(8,128)S(1)}, f32[33,32,128]{2,1,0:T(8,128)S(1)}, u32[]{:S(2)}, u32[]{:S(2)}) %collective-permute-start.10) | collective-permute-done | bytes 540704 | tf_op jit(solution)/shard_map/ppermute | solution.py:442
  49.0 11.1 %collective-permute-done.9.refs_0_.near_late = f32[33,32,128]{2,1,0:T(8,128)S(1)} collective-permute-done((f32[33,32,128]{2,1,0:T(8,128)S(1)}, f32[33,32,128]{2,1,0:T(8,128)S(1)}, u32[]{:S(2)}, u32[]{:S(2)}) %collective-permute-start.9) | collective-permute-done | bytes 540704 | tf_op jit(solution)/shard_map/ppermute | solution.py:442
  60.3 3.1 %shard_map.30 = (f32[21,40,2176]{2,1,0:T(8,128)S(1)}, f32[21,40,2176]{2,1,0:T(8,128)S(1)}, f32[2,16,128]{2,1,0:T(8,128)S(1)}) custom-call(f32[65,32,128]{2,1,0:T(8,128)S(1)} %get-tuple-element.23.refs_0_, f32[33,32,128]{2,1,0:T(8,128)S(1)} %collective-permute-done.refs_1_.first, f32[33,32,128]{2,1,0:T(8,128)S(1)} %collective-permute-done.1.refs_2_.second, ...), custom_call_target="tpu_custom_call" | custom-call | tf_op jit(solution)/shard_map/pallas_call | solution.py:469
  64.9 8.7 %collective-permute-start.6 = (f32[2,16,128]{2,1,0:T(8,128)S(1)}, f32[2,16,128]{2,1,0:T(8,128)S(1)}, u32[]{:S(2)}, u32[]{:S(2)}) collective-permute-start(f32[2,16,128]{2,1,0:T(8,128)S(1)} %add.24), channel_id=1, source_target_pairs={{0,2},{2,0},{4,6},{6,4},{8,10},{10,8},{12,14},{14,12},{1,3},{3,1},... | collective-permute-start | bytes 49160 | tf_op jit(solution)/shard_map/ppermute | solution.py:65
  73.5 1.7 %collective-permute-done.6 = f32[2,16,128]{2,1,0:T(8,128)S(1)} collective-permute-done((f32[2,16,128]{2,1,0:T(8,128)S(1)}, f32[2,16,128]{2,1,0:T(8,128)S(1)}, u32[]{:S(2)}, u32[]{:S(2)}) %collective-permute-start.6) | collective-permute-done | bytes 16416 | tf_op jit(solution)/shard_map/ppermute | solution.py:65
  75.3 3.4 %collective-permute-start.7 = (f32[2,8,128]{2,1,0:T(8,128)S(1)}, f32[2,8,128]{2,1,0:T(8,128)S(1)}, u32[]{:S(2)}, u32[]{:S(2)}) collective-permute-start(f32[2,8,128]{2,1,0:T(8,128)S(1)} %slice.12), channel_id=1, source_target_pairs={{0,4},{2,6},{4,8},{6,10},{8,12},{10,14},{1,5},{3,7},{5,9},{7,11},{... | collective-permute-start | bytes 24584 | tf_op jit(solution)/shard_map/ppermute | solution.py:475
  78.7 1.3 collective-permute-start.8
  80.1 5.0 %shard_map.33 = (f32[21,40,2176]{2,1,0:T(8,128)S(1)}, f32[21,40,2176]{2,1,0:T(8,128)S(1)}, f32[21,40,2176]{2,1,0:T(8,128)S(1)}, f32[21,40,2176]{2,1,0:T(8,128)S(1)}, f32[2,24,128]{2,1,0:T(8,128)S(1)}) custom-call(f32[21,40,2176]{2,1,0:T(8,128)S(1)} %get-tuple-element.29._, ...), custom_call_target="tpu_custom_call", output_to_operand_aliasing={{0}: (0, {}), {1}: (1, {})} | custom-call | tf_op jit(solution)/shard_map/pallas_call | solution.py:477
  85.3 8.7 %shard_map.34 = (f32[21,40,2176]{2,1,0:T(8,128)S(1)}, f32[21,40,2176]{2,1,0:T(8,128)S(1)}, f32[21,40,2176]{2,1,0:T(8,128)S(1)}, f32[21,40,2176]{2,1,0:T(8,128)S(1)}, f32[2,24,128]{2,1,0:T(8,128)S(1)}) custom-call(f32[2,24,128]{2,1,0:T(8,128)S(1)} %maximum_maximum_fusion.norms, ...), custom_call_target="tpu_custom_call", output_to_operand_aliasing={{0}: (6, {}), {1}: (7, {}), {2}: (8, {}), {3}: (9, {}), {4}... | custom-call | tf_op jit(solution)/shard_map/pallas_call | solution.py:485
  95.2 2.0 %collective-permute-start.15 = (f32[2,24,128]{2,1,0:T(8,128)S(1)}, f32[2,24,128]{2,1,0:T(8,128)S(1)}, u32[]{:S(2)}, u32[]{:S(2)}) collective-permute-start(f32[2,24,128]{2,1,0:T(8,128)S(1)} %add.26), channel_id=1, source_target_pairs={{0,2},{2,0},{4,6},{6,4},{8,10},{10,8},{12,14},{14,12},{1,3},{3,1},... | collective-permute-start | bytes 73736 | tf_op jit(solution)/shard_map/ppermute | solution.py:65
  97.3 1.8 %collective-permute-done.15 = f32[2,24,128]{2,1,0:T(8,128)S(1)} collective-permute-done((f32[2,24,128]{2,1,0:T(8,128)S(1)}, f32[2,24,128]{2,1,0:T(8,128)S(1)}, u32[]{:S(2)}, u32[]{:S(2)}) %collective-permute-start.15) | collective-permute-done | bytes 24608 | tf_op jit(solution)/shard_map/ppermute | solution.py:65
  99.1 5.4 %shard_map.35 = (f32[13,32,2048]{2,1,0:T(8,128)S(1)}, f32[8,128]{1,0:T(8,128)S(1)}, f32[21,40,2176]{2,1,0:T(8,128)S(1)}) custom-call(f32[21,40,2176]{2,1,0:T(8,128)S(1)} %get-tuple-element.36.phi, f32[21,40,2176]{2,1,0:T(8,128)S(1)} %get-tuple-element.37._, f32[2,24,128]{2,1,0:T(8,128)S(1)} %add.27.norms), custom_call_target="tpu_custom_call", output_to_operand_aliasing={{2}: (1, {})} | custom-call | tf_op jit(solution)/shard_map/pallas_call | solution.py:492
  105.6 2.0 %collective-permute-start.17 = (f32[8,128]{1,0:T(8,128)S(1)}, f32[8,128]{1,0:T(8,128)S(1)}, u32[]{:S(2)}, u32[]{:S(2)}) collective-permute-start(f32[8,128]{1,0:T(8,128)S(1)} %add.28), channel_id=1, source_target_pairs={{0,2},{2,0},{4,6},{6,4},{8,10},{10,8},{12,14},{14,12},{1,3},{3,1},... | collective-permute-start | bytes 12296 | tf_op jit(solution)/shard_map/ppermute | solution.py:65
  107.6 1.6 %collective-permute-done.17 = f32[8,128]{1,0:T(8,128)S(1)} collective-permute-done((f32[8,128]{1,0:T(8,128)S(1)}, f32[8,128]{1,0:T(8,128)S(1)}, u32[]{:S(2)}, u32[]{:S(2)}) %collective-permute-start.17) | collective-permute-done | bytes 4128 | tf_op jit(solution)/shard_map/ppermute | solution.py:65
  109.2 2.6 %collective-permute-start.18 = (f32[8,128]{1,0:T(8,128)S(1)}, f32[8,128]{1,0:T(8,128)S(1)}, u32[]{:S(2)}, u32[]{:S(2)}) collective-permute-start(f32[8,128]{1,0:T(8,128)S(1)} %add.29), channel_id=1, source_target_pairs={{0,4},{2,6},{4,0},{6,2},{8,12},{10,14},{12,8},{14,10},{1,5},{3,7},... | collective-permute-start | bytes 12296 | tf_op jit(solution)/shard_map/ppermute | solution.py:65
  111.9 1.6 %collective-permute-done.18 = f32[8,128]{1,0:T(8,128)S(1)} collective-permute-done((f32[8,128]{1,0:T(8,128)S(1)}, f32[8,128]{1,0:T(8,128)S(1)}, u32[]{:S(2)}, u32[]{:S(2)}) %collective-permute-start.18) | collective-permute-done | bytes 4128 | tf_op jit(solution)/shard_map/ppermute | solution.py:65
  113.5 3.0 %collective-permute-start.19 = (f32[8,128]{1,0:T(8,128)S(1)}, f32[8,128]{1,0:T(8,128)S(1)}, u32[]{:S(2)}, u32[]{:S(2)}) collective-permute-start(f32[8,128]{1,0:T(8,128)S(1)} %add.30), channel_id=1, source_target_pairs={{0,8},{2,10},{4,12},{6,14},{8,0},{10,2},{12,4},{14,6},{1,9},{3,11}... | collective-permute-start | bytes 12296 | tf_op jit(solution)/shard_map/ppermute | solution.py:65
  116.5 2.0 %collective-permute-start.20 = (s32[4]{0:T(128)S(1)}, s32[4]{0:T(128)S(1)}, u32[]{:S(2)}, u32[]{:S(2)}) collective-permute-start(s32[4]{0:T(128)S(1)} %copy-done.1), channel_id=1, source_target_pairs={{0,2},{2,0},{4,6},{6,4},{8,10},{10,8},{12,14},{14,12},{1,3},{3,1},... | collective-permute-start | bytes 56 | tf_op jit(solution)/shard_map/ppermute | solution.py:51
  118.5 1.5 %collective-permute-done.20.bracket = s32[4]{0:T(128)S(1)} collective-permute-done((s32[4]{0:T(128)S(1)}, s32[4]{0:T(128)S(1)}, u32[]{:S(2)}, u32[]{:S(2)}) %collective-permute-start.20) | collective-permute-done | bytes 48 | tf_op jit(solution)/shard_map/ppermute | solution.py:51
  120.9 2.1 %collective-permute-start.21 = (f32[4,32,2048]{2,1,0:T(8,128)S(1)}, f32[4,32,2048]{2,1,0:T(8,128)S(1)}, u32[]{:S(2)}, u32[]{:S(2)}) collective-permute-start(f32[4,32,2048]{2,1,0:T(8,128)S(1)} %shard_map.37), channel_id=1, source_target_pairs={{0,2},{2,0},{4,6},{6,4},{8,10},{10,8},{12,14},{14,12},{1,3},{3,1},... | collective-permute-start | bytes 3145736 | tf_op jit(solution)/shard_map/ppermute | solution.py:51
  123.0 1.8 %shard_map.36.whole_in = f32[4,32,4096]{2,1,0:T(8,128)} custom-call(s32[4]{0:T(128)S(1)} %copy-done.1, f32[13,32,2048]{2,1,0:T(8,128)S(1)} %get-tuple-element.39.window, f32[8,128]{1,0:T(8,128)S(1)} %add.31.squares), custom_call_target="tpu_custom_call" | custom-call | tf_op jit(solution)/shard_map/pallas_call | solution.py:511
  124.7 18.0 %collective-permute-done.21.other = f32[4,32,2048]{2,1,0:T(8,128)S(1)} collective-permute-done((f32[4,32,2048]{2,1,0:T(8,128)S(1)}, f32[4,32,2048]{2,1,0:T(8,128)S(1)}, u32[]{:S(2)}, u32[]{:S(2)}) %collective-permute-start.21) | collective-permute-done | bytes 1048608 | tf_op jit(solution)/shard_map/ppermute | solution.py:51
  (40 shorter events, 8.8 us)
Async XLA Ops:
  0.0 1.6 %copy-start = (f32[4,32,4096]{2,1,0:T(8,128)S(1)}, f32[4,32,4096]{2,1,0:T(8,128)}, u32[]{:S(2)}) copy-start(f32[4,32,4096]{2,1,0:T(8,128)} %x_ref.1) | copy-start | bytes 6291460
  2.0 16.2 %collective-permute-start = (f32[33,32,128]{2,1,0:T(8,128)S(1)}, f32[33,32,128]{2,1,0:T(8,128)S(1)}, u32[]{:S(2)}, u32[]{:S(2)}) collective-permute-start(f32[33,32,128]{2,1,0:T(8,128)S(1)} %get-tuple-element.24), channel_id=1, source_target_pairs={{0,2},{2,0},{4,6},{6,4},{8,10},{10,8},{12,14},{14,12},{1,3},{3,1},... | collective-permute-start | bytes 1622024 | tf_op jit(solution)/shard_map/ppermute | solution.py:51
  5.1 26.9 %collective-permute-start.2 = (f32[65,32,128]{2,1,0:T(8,128)S(1)}, f32[65,32,128]{2,1,0:T(8,128)S(1)}, u32[]{:S(2)}, u32[]{:S(2)}) collective-permute-start(f32[65,32,128]{2,1,0:T(8,128)S(1)} %get-tuple-element.23.refs_0_), channel_id=1, source_target_pairs={{2,6},{6,10},{10,14},{4,0},{8,4},{12,8},{3,7},{7,11},{11,15},{5,1}... | collective-permute-start | bytes 3194888 | tf_op jit(solution)/shard_map/ppermute | solution.py:442
  6.3 22.6 %collective-permute-start.1 = (f32[33,32,128]{2,1,0:T(8,128)S(1)}, f32[33,32,128]{2,1,0:T(8,128)S(1)}, u32[]{:S(2)}, u32[]{:S(2)}) collective-permute-start(f32[33,32,128]{2,1,0:T(8,128)S(1)} %get-tuple-element.25), channel_id=1, source_target_pairs={{0,2},{2,0},{4,6},{6,4},{8,10},{10,8},{12,14},{14,12},{1,3},{3,1},... | collective-permute-start | bytes 1622024 | tf_op jit(solution)/shard_map/ppermute | solution.py:51
  18.2 13.7 %collective-permute-start.3 = (f32[33,32,128]{2,1,0:T(8,128)S(1)}, f32[33,32,128]{2,1,0:T(8,128)S(1)}, u32[]{:S(2)}, u32[]{:S(2)}) collective-permute-start(f32[33,32,128]{2,1,0:T(8,128)S(1)} %collective-permute-done.refs_1_.first), channel_id=1, source_target_pairs={{0,4},{4,8},{8,12},{6,2},{10,6},{14,10},{1,5},{5,9},{9,13},{7,3},{... | collective-permute-start | bytes 1622024 | tf_op jit(solution)/shard_map/ppermute | solution.py:442
  29.1 31.0 %collective-permute-start.12 = (f32[49,32,128]{2,1,0:T(8,128)S(1)}, f32[49,32,128]{2,1,0:T(8,128)S(1)}, u32[]{:S(2)}, u32[]{:S(2)}) collective-permute-start(f32[49,32,128]{2,1,0:T(8,128)S(1)} %shard_map.31), channel_id=1, source_target_pairs={{2,6},{6,10},{10,14},{4,0},{8,4},{12,8},{3,7},{7,11},{11,15},{5,1}... | collective-permute-start | bytes 2408456 | tf_op jit(solution)/shard_map/ppermute | solution.py:442
  32.1 28.2 %collective-permute-start.4 = (f32[14,8,2176]{2,1,0:T(8,128)S(1)}, f32[14,8,2176]{2,1,0:T(8,128)S(1)}, u32[]{:S(2)}, u32[]{:S(2)}) collective-permute-start(f32[14,8,2176]{2,1,0:T(8,128)S(1)} %shard_map.29), channel_id=1, source_target_pairs={{0,1},{1,0},{2,3},{3,2},{4,5},{5,4},{6,7},{7,6},{8,9},{9,8},{10,11... | collective-permute-start | bytes 2924552 | tf_op jit(solution)/shard_map/ppermute | solution.py:112
  32.2 16.8 %collective-permute-start.10 = (f32[33,32,128]{2,1,0:T(8,128)S(1)}, f32[33,32,128]{2,1,0:T(8,128)S(1)}, u32[]{:S(2)}, u32[]{:S(2)}) collective-permute-start(f32[33,32,128]{2,1,0:T(8,128)S(1)} %get-tuple-element.27), channel_id=1, source_target_pairs={{0,4},{4,8},{8,12},{6,2},{10,6},{14,10},{1,5},{5,9},{9,13},{7,3},{... | collective-permute-start | bytes 1622024 | tf_op jit(solution)/shard_map/ppermute | solution.py:442
  36.4 23.7 %collective-permute-start.9 = (f32[33,32,128]{2,1,0:T(8,128)S(1)}, f32[33,32,128]{2,1,0:T(8,128)S(1)}, u32[]{:S(2)}, u32[]{:S(2)}) collective-permute-start(f32[33,32,128]{2,1,0:T(8,128)S(1)} %collective-permute-done.1.refs_2_.second), channel_id=1, source_target_pairs={{0,4},{4,8},{8,12},{6,2},{10,6},{14,10},{1,5},{5,9},{9,13},{7,3},{... | collective-permute-start | bytes 1622024 | tf_op jit(solution)/shard_map/ppermute | solution.py:442
  39.9 0.7 collective-permute-start.11
  60.2 25.0 %collective-permute-start.13 = (f32[8,8,2176]{2,1,0:T(8,128)S(1)}, f32[8,8,2176]{2,1,0:T(8,128)S(1)}, u32[]{:S(2)}, u32[]{:S(2)}) collective-permute-start(f32[8,8,2176]{2,1,0:T(8,128)S(1)} %shard_map.32), channel_id=1, source_target_pairs={{0,1},{1,0},{2,3},{3,2},{4,5},{5,4},{6,7},{7,6},{8,9},{9,8},{10,11... | collective-permute-start | bytes 1671176 | tf_op jit(solution)/shard_map/ppermute | solution.py:112
  63.5 1.4 collective-permute-start.5
  64.9 10.4 %collective-permute-start.6 = (f32[2,16,128]{2,1,0:T(8,128)S(1)}, f32[2,16,128]{2,1,0:T(8,128)S(1)}, u32[]{:S(2)}, u32[]{:S(2)}) collective-permute-start(f32[2,16,128]{2,1,0:T(8,128)S(1)} %add.24), channel_id=1, source_target_pairs={{0,2},{2,0},{4,6},{6,4},{8,10},{10,8},{12,14},{14,12},{1,3},{3,1},... | collective-permute-start | bytes 49160 | tf_op jit(solution)/shard_map/ppermute | solution.py:65
  75.3 9.9 %collective-permute-start.7 = (f32[2,8,128]{2,1,0:T(8,128)S(1)}, f32[2,8,128]{2,1,0:T(8,128)S(1)}, u32[]{:S(2)}, u32[]{:S(2)}) collective-permute-start(f32[2,8,128]{2,1,0:T(8,128)S(1)} %slice.12), channel_id=1, source_target_pairs={{0,4},{2,6},{4,8},{6,10},{8,12},{10,14},{1,5},{3,7},{5,9},{7,11},{... | collective-permute-start | bytes 24584 | tf_op jit(solution)/shard_map/ppermute | solution.py:475
  78.7 6.5 %collective-permute-start.8 = (f32[2,8,128]{2,1,0:T(8,128)S(1)}, f32[2,8,128]{2,1,0:T(8,128)S(1)}, u32[]{:S(2)}, u32[]{:S(2)}) collective-permute-start(f32[2,8,128]{2,1,0:T(8,128)S(1)} %slice.12), channel_id=1, source_target_pairs={{4,0},{6,2},{8,4},{10,6},{12,8},{14,10},{5,1},{7,3},{9,5},{11,7},{... | collective-permute-start | bytes 24584 | tf_op jit(solution)/shard_map/ppermute | solution.py:476
  94.0 1.3 collective-permute-start.14
  95.2 3.8 %collective-permute-start.15 = (f32[2,24,128]{2,1,0:T(8,128)S(1)}, f32[2,24,128]{2,1,0:T(8,128)S(1)}, u32[]{:S(2)}, u32[]{:S(2)}) collective-permute-start(f32[2,24,128]{2,1,0:T(8,128)S(1)} %add.26), channel_id=1, source_target_pairs={{0,2},{2,0},{4,6},{6,4},{8,10},{10,8},{12,14},{14,12},{1,3},{3,1},... | collective-permute-start | bytes 73736 | tf_op jit(solution)/shard_map/ppermute | solution.py:65
  99.1 17.5 %copy-start.1 = (s32[4]{0:T(128)S(1)}, s32[4]{0:T(128)}, u32[]{:S(2)}) copy-start(s32[4]{0:T(128)} %bracket.1) | copy-start | bytes 52
  104.5 1.2 collective-permute-start.16
  105.6 3.6 %collective-permute-start.17 = (f32[8,128]{1,0:T(8,128)S(1)}, f32[8,128]{1,0:T(8,128)S(1)}, u32[]{:S(2)}, u32[]{:S(2)}) collective-permute-start(f32[8,128]{1,0:T(8,128)S(1)} %add.28), channel_id=1, source_target_pairs={{0,2},{2,0},{4,6},{6,4},{8,10},{10,8},{12,14},{14,12},{1,3},{3,1},... | collective-permute-start | bytes 12296 | tf_op jit(solution)/shard_map/ppermute | solution.py:65
  109.2 4.2 %collective-permute-start.18 = (f32[8,128]{1,0:T(8,128)S(1)}, f32[8,128]{1,0:T(8,128)S(1)}, u32[]{:S(2)}, u32[]{:S(2)}) collective-permute-start(f32[8,128]{1,0:T(8,128)S(1)} %add.29), channel_id=1, source_target_pairs={{0,4},{2,6},{4,0},{6,2},{8,12},{10,14},{12,8},{14,10},{1,5},{3,7},... | collective-permute-start | bytes 12296 | tf_op jit(solution)/shard_map/ppermute | solution.py:65
  113.5 5.1 %collective-permute-start.19 = (f32[8,128]{1,0:T(8,128)S(1)}, f32[8,128]{1,0:T(8,128)S(1)}, u32[]{:S(2)}, u32[]{:S(2)}) collective-permute-start(f32[8,128]{1,0:T(8,128)S(1)} %add.30), channel_id=1, source_target_pairs={{0,8},{2,10},{4,12},{6,14},{8,0},{10,2},{12,4},{14,6},{1,9},{3,11}... | collective-permute-start | bytes 12296 | tf_op jit(solution)/shard_map/ppermute | solution.py:65
  116.5 3.6 %collective-permute-start.20 = (s32[4]{0:T(128)S(1)}, s32[4]{0:T(128)S(1)}, u32[]{:S(2)}, u32[]{:S(2)}) collective-permute-start(s32[4]{0:T(128)S(1)} %copy-done.1), channel_id=1, source_target_pairs={{0,2},{2,0},{4,6},{6,4},{8,10},{10,8},{12,14},{14,12},{1,3},{3,1},... | collective-permute-start | bytes 56 | tf_op jit(solution)/shard_map/ppermute | solution.py:51
  120.9 21.8 %collective-permute-start.21 = (f32[4,32,2048]{2,1,0:T(8,128)S(1)}, f32[4,32,2048]{2,1,0:T(8,128)S(1)}, u32[]{:S(2)}, u32[]{:S(2)}) collective-permute-start(f32[4,32,2048]{2,1,0:T(8,128)S(1)} %shard_map.37), channel_id=1, source_target_pairs={{0,2},{2,0},{4,6},{6,4},{8,10},{10,8},{12,14},{14,12},{1,3},{3,1},... | collective-permute-start | bytes 3145736 | tf_op jit(solution)/shard_map/ppermute | solution.py:51

commit v8 on v7

--- a/solution.py
+++ b/solution.py
@@ -62,7 +62,8 @@
         value = lax.psum(value, "space")
     count = lax.axis_size("img")
     for step in steps:
-        value = value + lax.ppermute(value, "img", [(i, i ^ step) for i in range(count)])
+        other = lax.ppermute(value, "img", [(i, i ^ step) for i in range(count)])
+        value = value + other
     return value
 
 
@@ -349,20 +350,14 @@
         drift_pass(new_phi, new_drift, new_norms, low, high, first, count, rows)
 
 
-def last_kernel(phi, _, norms, final, squares, theta, speeds, *, count, local, rows, done):
+def last_kernel(phi, _, norms, final, squares, theta, speeds, *, count, local, rows):
     hi, _ = pair_position()
     first = hi * (PAIR * local) - LOW
-    window = phi.shape[0]
+    top = LOW + PAIR * local
     tiles = final.shape[2] // LANES
-    shift = LOW - REACH
     speeds_of(norms, speeds)
-    theta_pass(phi, speeds, theta, done + 1, window - done - 1, first, count)
-
-    def store(k, t, value):
-        if t < tiles:
-            final[k - shift, :, tile_of(t)] = value[0:rows]
-
-    update_pass(phi, speeds, theta, shift, shift + final.shape[0], first, count, store)
+    theta_pass(phi, speeds, theta, LOW - 2, top + 1, first, count)
+    update_pass(phi, speeds, theta, LOW - 1, top, first, count, store_final(final, rows))
     position = (
         lax.broadcasted_iota(jnp.int32, squares.shape, 0) * LANES
         + lax.broadcasted_iota(jnp.int32, squares.shape, 1)
@@ -378,6 +373,25 @@
         return total + jnp.where(position == LOW + i + first, amount, 0.0)
 
     squares[...] = lax.fori_loop(0, PAIR * local, body, jnp.zeros(squares.shape, F32))
+
+
+def store_final(final, rows):
+    def store(k, t, value):
+        if t < final.shape[2] // LANES:
+            final[k - (LOW - REACH), :, tile_of(t)] = value[0:rows]
+
+    return store
+
+
+def rest_kernel(phi, norms, _, __, theta, final, speeds, *, count, local, rows, done):
+    hi, _ = pair_position()
+    first = hi * (PAIR * local) - LOW
+    top = LOW + PAIR * local
+    speeds_of(norms, speeds)
+    for low, high in ((done + 1, LOW - 2), (top + 1, phi.shape[0] - done - 1)):
+        theta_pass(phi, speeds, theta, low, high, first, count)
+    for low, high in ((LOW - REACH, LOW - 1), (top, top + REACH + 1)):
+        update_pass(phi, speeds, theta, low, high, first, count, store_final(final, rows))
 
 
 def combine_kernel(bracket, window, squares, out, *scratch, count, own):
@@ -489,11 +503,16 @@
     )(*operands, *state)
     scratch = [pltpu.VMEM((lines, LANES), F32)]
     norms = small_sum(norms, (1,))
-    final, squares, _ = call(
-        functools.partial(last_kernel, count=count, local=local, rows=rows, done=2 * (ITERS - 1)),
-        (shape((PAIR * local + 2 * REACH + 1, rows, half)), shape((SUBLANES, LANES)), held),
+    final_shape = shape((PAIR * local + 2 * REACH + 1, rows, half))
+    final, squares, theta = call(
+        functools.partial(last_kernel, count=count, local=local, rows=rows),
+        (final_shape, shape((SUBLANES, LANES)), held),
         scratch=scratch, operands=3, aliases={1: 2},
     )(phi, drift, norms)
+    _, final = call(
+        functools.partial(rest_kernel, count=count, local=local, rows=rows, done=2 * (ITERS - 1)),
+        (held, final_shape), scratch=scratch, operands=4, aliases={2: 0, 3: 1},
+    )(phi, norms, theta, final)
     steps = []
     step = 1
     while step < devices:

time: 144 us -> 143 us (level)
    pallas_call x1 -> x2, Pallas kernels: 5.38 us -> 5.47 us  [the longest x1 4.09 us: per_device(): call(functools.partial(last_kernel, count=count, local=local, rows=rows),...]
  transfers between devices with their start and end apart: 22 -> 22, of which waited for: 14 -> 14; matrix products, arithmetic and copies ran while one was open for 0% -> 0% of each run, Pallas kernels for 7% -> 8%
where the time goes in v8:
time: 143 us
  waiting for transfers between devices  65.3 us (46%)
  starting transfers between devices  48.8 us (34%)
  Pallas kernels  26.8 us (19%)
  local copies, waits for them, and re-layouts  1.68 us (1%)
    ppermute x4, waiting for transfers between devices, swap_pairs(): return lax.ppermute(value, 'img', [(i, i ^ 1) for i in range(count)])  34.3 us
    ppermute x6, waiting for transfers between devices, per_device(): lax.ppermute(value, 'img', [p for p in ahead if p[0] % PAIR in up] + [p f...  21 us
    ppermute x5, starting transfers between devices, small_sum(): other = lax.ppermute(value, 'img', [(i, i ^ step) for i in range(count)])  18.4 us
    ppermute x6, starting transfers between devices, per_device(): lax.ppermute(value, 'img', [p for p in ahead if p[0] % PAIR in up] + [p f...  14.9 us
    ppermute x4, starting transfers between devices, swap_pairs(): return lax.ppermute(value, 'img', [(i, i ^ 1) for i in range(count)])  9.99 us
    pallas_call x1, Pallas kernels, per_device(): call(functools.partial(middle_outer_kernel, count=count, local=local), (h...  8.69 us
    ppermute x5, waiting for transfers between devices, small_sum(): other = lax.ppermute(value, 'img', [(i, i ^ step) for i in range(count)])  6.7 us
    pallas_call x1, Pallas kernels, per_device(): call(functools.partial(middle_inner_kernel, count=count, local=local, row...  5.05 us
  transfers between devices with their start and end apart: 22, of which 14 were waited for; matrix products, arithmetic and copies ran while one was open for 0% of the time, Pallas kernels for 8%

profile of v8, /device:TPU:0, one launch (start us, length us, event | category | flops | bytes accessed | tf_op | source)
XLA Modules:
  0.0 142.9 jit_solution(17867646277081008206)
XLA Ops:
  0.0 1.6 %copy-done = f32[4,32,4096]{2,1,0:T(8,128)S(1)} copy-done((f32[4,32,4096]{2,1,0:T(8,128)S(1)}, f32[4,32,4096]{2,1,0:T(8,128)}, u32[]{:S(2)}) %copy-start) | copy-done | bytes 2097176
  2.0 3.1 %collective-permute-start = (f32[33,32,128]{2,1,0:T(8,128)S(1)}, f32[33,32,128]{2,1,0:T(8,128)S(1)}, u32[]{:S(2)}, u32[]{:S(2)}) collective-permute-start(f32[33,32,128]{2,1,0:T(8,128)S(1)} %get-tuple-element.26), channel_id=1, source_target_pairs={{0,2},{2,0},{4,6},{6,4},{8,10},{10,8},{12,14},{14,12},{1,3},{3,1},... | collective-permute-start | bytes 1622024 | tf_op jit(solution)/shard_map/ppermute | solution.py:51
  6.3 2.8 %collective-permute-start.1 = (f32[33,32,128]{2,1,0:T(8,128)S(1)}, f32[33,32,128]{2,1,0:T(8,128)S(1)}, u32[]{:S(2)}, u32[]{:S(2)}) collective-permute-start(f32[33,32,128]{2,1,0:T(8,128)S(1)} %get-tuple-element.27), channel_id=1, source_target_pairs={{0,2},{2,0},{4,6},{6,4},{8,10},{10,8},{12,14},{14,12},{1,3},{3,1},... | collective-permute-start | bytes 1622024 | tf_op jit(solution)/shard_map/ppermute | solution.py:51
  9.2 9.0 %collective-permute-done.refs_1_.first = f32[33,32,128]{2,1,0:T(8,128)S(1)} collective-permute-done((f32[33,32,128]{2,1,0:T(8,128)S(1)}, f32[33,32,128]{2,1,0:T(8,128)S(1)}, u32[]{:S(2)}, u32[]{:S(2)}) %collective-permute-start) | collective-permute-done | bytes 540704 | tf_op jit(solution)/shard_map/ppermute | solution.py:51
  18.2 4.0 %collective-permute-start.3 = (f32[33,32,128]{2,1,0:T(8,128)S(1)}, f32[33,32,128]{2,1,0:T(8,128)S(1)}, u32[]{:S(2)}, u32[]{:S(2)}) collective-permute-start(f32[33,32,128]{2,1,0:T(8,128)S(1)} %collective-permute-done.refs_1_.first), channel_id=1, source_target_pairs={{0,4},{4,8},{8,12},{6,2},{10,6},{14,10},{1,5},{5,9},{9,13},{7,3},{... | collective-permute-start | bytes 1622024 | tf_op jit(solution)/shard_map/ppermute | solution.py:456
  22.2 6.7 %collective-permute-done.1.refs_2_.second = f32[33,32,128]{2,1,0:T(8,128)S(1)} collective-permute-done((f32[33,32,128]{2,1,0:T(8,128)S(1)}, f32[33,32,128]{2,1,0:T(8,128)S(1)}, u32[]{:S(2)}, u32[]{:S(2)}) %collective-permute-start.1) | collective-permute-done | bytes 540704 | tf_op jit(solution)/shard_map/ppermute | solution.py:51
  29.1 1.3 collective-permute-start.12
  30.4 1.5 %collective-permute-done.2.refs_3_ = f32[65,32,128]{2,1,0:T(8,128)S(1)} collective-permute-done((f32[65,32,128]{2,1,0:T(8,128)S(1)}, f32[65,32,128]{2,1,0:T(8,128)S(1)}, u32[]{:S(2)}, u32[]{:S(2)}) %collective-permute-start.2) | collective-permute-done | bytes 1064992 | tf_op jit(solution)/shard_map/ppermute | solution.py:456
  32.2 4.2 %collective-permute-start.10 = (f32[33,32,128]{2,1,0:T(8,128)S(1)}, f32[33,32,128]{2,1,0:T(8,128)S(1)}, u32[]{:S(2)}, u32[]{:S(2)}) collective-permute-start(f32[33,32,128]{2,1,0:T(8,128)S(1)} %get-tuple-element.29), channel_id=1, source_target_pairs={{0,4},{4,8},{8,12},{6,2},{10,6},{14,10},{1,5},{5,9},{9,13},{7,3},{... | collective-permute-start | bytes 1622024 | tf_op jit(solution)/shard_map/ppermute | solution.py:456
  36.4 3.5 %collective-permute-start.9 = (f32[33,32,128]{2,1,0:T(8,128)S(1)}, f32[33,32,128]{2,1,0:T(8,128)S(1)}, u32[]{:S(2)}, u32[]{:S(2)}) collective-permute-start(f32[33,32,128]{2,1,0:T(8,128)S(1)} %collective-permute-done.1.refs_2_.second), channel_id=1, source_target_pairs={{0,4},{4,8},{8,12},{6,2},{10,6},{14,10},{1,5},{5,9},{9,13},{7,3},{... | collective-permute-start | bytes 1622024 | tf_op jit(solution)/shard_map/ppermute | solution.py:456
  40.6 8.4 %collective-permute-done.10.refs_2_.far_early = f32[33,32,128]{2,1,0:T(8,128)S(1)} collective-permute-done((f32[33,32,128]{2,1,0:T(8,128)S(1)}, f32[33,32,128]{2,1,0:T(8,128)S(1)}, u32[]{:S(2)}, u32[]{:S(2)}) %collective-permute-start.10) | collective-permute-done | bytes 540704 | tf_op jit(solution)/shard_map/ppermute | solution.py:456
  49.0 11.1 %collective-permute-done.9.refs_0_.near_late = f32[33,32,128]{2,1,0:T(8,128)S(1)} collective-permute-done((f32[33,32,128]{2,1,0:T(8,128)S(1)}, f32[33,32,128]{2,1,0:T(8,128)S(1)}, u32[]{:S(2)}, u32[]{:S(2)}) %collective-permute-start.9) | collective-permute-done | bytes 540704 | tf_op jit(solution)/shard_map/ppermute | solution.py:456
  60.3 3.1 %shard_map.30 = (f32[21,40,2176]{2,1,0:T(8,128)S(1)}, f32[21,40,2176]{2,1,0:T(8,128)S(1)}, f32[2,16,128]{2,1,0:T(8,128)S(1)}) custom-call(f32[65,32,128]{2,1,0:T(8,128)S(1)} %get-tuple-element.25.refs_0_, f32[33,32,128]{2,1,0:T(8,128)S(1)} %collective-permute-done.refs_1_.first, f32[33,32,128]{2,1,0:T(8,128)S(1)} %collective-permute-done.1.refs_2_.second, ...), custom_call_target="tpu_custom_call" | custom-call | tf_op jit(solution)/shard_map/pallas_call | solution.py:483
  64.9 8.7 %collective-permute-start.6 = (f32[2,16,128]{2,1,0:T(8,128)S(1)}, f32[2,16,128]{2,1,0:T(8,128)S(1)}, u32[]{:S(2)}, u32[]{:S(2)}) collective-permute-start(f32[2,16,128]{2,1,0:T(8,128)S(1)} %add.24), channel_id=1, source_target_pairs={{0,2},{2,0},{4,6},{6,4},{8,10},{10,8},{12,14},{14,12},{1,3},{3,1},... | collective-permute-start | bytes 49160 | tf_op jit(solution)/shard_map/ppermute | solution.py:65
  73.5 1.7 %collective-permute-done.6 = f32[2,16,128]{2,1,0:T(8,128)S(1)} collective-permute-done((f32[2,16,128]{2,1,0:T(8,128)S(1)}, f32[2,16,128]{2,1,0:T(8,128)S(1)}, u32[]{:S(2)}, u32[]{:S(2)}) %collective-permute-start.6) | collective-permute-done | bytes 16416 | tf_op jit(solution)/shard_map/ppermute | solution.py:65
  75.3 3.4 %collective-permute-start.7 = (f32[2,8,128]{2,1,0:T(8,128)S(1)}, f32[2,8,128]{2,1,0:T(8,128)S(1)}, u32[]{:S(2)}, u32[]{:S(2)}) collective-permute-start(f32[2,8,128]{2,1,0:T(8,128)S(1)} %slice.12), channel_id=1, source_target_pairs={{0,4},{2,6},{4,8},{6,10},{8,12},{10,14},{1,5},{3,7},{5,9},{7,11},{... | collective-permute-start | bytes 24584 | tf_op jit(solution)/shard_map/ppermute | solution.py:489
  78.7 1.3 collective-permute-start.8
  80.1 5.0 %shard_map.33 = (f32[21,40,2176]{2,1,0:T(8,128)S(1)}, f32[21,40,2176]{2,1,0:T(8,128)S(1)}, f32[21,40,2176]{2,1,0:T(8,128)S(1)}, f32[21,40,2176]{2,1,0:T(8,128)S(1)}, f32[2,24,128]{2,1,0:T(8,128)S(1)}) custom-call(f32[21,40,2176]{2,1,0:T(8,128)S(1)} %get-tuple-element.31._, ...), custom_call_target="tpu_custom_call", output_to_operand_aliasing={{0}: (0, {}), {1}: (1, {})} | custom-call | tf_op jit(solution)/shard_map/pallas_call | solution.py:491
  85.3 8.7 %shard_map.34 = (f32[21,40,2176]{2,1,0:T(8,128)S(1)}, f32[21,40,2176]{2,1,0:T(8,128)S(1)}, f32[21,40,2176]{2,1,0:T(8,128)S(1)}, f32[21,40,2176]{2,1,0:T(8,128)S(1)}, f32[2,24,128]{2,1,0:T(8,128)S(1)}) custom-call(f32[2,24,128]{2,1,0:T(8,128)S(1)} %maximum_maximum_fusion.norms, ...), custom_call_target="tpu_custom_call", output_to_operand_aliasing={{0}: (6, {}), {1}: (7, {}), {2}: (8, {}), {3}: (9, {}), {4}... | custom-call | tf_op jit(solution)/shard_map/pallas_call | solution.py:499
  95.2 2.0 %collective-permute-start.15 = (f32[2,24,128]{2,1,0:T(8,128)S(1)}, f32[2,24,128]{2,1,0:T(8,128)S(1)}, u32[]{:S(2)}, u32[]{:S(2)}) collective-permute-start(f32[2,24,128]{2,1,0:T(8,128)S(1)} %add.26), channel_id=1, source_target_pairs={{0,2},{2,0},{4,6},{6,4},{8,10},{10,8},{12,14},{14,12},{1,3},{3,1},... | collective-permute-start | bytes 73736 | tf_op jit(solution)/shard_map/ppermute | solution.py:65
  97.3 1.8 %collective-permute-done.15 = f32[2,24,128]{2,1,0:T(8,128)S(1)} collective-permute-done((f32[2,24,128]{2,1,0:T(8,128)S(1)}, f32[2,24,128]{2,1,0:T(8,128)S(1)}, u32[]{:S(2)}, u32[]{:S(2)}) %collective-permute-start.15) | collective-permute-done | bytes 24608 | tf_op jit(solution)/shard_map/ppermute | solution.py:65
  99.1 4.1 %shard_map.35 = (f32[13,32,2048]{2,1,0:T(8,128)S(1)}, f32[8,128]{1,0:T(8,128)S(1)}, f32[21,40,2176]{2,1,0:T(8,128)S(1)}) custom-call(f32[21,40,2176]{2,1,0:T(8,128)S(1)} %get-tuple-element.38.phi, f32[21,40,2176]{2,1,0:T(8,128)S(1)} %get-tuple-element.40._, f32[2,24,128]{2,1,0:T(8,128)S(1)} %add.27.norms), custom_call_target="tpu_custom_call", output_to_operand_aliasing={{2}: (1, {})} | custom-call | tf_op jit(solution)/shard_map/pallas_call | solution.py:507
  104.3 2.0 %collective-permute-start.17 = (f32[8,128]{1,0:T(8,128)S(1)}, f32[8,128]{1,0:T(8,128)S(1)}, u32[]{:S(2)}, u32[]{:S(2)}) collective-permute-start(f32[8,128]{1,0:T(8,128)S(1)} %add.28), channel_id=1, source_target_pairs={{0,2},{2,0},{4,6},{6,4},{8,10},{10,8},{12,14},{14,12},{1,3},{3,1},... | collective-permute-start | bytes 12296 | tf_op jit(solution)/shard_map/ppermute | solution.py:65
  106.4 1.6 %collective-permute-done.17 = f32[8,128]{1,0:T(8,128)S(1)} collective-permute-done((f32[8,128]{1,0:T(8,128)S(1)}, f32[8,128]{1,0:T(8,128)S(1)}, u32[]{:S(2)}, u32[]{:S(2)}) %collective-permute-start.17) | collective-permute-done | bytes 4128 | tf_op jit(solution)/shard_map/ppermute | solution.py:65
  107.9 2.6 %collective-permute-start.18 = (f32[8,128]{1,0:T(8,128)S(1)}, f32[8,128]{1,0:T(8,128)S(1)}, u32[]{:S(2)}, u32[]{:S(2)}) collective-permute-start(f32[8,128]{1,0:T(8,128)S(1)} %add.29), channel_id=1, source_target_pairs={{0,4},{2,6},{4,0},{6,2},{8,12},{10,14},{12,8},{14,10},{1,5},{3,7},... | collective-permute-start | bytes 12296 | tf_op jit(solution)/shard_map/ppermute | solution.py:65
  110.6 1.6 %collective-permute-done.18 = f32[8,128]{1,0:T(8,128)S(1)} collective-permute-done((f32[8,128]{1,0:T(8,128)S(1)}, f32[8,128]{1,0:T(8,128)S(1)}, u32[]{:S(2)}, u32[]{:S(2)}) %collective-permute-start.18) | collective-permute-done | bytes 4128 | tf_op jit(solution)/shard_map/ppermute | solution.py:65
  112.2 3.0 %collective-permute-start.19 = (f32[8,128]{1,0:T(8,128)S(1)}, f32[8,128]{1,0:T(8,128)S(1)}, u32[]{:S(2)}, u32[]{:S(2)}) collective-permute-start(f32[8,128]{1,0:T(8,128)S(1)} %add.30), channel_id=1, source_target_pairs={{0,8},{2,10},{4,12},{6,14},{8,0},{10,2},{12,4},{14,6},{1,9},{3,11}... | collective-permute-start | bytes 12296 | tf_op jit(solution)/shard_map/ppermute | solution.py:65
  115.2 2.0 %collective-permute-start.20 = (s32[4]{0:T(128)S(1)}, s32[4]{0:T(128)S(1)}, u32[]{:S(2)}, u32[]{:S(2)}) collective-permute-start(s32[4]{0:T(128)S(1)} %copy-done.1), channel_id=1, source_target_pairs={{0,2},{2,0},{4,6},{6,4},{8,10},{10,8},{12,14},{14,12},{1,3},{3,1},... | collective-permute-start | bytes 56 | tf_op jit(solution)/shard_map/ppermute | solution.py:51
  117.2 1.4 shard_map.36
  119.6 2.1 %collective-permute-start.21 = (f32[4,32,2048]{2,1,0:T(8,128)S(1)}, f32[4,32,2048]{2,1,0:T(8,128)S(1)}, u32[]{:S(2)}, u32[]{:S(2)}) collective-permute-start(f32[4,32,2048]{2,1,0:T(8,128)S(1)} %shard_map.38), channel_id=1, source_target_pairs={{0,2},{2,0},{4,6},{6,4},{8,10},{10,8},{12,14},{14,12},{1,3},{3,1},... | collective-permute-start | bytes 3145736 | tf_op jit(solution)/shard_map/ppermute | solution.py:51
  121.7 1.8 %shard_map.37.whole_in = f32[4,32,4096]{2,1,0:T(8,128)} custom-call(s32[4]{0:T(128)S(1)} %copy-done.1, f32[13,32,2048]{2,1,0:T(8,128)S(1)} %get-tuple-element.43.window, f32[8,128]{1,0:T(8,128)S(1)} %add.31.squares), custom_call_target="tpu_custom_call" | custom-call | tf_op jit(solution)/shard_map/pallas_call | solution.py:530
  123.4 18.5 %collective-permute-done.21.other = f32[4,32,2048]{2,1,0:T(8,128)S(1)} collective-permute-done((f32[4,32,2048]{2,1,0:T(8,128)S(1)}, f32[4,32,2048]{2,1,0:T(8,128)S(1)}, u32[]{:S(2)}, u32[]{:S(2)}) %collective-permute-start.21) | collective-permute-done | bytes 1048608 | tf_op jit(solution)/shard_map/ppermute | solution.py:51
  (41 shorter events, 8.9 us)
Async XLA Ops:
  0.0 1.6 %copy-start = (f32[4,32,4096]{2,1,0:T(8,128)S(1)}, f32[4,32,4096]{2,1,0:T(8,128)}, u32[]{:S(2)}) copy-start(f32[4,32,4096]{2,1,0:T(8,128)} %x_ref.1) | copy-start | bytes 6291460
  2.0 16.2 %collective-permute-start = (f32[33,32,128]{2,1,0:T(8,128)S(1)}, f32[33,32,128]{2,1,0:T(8,128)S(1)}, u32[]{:S(2)}, u32[]{:S(2)}) collective-permute-start(f32[33,32,128]{2,1,0:T(8,128)S(1)} %get-tuple-element.26), channel_id=1, source_target_pairs={{0,2},{2,0},{4,6},{6,4},{8,10},{10,8},{12,14},{14,12},{1,3},{3,1},... | collective-permute-start | bytes 1622024 | tf_op jit(solution)/shard_map/ppermute | solution.py:51
  5.1 26.9 %collective-permute-start.2 = (f32[65,32,128]{2,1,0:T(8,128)S(1)}, f32[65,32,128]{2,1,0:T(8,128)S(1)}, u32[]{:S(2)}, u32[]{:S(2)}) collective-permute-start(f32[65,32,128]{2,1,0:T(8,128)S(1)} %get-tuple-element.25.refs_0_), channel_id=1, source_target_pairs={{2,6},{6,10},{10,14},{4,0},{8,4},{12,8},{3,7},{7,11},{11,15},{5,1}... | collective-permute-start | bytes 3194888 | tf_op jit(solution)/shard_map/ppermute | solution.py:456
  6.3 22.6 %collective-permute-start.1 = (f32[33,32,128]{2,1,0:T(8,128)S(1)}, f32[33,32,128]{2,1,0:T(8,128)S(1)}, u32[]{:S(2)}, u32[]{:S(2)}) collective-permute-start(f32[33,32,128]{2,1,0:T(8,128)S(1)} %get-tuple-element.27), channel_id=1, source_target_pairs={{0,2},{2,0},{4,6},{6,4},{8,10},{10,8},{12,14},{14,12},{1,3},{3,1},... | collective-permute-start | bytes 1622024 | tf_op jit(solution)/shard_map/ppermute | solution.py:51
  18.2 13.7 %collective-permute-start.3 = (f32[33,32,128]{2,1,0:T(8,128)S(1)}, f32[33,32,128]{2,1,0:T(8,128)S(1)}, u32[]{:S(2)}, u32[]{:S(2)}) collective-permute-start(f32[33,32,128]{2,1,0:T(8,128)S(1)} %collective-permute-done.refs_1_.first), channel_id=1, source_target_pairs={{0,4},{4,8},{8,12},{6,2},{10,6},{14,10},{1,5},{5,9},{9,13},{7,3},{... | collective-permute-start | bytes 1622024 | tf_op jit(solution)/shard_map/ppermute | solution.py:456
  29.1 31.0 %collective-permute-start.12 = (f32[49,32,128]{2,1,0:T(8,128)S(1)}, f32[49,32,128]{2,1,0:T(8,128)S(1)}, u32[]{:S(2)}, u32[]{:S(2)}) collective-permute-start(f32[49,32,128]{2,1,0:T(8,128)S(1)} %shard_map.31), channel_id=1, source_target_pairs={{2,6},{6,10},{10,14},{4,0},{8,4},{12,8},{3,7},{7,11},{11,15},{5,1}... | collective-permute-start | bytes 2408456 | tf_op jit(solution)/shard_map/ppermute | solution.py:456
  32.1 28.2 %collective-permute-start.4 = (f32[14,8,2176]{2,1,0:T(8,128)S(1)}, f32[14,8,2176]{2,1,0:T(8,128)S(1)}, u32[]{:S(2)}, u32[]{:S(2)}) collective-permute-start(f32[14,8,2176]{2,1,0:T(8,128)S(1)} %shard_map.29), channel_id=1, source_target_pairs={{0,1},{1,0},{2,3},{3,2},{4,5},{5,4},{6,7},{7,6},{8,9},{9,8},{10,11... | collective-permute-start | bytes 2924552 | tf_op jit(solution)/shard_map/ppermute | solution.py:113
  32.2 16.8 %collective-permute-start.10 = (f32[33,32,128]{2,1,0:T(8,128)S(1)}, f32[33,32,128]{2,1,0:T(8,128)S(1)}, u32[]{:S(2)}, u32[]{:S(2)}) collective-permute-start(f32[33,32,128]{2,1,0:T(8,128)S(1)} %get-tuple-element.29), channel_id=1, source_target_pairs={{0,4},{4,8},{8,12},{6,2},{10,6},{14,10},{1,5},{5,9},{9,13},{7,3},{... | collective-permute-start | bytes 1622024 | tf_op jit(solution)/shard_map/ppermute | solution.py:456
  36.4 23.7 %collective-permute-start.9 = (f32[33,32,128]{2,1,0:T(8,128)S(1)}, f32[33,32,128]{2,1,0:T(8,128)S(1)}, u32[]{:S(2)}, u32[]{:S(2)}) collective-permute-start(f32[33,32,128]{2,1,0:T(8,128)S(1)} %collective-permute-done.1.refs_2_.second), channel_id=1, source_target_pairs={{0,4},{4,8},{8,12},{6,2},{10,6},{14,10},{1,5},{5,9},{9,13},{7,3},{... | collective-permute-start | bytes 1622024 | tf_op jit(solution)/shard_map/ppermute | solution.py:456
  39.9 0.7 collective-permute-start.11
  60.2 25.0 %collective-permute-start.13 = (f32[8,8,2176]{2,1,0:T(8,128)S(1)}, f32[8,8,2176]{2,1,0:T(8,128)S(1)}, u32[]{:S(2)}, u32[]{:S(2)}) collective-permute-start(f32[8,8,2176]{2,1,0:T(8,128)S(1)} %shard_map.32), channel_id=1, source_target_pairs={{0,1},{1,0},{2,3},{3,2},{4,5},{5,4},{6,7},{7,6},{8,9},{9,8},{10,11... | collective-permute-start | bytes 1671176 | tf_op jit(solution)/shard_map/ppermute | solution.py:113
  63.5 1.4 collective-permute-start.5
  64.9 10.4 %collective-permute-start.6 = (f32[2,16,128]{2,1,0:T(8,128)S(1)}, f32[2,16,128]{2,1,0:T(8,128)S(1)}, u32[]{:S(2)}, u32[]{:S(2)}) collective-permute-start(f32[2,16,128]{2,1,0:T(8,128)S(1)} %add.24), channel_id=1, source_target_pairs={{0,2},{2,0},{4,6},{6,4},{8,10},{10,8},{12,14},{14,12},{1,3},{3,1},... | collective-permute-start | bytes 49160 | tf_op jit(solution)/shard_map/ppermute | solution.py:65
  75.3 9.9 %collective-permute-start.7 = (f32[2,8,128]{2,1,0:T(8,128)S(1)}, f32[2,8,128]{2,1,0:T(8,128)S(1)}, u32[]{:S(2)}, u32[]{:S(2)}) collective-permute-start(f32[2,8,128]{2,1,0:T(8,128)S(1)} %slice.12), channel_id=1, source_target_pairs={{0,4},{2,6},{4,8},{6,10},{8,12},{10,14},{1,5},{3,7},{5,9},{7,11},{... | collective-permute-start | bytes 24584 | tf_op jit(solution)/shard_map/ppermute | solution.py:489
  78.7 6.5 %collective-permute-start.8 = (f32[2,8,128]{2,1,0:T(8,128)S(1)}, f32[2,8,128]{2,1,0:T(8,128)S(1)}, u32[]{:S(2)}, u32[]{:S(2)}) collective-permute-start(f32[2,8,128]{2,1,0:T(8,128)S(1)} %slice.12), channel_id=1, source_target_pairs={{4,0},{6,2},{8,4},{10,6},{12,8},{14,10},{5,1},{7,3},{9,5},{11,7},{... | collective-permute-start | bytes 24584 | tf_op jit(solution)/shard_map/ppermute | solution.py:490
  94.0 1.3 collective-permute-start.14
  95.2 3.8 %collective-permute-start.15 = (f32[2,24,128]{2,1,0:T(8,128)S(1)}, f32[2,24,128]{2,1,0:T(8,128)S(1)}, u32[]{:S(2)}, u32[]{:S(2)}) collective-permute-start(f32[2,24,128]{2,1,0:T(8,128)S(1)} %add.26), channel_id=1, source_target_pairs={{0,2},{2,0},{4,6},{6,4},{8,10},{10,8},{12,14},{14,12},{1,3},{3,1},... | collective-permute-start | bytes 73736 | tf_op jit(solution)/shard_map/ppermute | solution.py:65
  99.1 16.2 %copy-start.1 = (s32[4]{0:T(128)S(1)}, s32[4]{0:T(128)}, u32[]{:S(2)}) copy-start(s32[4]{0:T(128)} %bracket.1) | copy-start | bytes 52
  103.2 1.2 collective-permute-start.16
  104.3 3.6 %collective-permute-start.17 = (f32[8,128]{1,0:T(8,128)S(1)}, f32[8,128]{1,0:T(8,128)S(1)}, u32[]{:S(2)}, u32[]{:S(2)}) collective-permute-start(f32[8,128]{1,0:T(8,128)S(1)} %add.28), channel_id=1, source_target_pairs={{0,2},{2,0},{4,6},{6,4},{8,10},{10,8},{12,14},{14,12},{1,3},{3,1},... | collective-permute-start | bytes 12296 | tf_op jit(solution)/shard_map/ppermute | solution.py:65
  107.9 4.2 %collective-permute-start.18 = (f32[8,128]{1,0:T(8,128)S(1)}, f32[8,128]{1,0:T(8,128)S(1)}, u32[]{:S(2)}, u32[]{:S(2)}) collective-permute-start(f32[8,128]{1,0:T(8,128)S(1)} %add.29), channel_id=1, source_target_pairs={{0,4},{2,6},{4,0},{6,2},{8,12},{10,14},{12,8},{14,10},{1,5},{3,7},... | collective-permute-start | bytes 12296 | tf_op jit(solution)/shard_map/ppermute | solution.py:65
  112.2 6.4 %collective-permute-start.19 = (f32[8,128]{1,0:T(8,128)S(1)}, f32[8,128]{1,0:T(8,128)S(1)}, u32[]{:S(2)}, u32[]{:S(2)}) collective-permute-start(f32[8,128]{1,0:T(8,128)S(1)} %add.30), channel_id=1, source_target_pairs={{0,8},{2,10},{4,12},{6,14},{8,0},{10,2},{12,4},{14,6},{1,9},{3,11}... | collective-permute-start | bytes 12296 | tf_op jit(solution)/shard_map/ppermute | solution.py:65
  115.2 3.6 %collective-permute-start.20 = (s32[4]{0:T(128)S(1)}, s32[4]{0:T(128)S(1)}, u32[]{:S(2)}, u32[]{:S(2)}) collective-permute-start(s32[4]{0:T(128)S(1)} %copy-done.1), channel_id=1, source_target_pairs={{0,2},{2,0},{4,6},{6,4},{8,10},{10,8},{12,14},{14,12},{1,3},{3,1},... | collective-permute-start | bytes 56 | tf_op jit(solution)/shard_map/ppermute | solution.py:51
  119.6 22.3 %collective-permute-start.21 = (f32[4,32,2048]{2,1,0:T(8,128)S(1)}, f32[4,32,2048]{2,1,0:T(8,128)S(1)}, u32[]{:S(2)}, u32[]{:S(2)}) collective-permute-start(f32[4,32,2048]{2,1,0:T(8,128)S(1)} %shard_map.38), channel_id=1, source_target_pairs={{0,2},{2,0},{4,6},{6,4},{8,10},{10,8},{12,14},{14,12},{1,3},{3,1},... | collective-permute-start | bytes 3145736 | tf_op jit(solution)/shard_map/ppermute | solution.py:51

commit v9 on v8

--- a/solution.py
+++ b/solution.py
@@ -116,7 +116,7 @@
     return jnp.concatenate([after, before], axis=1)
 
 
-def pack_kernel(x_ref, keep_ref, send_first, send_second, shared_ref, extra_ref):
+def pack_kernel(x_ref, *refs, sent):
     _, lo = pair_position()
     local, rows, columns = x_ref.shape
     half = columns // PAIR
@@ -137,11 +137,12 @@
             )
         ref[len(chosen) * tiles] = pack_edges(edges)
 
-    fill(send_first, 1 - lo, range(CHUNKS[1]))
-    fill(send_second, 1 - lo, range(CHUNKS[1], local))
-    fill(keep_ref, lo, range(local))
-    fill(shared_ref, lo, range(local - SHARED, local))
-    fill(extra_ref, lo, range(local - FAR, local - SHARED))
+    if sent:
+        chosen = (range(CHUNKS[1]), range(CHUNKS[1], local))
+    else:
+        chosen = (range(local), range(local - SHARED, local), range(local - FAR, local - SHARED))
+    for ref, images in zip(refs, chosen):
+        fill(ref, 1 - lo if sent else lo, images)
 
 
 def far_kernel(first, second, out):
@@ -460,10 +461,12 @@
     tiles = half // LANES
     message = lambda n: shape((n * tiles + 1, rows, LANES))
     first_chunk = CHUNKS[1]
-    keep, send_first, send_second, shared, extra = call(
-        pack_kernel,
-        (message(local), message(first_chunk), message(local - first_chunk), message(SHARED), message(FAR - SHARED)),
-        operands=1,
+    send_first, send_second = call(
+        functools.partial(pack_kernel, sent=True), (message(first_chunk), message(local - first_chunk)), operands=1
+    )(path)
+    keep, shared, extra = call(
+        functools.partial(pack_kernel, sent=False),
+        (message(local), message(SHARED), message(FAR - SHARED)), operands=1,
     )(path)
     recv = [swap_pairs(send_first), swap_pairs(send_second)]
     other_bracket = swap_pairs(bracket)

time: 143 us -> 143 us (level)
  no operation moved by 1% of the time
where the time goes in v9:
time: 143 us
  waiting for transfers between devices  65.3 us (46%)
  starting transfers between devices  48.5 us (34%)
  Pallas kernels  26.9 us (19%)
  local copies, waits for them, and re-layouts  1.68 us (1%)
    ppermute x4, waiting for transfers between devices, swap_pairs(): return lax.ppermute(value, 'img', [(i, i ^ 1) for i in range(count)])  34 us
    ppermute x6, waiting for transfers between devices, per_device(): lax.ppermute(value, 'img', [p for p in ahead if p[0] % PAIR in up] + [p f...  21.3 us
    ppermute x5, starting transfers between devices, small_sum(): other = lax.ppermute(value, 'img', [(i, i ^ step) for i in range(count)])  18.4 us
    ppermute x6, starting transfers between devices, per_device(): lax.ppermute(value, 'img', [p for p in ahead if p[0] % PAIR in up] + [p f...  14.7 us
    ppermute x4, starting transfers between devices, swap_pairs(): return lax.ppermute(value, 'img', [(i, i ^ 1) for i in range(count)])  9.99 us
    pallas_call x1, Pallas kernels, per_device(): call(functools.partial(middle_outer_kernel, count=count, local=local), (h...  8.69 us
    ppermute x5, waiting for transfers between devices, small_sum(): other = lax.ppermute(value, 'img', [(i, i ^ step) for i in range(count)])  6.7 us
    pallas_call x1, Pallas kernels, per_device(): call(functools.partial(middle_inner_kernel, count=count, local=local, row...  5.05 us
  transfers between devices with their start and end apart: 22, of which 14 were waited for; matrix products, arithmetic and copies ran while one was open for 0% of the time, Pallas kernels for 8%

profile of v9, /device:TPU:0, one launch (start us, length us, event | category | flops | bytes accessed | tf_op | source)
XLA Modules:
  0.0 142.7 jit_solution(11208527269725179919)
XLA Ops:
  0.0 1.6 %copy-done = f32[4,32,4096]{2,1,0:T(8,128)S(1)} copy-done((f32[4,32,4096]{2,1,0:T(8,128)S(1)}, f32[4,32,4096]{2,1,0:T(8,128)}, u32[]{:S(2)}) %copy-start) | copy-done | bytes 2097176
  1.8 3.1 %collective-permute-start = (f32[33,32,128]{2,1,0:T(8,128)S(1)}, f32[33,32,128]{2,1,0:T(8,128)S(1)}, u32[]{:S(2)}, u32[]{:S(2)}) collective-permute-start(f32[33,32,128]{2,1,0:T(8,128)S(1)} %get-tuple-element.26), channel_id=1, source_target_pairs={{0,2},{2,0},{4,6},{6,4},{8,10},{10,8},{12,14},{14,12},{1,3},{3,1},... | collective-permute-start | bytes 1622024 | tf_op jit(solution)/shard_map/ppermute | solution.py:51
  5.2 1.3 collective-permute-start.2
  6.5 2.8 %collective-permute-start.1 = (f32[33,32,128]{2,1,0:T(8,128)S(1)}, f32[33,32,128]{2,1,0:T(8,128)S(1)}, u32[]{:S(2)}, u32[]{:S(2)}) collective-permute-start(f32[33,32,128]{2,1,0:T(8,128)S(1)} %get-tuple-element.27), channel_id=1, source_target_pairs={{0,2},{2,0},{4,6},{6,4},{8,10},{10,8},{12,14},{14,12},{1,3},{3,1},... | collective-permute-start | bytes 1622024 | tf_op jit(solution)/shard_map/ppermute | solution.py:51
  9.3 8.7 %collective-permute-done.refs_1_.first = f32[33,32,128]{2,1,0:T(8,128)S(1)} collective-permute-done((f32[33,32,128]{2,1,0:T(8,128)S(1)}, f32[33,32,128]{2,1,0:T(8,128)S(1)}, u32[]{:S(2)}, u32[]{:S(2)}) %collective-permute-start) | collective-permute-done | bytes 540704 | tf_op jit(solution)/shard_map/ppermute | solution.py:51
  18.0 4.0 %collective-permute-start.3 = (f32[33,32,128]{2,1,0:T(8,128)S(1)}, f32[33,32,128]{2,1,0:T(8,128)S(1)}, u32[]{:S(2)}, u32[]{:S(2)}) collective-permute-start(f32[33,32,128]{2,1,0:T(8,128)S(1)} %collective-permute-done.refs_1_.first), channel_id=1, source_target_pairs={{0,4},{4,8},{8,12},{6,2},{10,6},{14,10},{1,5},{5,9},{9,13},{7,3},{... | collective-permute-start | bytes 1622024 | tf_op jit(solution)/shard_map/ppermute | solution.py:457
  22.0 6.7 %collective-permute-done.1.refs_2_.second = f32[33,32,128]{2,1,0:T(8,128)S(1)} collective-permute-done((f32[33,32,128]{2,1,0:T(8,128)S(1)}, f32[33,32,128]{2,1,0:T(8,128)S(1)}, u32[]{:S(2)}, u32[]{:S(2)}) %collective-permute-start.1) | collective-permute-done | bytes 540704 | tf_op jit(solution)/shard_map/ppermute | solution.py:51
  30.2 1.8 %collective-permute-done.2.refs_3_ = f32[65,32,128]{2,1,0:T(8,128)S(1)} collective-permute-done((f32[65,32,128]{2,1,0:T(8,128)S(1)}, f32[65,32,128]{2,1,0:T(8,128)S(1)}, u32[]{:S(2)}, u32[]{:S(2)}) %collective-permute-start.2) | collective-permute-done | bytes 1064992 | tf_op jit(solution)/shard_map/ppermute | solution.py:457
  32.3 3.9 %collective-permute-start.10 = (f32[33,32,128]{2,1,0:T(8,128)S(1)}, f32[33,32,128]{2,1,0:T(8,128)S(1)}, u32[]{:S(2)}, u32[]{:S(2)}) collective-permute-start(f32[33,32,128]{2,1,0:T(8,128)S(1)} %get-tuple-element.29), channel_id=1, source_target_pairs={{0,4},{4,8},{8,12},{6,2},{10,6},{14,10},{1,5},{5,9},{9,13},{7,3},{... | collective-permute-start | bytes 1622024 | tf_op jit(solution)/shard_map/ppermute | solution.py:457
  36.2 3.5 %collective-permute-start.9 = (f32[33,32,128]{2,1,0:T(8,128)S(1)}, f32[33,32,128]{2,1,0:T(8,128)S(1)}, u32[]{:S(2)}, u32[]{:S(2)}) collective-permute-start(f32[33,32,128]{2,1,0:T(8,128)S(1)} %collective-permute-done.1.refs_2_.second), channel_id=1, source_target_pairs={{0,4},{4,8},{8,12},{6,2},{10,6},{14,10},{1,5},{5,9},{9,13},{7,3},{... | collective-permute-start | bytes 1622024 | tf_op jit(solution)/shard_map/ppermute | solution.py:457
  40.4 8.4 %collective-permute-done.10.refs_2_.far_early = f32[33,32,128]{2,1,0:T(8,128)S(1)} collective-permute-done((f32[33,32,128]{2,1,0:T(8,128)S(1)}, f32[33,32,128]{2,1,0:T(8,128)S(1)}, u32[]{:S(2)}, u32[]{:S(2)}) %collective-permute-start.10) | collective-permute-done | bytes 540704 | tf_op jit(solution)/shard_map/ppermute | solution.py:457
  48.8 11.1 %collective-permute-done.9.refs_0_.near_late = f32[33,32,128]{2,1,0:T(8,128)S(1)} collective-permute-done((f32[33,32,128]{2,1,0:T(8,128)S(1)}, f32[33,32,128]{2,1,0:T(8,128)S(1)}, u32[]{:S(2)}, u32[]{:S(2)}) %collective-permute-start.9) | collective-permute-done | bytes 540704 | tf_op jit(solution)/shard_map/ppermute | solution.py:457
  60.1 3.1 %shard_map.31 = (f32[21,40,2176]{2,1,0:T(8,128)S(1)}, f32[21,40,2176]{2,1,0:T(8,128)S(1)}, f32[2,16,128]{2,1,0:T(8,128)S(1)}) custom-call(f32[65,32,128]{2,1,0:T(8,128)S(1)} %get-tuple-element.25.refs_0_, f32[33,32,128]{2,1,0:T(8,128)S(1)} %collective-permute-done.refs_1_.first, f32[33,32,128]{2,1,0:T(8,128)S(1)} %collective-permute-done.1.refs_2_.second, ...), custom_call_target="tpu_custom_call" | custom-call | tf_op jit(solution)/shard_map/pallas_call | solution.py:486
  64.7 8.7 %collective-permute-start.6 = (f32[2,16,128]{2,1,0:T(8,128)S(1)}, f32[2,16,128]{2,1,0:T(8,128)S(1)}, u32[]{:S(2)}, u32[]{:S(2)}) collective-permute-start(f32[2,16,128]{2,1,0:T(8,128)S(1)} %add.24), channel_id=1, source_target_pairs={{0,2},{2,0},{4,6},{6,4},{8,10},{10,8},{12,14},{14,12},{1,3},{3,1},... | collective-permute-start | bytes 49160 | tf_op jit(solution)/shard_map/ppermute | solution.py:65
  73.4 1.7 %collective-permute-done.6 = f32[2,16,128]{2,1,0:T(8,128)S(1)} collective-permute-done((f32[2,16,128]{2,1,0:T(8,128)S(1)}, f32[2,16,128]{2,1,0:T(8,128)S(1)}, u32[]{:S(2)}, u32[]{:S(2)}) %collective-permute-start.6) | collective-permute-done | bytes 16416 | tf_op jit(solution)/shard_map/ppermute | solution.py:65
  75.1 3.4 %collective-permute-start.7 = (f32[2,8,128]{2,1,0:T(8,128)S(1)}, f32[2,8,128]{2,1,0:T(8,128)S(1)}, u32[]{:S(2)}, u32[]{:S(2)}) collective-permute-start(f32[2,8,128]{2,1,0:T(8,128)S(1)} %slice.12), channel_id=1, source_target_pairs={{0,4},{2,6},{4,8},{6,10},{8,12},{10,14},{1,5},{3,7},{5,9},{7,11},{... | collective-permute-start | bytes 24584 | tf_op jit(solution)/shard_map/ppermute | solution.py:492
  78.5 1.3 collective-permute-start.8
  79.9 5.0 %shard_map.34 = (f32[21,40,2176]{2,1,0:T(8,128)S(1)}, f32[21,40,2176]{2,1,0:T(8,128)S(1)}, f32[21,40,2176]{2,1,0:T(8,128)S(1)}, f32[21,40,2176]{2,1,0:T(8,128)S(1)}, f32[2,24,128]{2,1,0:T(8,128)S(1)}) custom-call(f32[21,40,2176]{2,1,0:T(8,128)S(1)} %get-tuple-element.31._, ...), custom_call_target="tpu_custom_call", output_to_operand_aliasing={{0}: (0, {}), {1}: (1, {})} | custom-call | tf_op jit(solution)/shard_map/pallas_call | solution.py:494
  85.1 8.7 %shard_map.35 = (f32[21,40,2176]{2,1,0:T(8,128)S(1)}, f32[21,40,2176]{2,1,0:T(8,128)S(1)}, f32[21,40,2176]{2,1,0:T(8,128)S(1)}, f32[21,40,2176]{2,1,0:T(8,128)S(1)}, f32[2,24,128]{2,1,0:T(8,128)S(1)}) custom-call(f32[2,24,128]{2,1,0:T(8,128)S(1)} %maximum_maximum_fusion.norms, ...), custom_call_target="tpu_custom_call", output_to_operand_aliasing={{0}: (6, {}), {1}: (7, {}), {2}: (8, {}), {3}: (9, {}), {4}... | custom-call | tf_op jit(solution)/shard_map/pallas_call | solution.py:502
  95.1 2.0 %collective-permute-start.15 = (f32[2,24,128]{2,1,0:T(8,128)S(1)}, f32[2,24,128]{2,1,0:T(8,128)S(1)}, u32[]{:S(2)}, u32[]{:S(2)}) collective-permute-start(f32[2,24,128]{2,1,0:T(8,128)S(1)} %add.26), channel_id=1, source_target_pairs={{0,2},{2,0},{4,6},{6,4},{8,10},{10,8},{12,14},{14,12},{1,3},{3,1},... | collective-permute-start | bytes 73736 | tf_op jit(solution)/shard_map/ppermute | solution.py:65
  97.1 1.8 %collective-permute-done.15 = f32[2,24,128]{2,1,0:T(8,128)S(1)} collective-permute-done((f32[2,24,128]{2,1,0:T(8,128)S(1)}, f32[2,24,128]{2,1,0:T(8,128)S(1)}, u32[]{:S(2)}, u32[]{:S(2)}) %collective-permute-start.15) | collective-permute-done | bytes 24608 | tf_op jit(solution)/shard_map/ppermute | solution.py:65
  98.9 4.1 %shard_map.36 = (f32[13,32,2048]{2,1,0:T(8,128)S(1)}, f32[8,128]{1,0:T(8,128)S(1)}, f32[21,40,2176]{2,1,0:T(8,128)S(1)}) custom-call(f32[21,40,2176]{2,1,0:T(8,128)S(1)} %get-tuple-element.38.phi, f32[21,40,2176]{2,1,0:T(8,128)S(1)} %get-tuple-element.40._, f32[2,24,128]{2,1,0:T(8,128)S(1)} %add.27.norms), custom_call_target="tpu_custom_call", output_to_operand_aliasing={{2}: (1, {})} | custom-call | tf_op jit(solution)/shard_map/pallas_call | solution.py:510
  104.2 2.0 %collective-permute-start.17 = (f32[8,128]{1,0:T(8,128)S(1)}, f32[8,128]{1,0:T(8,128)S(1)}, u32[]{:S(2)}, u32[]{:S(2)}) collective-permute-start(f32[8,128]{1,0:T(8,128)S(1)} %add.28), channel_id=1, source_target_pairs={{0,2},{2,0},{4,6},{6,4},{8,10},{10,8},{12,14},{14,12},{1,3},{3,1},... | collective-permute-start | bytes 12296 | tf_op jit(solution)/shard_map/ppermute | solution.py:65
  106.2 1.6 %collective-permute-done.17 = f32[8,128]{1,0:T(8,128)S(1)} collective-permute-done((f32[8,128]{1,0:T(8,128)S(1)}, f32[8,128]{1,0:T(8,128)S(1)}, u32[]{:S(2)}, u32[]{:S(2)}) %collective-permute-start.17) | collective-permute-done | bytes 4128 | tf_op jit(solution)/shard_map/ppermute | solution.py:65
  107.8 2.6 %collective-permute-start.18 = (f32[8,128]{1,0:T(8,128)S(1)}, f32[8,128]{1,0:T(8,128)S(1)}, u32[]{:S(2)}, u32[]{:S(2)}) collective-permute-start(f32[8,128]{1,0:T(8,128)S(1)} %add.29), channel_id=1, source_target_pairs={{0,4},{2,6},{4,0},{6,2},{8,12},{10,14},{12,8},{14,10},{1,5},{3,7},... | collective-permute-start | bytes 12296 | tf_op jit(solution)/shard_map/ppermute | solution.py:65
  110.4 1.6 %collective-permute-done.18 = f32[8,128]{1,0:T(8,128)S(1)} collective-permute-done((f32[8,128]{1,0:T(8,128)S(1)}, f32[8,128]{1,0:T(8,128)S(1)}, u32[]{:S(2)}, u32[]{:S(2)}) %collective-permute-start.18) | collective-permute-done | bytes 4128 | tf_op jit(solution)/shard_map/ppermute | solution.py:65
  112.0 3.0 %collective-permute-start.19 = (f32[8,128]{1,0:T(8,128)S(1)}, f32[8,128]{1,0:T(8,128)S(1)}, u32[]{:S(2)}, u32[]{:S(2)}) collective-permute-start(f32[8,128]{1,0:T(8,128)S(1)} %add.30), channel_id=1, source_target_pairs={{0,8},{2,10},{4,12},{6,14},{8,0},{10,2},{12,4},{14,6},{1,9},{3,11}... | collective-permute-start | bytes 12296 | tf_op jit(solution)/shard_map/ppermute | solution.py:65
  115.0 2.0 %collective-permute-start.20 = (s32[4]{0:T(128)S(1)}, s32[4]{0:T(128)S(1)}, u32[]{:S(2)}, u32[]{:S(2)}) collective-permute-start(s32[4]{0:T(128)S(1)} %copy-done.1), channel_id=1, source_target_pairs={{0,2},{2,0},{4,6},{6,4},{8,10},{10,8},{12,14},{14,12},{1,3},{3,1},... | collective-permute-start | bytes 56 | tf_op jit(solution)/shard_map/ppermute | solution.py:51
  117.1 1.4 shard_map.37
  119.4 2.1 %collective-permute-start.21 = (f32[4,32,2048]{2,1,0:T(8,128)S(1)}, f32[4,32,2048]{2,1,0:T(8,128)S(1)}, u32[]{:S(2)}, u32[]{:S(2)}) collective-permute-start(f32[4,32,2048]{2,1,0:T(8,128)S(1)} %shard_map.39), channel_id=1, source_target_pairs={{0,2},{2,0},{4,6},{6,4},{8,10},{10,8},{12,14},{14,12},{1,3},{3,1},... | collective-permute-start | bytes 3145736 | tf_op jit(solution)/shard_map/ppermute | solution.py:51
  121.5 1.8 %shard_map.38.whole_in = f32[4,32,4096]{2,1,0:T(8,128)} custom-call(s32[4]{0:T(128)S(1)} %copy-done.1, f32[13,32,2048]{2,1,0:T(8,128)S(1)} %get-tuple-element.43.window, f32[8,128]{1,0:T(8,128)S(1)} %add.31.squares), custom_call_target="tpu_custom_call" | custom-call | tf_op jit(solution)/shard_map/pallas_call | solution.py:533
  123.3 18.5 %collective-permute-done.21.other = f32[4,32,2048]{2,1,0:T(8,128)S(1)} collective-permute-done((f32[4,32,2048]{2,1,0:T(8,128)S(1)}, f32[4,32,2048]{2,1,0:T(8,128)S(1)}, u32[]{:S(2)}, u32[]{:S(2)}) %collective-permute-start.21) | collective-permute-done | bytes 1048608 | tf_op jit(solution)/shard_map/ppermute | solution.py:51
  (42 shorter events, 9.0 us)
Async XLA Ops:
  0.0 1.6 %copy-start = (f32[4,32,4096]{2,1,0:T(8,128)S(1)}, f32[4,32,4096]{2,1,0:T(8,128)}, u32[]{:S(2)}) copy-start(f32[4,32,4096]{2,1,0:T(8,128)} %x_ref.3) | copy-start | bytes 6291460
  1.8 16.2 %collective-permute-start = (f32[33,32,128]{2,1,0:T(8,128)S(1)}, f32[33,32,128]{2,1,0:T(8,128)S(1)}, u32[]{:S(2)}, u32[]{:S(2)}) collective-permute-start(f32[33,32,128]{2,1,0:T(8,128)S(1)} %get-tuple-element.26), channel_id=1, source_target_pairs={{0,2},{2,0},{4,6},{6,4},{8,10},{10,8},{12,14},{14,12},{1,3},{3,1},... | collective-permute-start | bytes 1622024 | tf_op jit(solution)/shard_map/ppermute | solution.py:51
  5.2 26.9 %collective-permute-start.2 = (f32[65,32,128]{2,1,0:T(8,128)S(1)}, f32[65,32,128]{2,1,0:T(8,128)S(1)}, u32[]{:S(2)}, u32[]{:S(2)}) collective-permute-start(f32[65,32,128]{2,1,0:T(8,128)S(1)} %get-tuple-element.25.refs_0_), channel_id=1, source_target_pairs={{2,6},{6,10},{10,14},{4,0},{8,4},{12,8},{3,7},{7,11},{11,15},{5,1}... | collective-permute-start | bytes 3194888 | tf_op jit(solution)/shard_map/ppermute | solution.py:457
  6.5 22.3 %collective-permute-start.1 = (f32[33,32,128]{2,1,0:T(8,128)S(1)}, f32[33,32,128]{2,1,0:T(8,128)S(1)}, u32[]{:S(2)}, u32[]{:S(2)}) collective-permute-start(f32[33,32,128]{2,1,0:T(8,128)S(1)} %get-tuple-element.27), channel_id=1, source_target_pairs={{0,2},{2,0},{4,6},{6,4},{8,10},{10,8},{12,14},{14,12},{1,3},{3,1},... | collective-permute-start | bytes 1622024 | tf_op jit(solution)/shard_map/ppermute | solution.py:51
  18.0 14.0 %collective-permute-start.3 = (f32[33,32,128]{2,1,0:T(8,128)S(1)}, f32[33,32,128]{2,1,0:T(8,128)S(1)}, u32[]{:S(2)}, u32[]{:S(2)}) collective-permute-start(f32[33,32,128]{2,1,0:T(8,128)S(1)} %collective-permute-done.refs_1_.first), channel_id=1, source_target_pairs={{0,4},{4,8},{8,12},{6,2},{10,6},{14,10},{1,5},{5,9},{9,13},{7,3},{... | collective-permute-start | bytes 1622024 | tf_op jit(solution)/shard_map/ppermute | solution.py:457
  28.9 31.0 %collective-permute-start.12 = (f32[49,32,128]{2,1,0:T(8,128)S(1)}, f32[49,32,128]{2,1,0:T(8,128)S(1)}, u32[]{:S(2)}, u32[]{:S(2)}) collective-permute-start(f32[49,32,128]{2,1,0:T(8,128)S(1)} %shard_map.32), channel_id=1, source_target_pairs={{2,6},{6,10},{10,14},{4,0},{8,4},{12,8},{3,7},{7,11},{11,15},{5,1}... | collective-permute-start | bytes 2408456 | tf_op jit(solution)/shard_map/ppermute | solution.py:457
  32.2 27.9 %collective-permute-start.4 = (f32[14,8,2176]{2,1,0:T(8,128)S(1)}, f32[14,8,2176]{2,1,0:T(8,128)S(1)}, u32[]{:S(2)}, u32[]{:S(2)}) collective-permute-start(f32[14,8,2176]{2,1,0:T(8,128)S(1)} %shard_map.30), channel_id=1, source_target_pairs={{0,1},{1,0},{2,3},{3,2},{4,5},{5,4},{6,7},{7,6},{8,9},{9,8},{10,11... | collective-permute-start | bytes 2924552 | tf_op jit(solution)/shard_map/ppermute | solution.py:113
  32.3 16.5 %collective-permute-start.10 = (f32[33,32,128]{2,1,0:T(8,128)S(1)}, f32[33,32,128]{2,1,0:T(8,128)S(1)}, u32[]{:S(2)}, u32[]{:S(2)}) collective-permute-start(f32[33,32,128]{2,1,0:T(8,128)S(1)} %get-tuple-element.29), channel_id=1, source_target_pairs={{0,4},{4,8},{8,12},{6,2},{10,6},{14,10},{1,5},{5,9},{9,13},{7,3},{... | collective-permute-start | bytes 1622024 | tf_op jit(solution)/shard_map/ppermute | solution.py:457
  36.2 23.7 %collective-permute-start.9 = (f32[33,32,128]{2,1,0:T(8,128)S(1)}, f32[33,32,128]{2,1,0:T(8,128)S(1)}, u32[]{:S(2)}, u32[]{:S(2)}) collective-permute-start(f32[33,32,128]{2,1,0:T(8,128)S(1)} %collective-permute-done.1.refs_2_.second), channel_id=1, source_target_pairs={{0,4},{4,8},{8,12},{6,2},{10,6},{14,10},{1,5},{5,9},{9,13},{7,3},{... | collective-permute-start | bytes 1622024 | tf_op jit(solution)/shard_map/ppermute | solution.py:457
  39.7 0.7 collective-permute-start.11
  60.1 25.0 %collective-permute-start.13 = (f32[8,8,2176]{2,1,0:T(8,128)S(1)}, f32[8,8,2176]{2,1,0:T(8,128)S(1)}, u32[]{:S(2)}, u32[]{:S(2)}) collective-permute-start(f32[8,8,2176]{2,1,0:T(8,128)S(1)} %shard_map.33), channel_id=1, source_target_pairs={{0,1},{1,0},{2,3},{3,2},{4,5},{5,4},{6,7},{7,6},{8,9},{9,8},{10,11... | collective-permute-start | bytes 1671176 | tf_op jit(solution)/shard_map/ppermute | solution.py:113
  63.3 1.4 collective-permute-start.5
  64.7 10.4 %collective-permute-start.6 = (f32[2,16,128]{2,1,0:T(8,128)S(1)}, f32[2,16,128]{2,1,0:T(8,128)S(1)}, u32[]{:S(2)}, u32[]{:S(2)}) collective-permute-start(f32[2,16,128]{2,1,0:T(8,128)S(1)} %add.24), channel_id=1, source_target_pairs={{0,2},{2,0},{4,6},{6,4},{8,10},{10,8},{12,14},{14,12},{1,3},{3,1},... | collective-permute-start | bytes 49160 | tf_op jit(solution)/shard_map/ppermute | solution.py:65
  75.1 9.9 %collective-permute-start.7 = (f32[2,8,128]{2,1,0:T(8,128)S(1)}, f32[2,8,128]{2,1,0:T(8,128)S(1)}, u32[]{:S(2)}, u32[]{:S(2)}) collective-permute-start(f32[2,8,128]{2,1,0:T(8,128)S(1)} %slice.12), channel_id=1, source_target_pairs={{0,4},{2,6},{4,8},{6,10},{8,12},{10,14},{1,5},{3,7},{5,9},{7,11},{... | collective-permute-start | bytes 24584 | tf_op jit(solution)/shard_map/ppermute | solution.py:492
  78.5 6.5 %collective-permute-start.8 = (f32[2,8,128]{2,1,0:T(8,128)S(1)}, f32[2,8,128]{2,1,0:T(8,128)S(1)}, u32[]{:S(2)}, u32[]{:S(2)}) collective-permute-start(f32[2,8,128]{2,1,0:T(8,128)S(1)} %slice.12), channel_id=1, source_target_pairs={{4,0},{6,2},{8,4},{10,6},{12,8},{14,10},{5,1},{7,3},{9,5},{11,7},{... | collective-permute-start | bytes 24584 | tf_op jit(solution)/shard_map/ppermute | solution.py:493
  93.8 1.3 collective-permute-start.14
  95.1 3.8 %collective-permute-start.15 = (f32[2,24,128]{2,1,0:T(8,128)S(1)}, f32[2,24,128]{2,1,0:T(8,128)S(1)}, u32[]{:S(2)}, u32[]{:S(2)}) collective-permute-start(f32[2,24,128]{2,1,0:T(8,128)S(1)} %add.26), channel_id=1, source_target_pairs={{0,2},{2,0},{4,6},{6,4},{8,10},{10,8},{12,14},{14,12},{1,3},{3,1},... | collective-permute-start | bytes 73736 | tf_op jit(solution)/shard_map/ppermute | solution.py:65
  98.9 16.2 %copy-start.1 = (s32[4]{0:T(128)S(1)}, s32[4]{0:T(128)}, u32[]{:S(2)}) copy-start(s32[4]{0:T(128)} %bracket.1) | copy-start | bytes 52
  103.0 1.2 collective-permute-start.16
  104.2 3.6 %collective-permute-start.17 = (f32[8,128]{1,0:T(8,128)S(1)}, f32[8,128]{1,0:T(8,128)S(1)}, u32[]{:S(2)}, u32[]{:S(2)}) collective-permute-start(f32[8,128]{1,0:T(8,128)S(1)} %add.28), channel_id=1, source_target_pairs={{0,2},{2,0},{4,6},{6,4},{8,10},{10,8},{12,14},{14,12},{1,3},{3,1},... | collective-permute-start | bytes 12296 | tf_op jit(solution)/shard_map/ppermute | solution.py:65
  107.8 4.2 %collective-permute-start.18 = (f32[8,128]{1,0:T(8,128)S(1)}, f32[8,128]{1,0:T(8,128)S(1)}, u32[]{:S(2)}, u32[]{:S(2)}) collective-permute-start(f32[8,128]{1,0:T(8,128)S(1)} %add.29), channel_id=1, source_target_pairs={{0,4},{2,6},{4,0},{6,2},{8,12},{10,14},{12,8},{14,10},{1,5},{3,7},... | collective-permute-start | bytes 12296 | tf_op jit(solution)/shard_map/ppermute | solution.py:65
  112.0 6.4 %collective-permute-start.19 = (f32[8,128]{1,0:T(8,128)S(1)}, f32[8,128]{1,0:T(8,128)S(1)}, u32[]{:S(2)}, u32[]{:S(2)}) collective-permute-start(f32[8,128]{1,0:T(8,128)S(1)} %add.30), channel_id=1, source_target_pairs={{0,8},{2,10},{4,12},{6,14},{8,0},{10,2},{12,4},{14,6},{1,9},{3,11}... | collective-permute-start | bytes 12296 | tf_op jit(solution)/shard_map/ppermute | solution.py:65
  115.0 3.6 %collective-permute-start.20 = (s32[4]{0:T(128)S(1)}, s32[4]{0:T(128)S(1)}, u32[]{:S(2)}, u32[]{:S(2)}) collective-permute-start(s32[4]{0:T(128)S(1)} %copy-done.1), channel_id=1, source_target_pairs={{0,2},{2,0},{4,6},{6,4},{8,10},{10,8},{12,14},{14,12},{1,3},{3,1},... | collective-permute-start | bytes 56 | tf_op jit(solution)/shard_map/ppermute | solution.py:51
  119.4 22.3 %collective-permute-start.21 = (f32[4,32,2048]{2,1,0:T(8,128)S(1)}, f32[4,32,2048]{2,1,0:T(8,128)S(1)}, u32[]{:S(2)}, u32[]{:S(2)}) collective-permute-start(f32[4,32,2048]{2,1,0:T(8,128)S(1)} %shard_map.39), channel_id=1, source_target_pairs={{0,2},{2,0},{4,6},{6,4},{8,10},{10,8},{12,14},{14,12},{1,3},{3,1},... | collective-permute-start | bytes 3145736 | tf_op jit(solution)/shard_map/ppermute | solution.py:51
